TPU v7x, 128 devices: a whole 4x4x4 slice. The times are simulated.
128 devices in a mesh: row: 8 (over y, x_hi), col: 16 (over z, x_lo, core).
Axes of the slice: x: 4 (x_hi: 2, x_lo: 2; x = x_hi * 2 + x_lo), y: 4, z: 4, core: 2. Of those that a mesh axis runs over, the one named last changes fastest.
Arguments:
- h_slab: bfloat16 [4096, 96000], P('row', 'col'), may hold values from -0.01953125 to 0.01953125
- vectors: bfloat16 [96000, 1024], P('col'), may hold values from -6 to 6
- left_rows: bfloat16 [4096, 1024], P('row'), may hold values from -0.09375 to 0.09375
Outputs:
- projected: float32 [1024, 1024], replicated
All inputs are finite; a program needn't handle non-finite values.
Results may differ from a plain program's by a relative error of at most 0.0003.
Values sent between devices are 32-bit elements; how exact they have to be, the bound alone decides.
No kernel may reach another device: no remote copies, remote signals or barrier semaphores. Data moves between devices by JAX's collectives and lax.ppermute only.
A program may use at most 128 MiB of HBM per device.

v0:
```python
import functools

import jax
import jax.numpy as jnp
from jax import lax
from jax.experimental import pallas as pl
from jax.experimental.pallas import tpu as pltpu
from jax.sharding import Mesh, PartitionSpec as P


AXES = ("y", "xh", "z", "xl", "core")
SIZES = (4, 2, 4, 2, 2)
PLANE = ("y", "xh", "xl")
F32 = jnp.float32
ANY = pl.BlockSpec(memory_space=pl.ANY)
HBM = pl.BlockSpec(memory_space=pltpu.HBM)
VMEM = pl.BlockSpec(memory_space=pltpu.VMEM)


def rank(y, x, z, core):
    return (((y * 2 + x // 2) * 4 + z) * 2 + x % 2) * 2 + core


def shift(value, axis, step):
    size = lax.axis_size(axis)
    return lax.ppermute(value, axis, [(i, (i + step) % size) for i in range(size)])


def ring_shift(value, step):
    pairs = []
    for y in range(4):
        for x in range(4):
            for z in range(4):
                pairs.append((rank(y, x, z, 0), rank(y, x, (z + step) % 4, 0)))
                pairs.append((rank(y, x, z, 1), rank((y + step) % 4, x, z, 1)))
    return lax.ppermute(value, AXES, pairs)


def plane_groups():
    groups = [[rank(y, x, z, 0) for y in range(4) for x in range(4)] for z in range(4)]
    return groups + [[rank(y, x, z, 1) for z in range(4) for x in range(4)] for y in range(4)]


def resident(value):
    return pltpu.with_memory_space_constraint(value, pltpu.VMEM)


def streamed(value):
    return pltpu.with_memory_space_constraint(value, pltpu.HBM)


def cuts(depth):
    return [(start, min(1536, depth - start)) for start in range(0, depth, 1536)]


def multiply(left, right):
    return lax.dot_general(left, right, (((0,), (0,)), ((), ())), preferred_element_type=F32)


def columns_of(v, ahead, rows=None):
    width = v.shape[1] // 4
    column = pl.multiple_of(lax.rem(lax.axis_index("z") + ahead, 4) * width, width)
    return v.at[:, pl.ds(column, width)] if rows is None else v.at[rows, pl.ds(column, width)]


def emit(total, keep, give):
    core = lax.axis_index("core")
    rows = total.shape[0] // 2
    keep[...] = total[pl.ds(pl.multiple_of(core * rows, rows), rows), :]
    give[...] = total[pl.ds(pl.multiple_of((1 - core) * rows, rows), rows), :]


def opening_kernel(ahead, following, h, v, keep, give, h_here, v_next, v_here, total, sem):
    copies = []
    for i, (start, size) in enumerate(cuts(h.shape[0])):
        rows = pl.ds(start, size)
        one = pltpu.make_async_copy(h.at[rows], h_here.at[rows], sem.at[2 * i])
        two = pltpu.make_async_copy(columns_of(v, ahead, rows), v_here.at[rows], sem.at[2 * i + 1])
        one.start()
        two.start()
        copies.append((start, size, one, two))
    fetch = pltpu.make_async_copy(columns_of(v, following), v_next, sem.at[2 * len(copies)])
    fetch.start()
    for start, size, one, two in copies:
        one.wait()
        two.wait()
        part = multiply(v_here[start : start + size], h_here[start : start + size])
        if start == 0:
            total[...] = part
        else:
            total[...] += part
    emit(total, keep, give)
    fetch.wait()


def middle_kernel(following, h_here, v_here, v, keep, give, v_next, total, sem):
    fetch = pltpu.make_async_copy(columns_of(v, following), v_next, sem)
    fetch.start()
    total[...] = multiply(v_here[...], h_here[...])
    emit(total, keep, give)
    fetch.wait()


def closing_kernel(h_here, v_here, keep, give, total):
    total[...] = multiply(v_here[...], h_here[...])
    emit(total, keep, give)


def kernel_call(kernel, h, v, ins, outs, scratch):
    width, rows = v.shape[1] // 4, h.shape[1]
    piece = pltpu.VMEM((width // 2, rows), F32)
    return pl.pallas_call(
        kernel,
        in_specs=ins,
        out_specs=[VMEM] * (2 + len(outs)),
        out_shape=[piece, piece, *outs],
        scratch_shapes=scratch,
        cost_estimate=pl.CostEstimate(flops=2 * h.shape[0] * width * rows, bytes_accessed=h.shape[0] * width * 2, transcendentals=0),
        compiler_params=pltpu.CompilerParams(vmem_limit_bytes=8 * 2**20),
    )


def products(h, v):
    depth, rows = h.shape
    block = pltpu.VMEM((depth, v.shape[1] // 4), v.dtype)
    slab = pltpu.VMEM((depth, rows), h.dtype)
    total = pltpu.VMEM((v.shape[1] // 4, rows), F32)
    v = streamed(v)
    sems = pltpu.SemaphoreType.DMA((2 * len(cuts(depth)) + 1,))

    def opening(ahead, following):
        kernel = functools.partial(opening_kernel, ahead, following)
        return kernel_call(kernel, h, v, [HBM, HBM], [slab, block], [block, total, sems])(streamed(h), v)

    def middle(following, h_here, v_here):
        kernel = functools.partial(middle_kernel, following)
        call = kernel_call(kernel, h, v, [VMEM, VMEM, HBM], [block], [total, pltpu.SemaphoreType.DMA])
        return call(resident(h_here), resident(v_here), v)

    def closing(h_here, v_here):
        call = kernel_call(closing_kernel, h, v, [VMEM, VMEM], [], [total])
        return call(resident(h_here), resident(v_here))

    return opening, middle, closing


def near_kernel(*refs):
    own, other, out, sem = refs[:3], refs[3:6], refs[6], refs[7]
    steps = (0, 3, 1)
    write([(ref, step, 0) for ref, step in zip(own, steps)], [(ref, step, 0) for ref, step in zip(other, steps)], out, sem)


def far_kernel(*refs):
    own, other, out, sem = refs[:2], refs[2:4], refs[5], refs[6]
    write([(own[0], 2, 0), (own[1], 2, 1)], [(other[0], 2, 0), (other[1], 2, 1)], out, sem)


def write(own, other, out, sem):
    y, z, core = lax.axis_index("y"), lax.axis_index("z"), lax.axis_index("core")

    def run(first, second):
        made = []
        for ref, step, part in first:
            rows = ref.shape[0]
            column = pl.multiple_of(lax.rem(z + step, 4) * 256, 256)
            made.append((ref, out.at[pl.ds(part * rows, rows), pl.ds(column, 128)]))
        for ref, step, part in second:
            row = pl.multiple_of(lax.rem(y + step, 4) * 256, 256)
            for k in range(ref.shape[0] // 256):
                column = (part * 2 + k) * 256 + 128
                made.append((ref.at[pl.ds(k * 256, 256)], out.at[pl.ds(row, 256), pl.ds(column, 128)]))
        made = [pltpu.make_async_copy(src, dst, sem.at[i]) for i, (src, dst) in enumerate(made)]
        for copy in made:
            copy.start()
        for copy in made:
            copy.wait()

    @pl.when(core == 0)
    def _():
        run(own, other)

    @pl.when(core == 1)
    def _():
        run(other, own)


def place_near(own, other, nvec):
    return pl.pallas_call(
        near_kernel,
        in_specs=[ANY] * 6,
        out_specs=ANY,
        out_shape=jax.ShapeDtypeStruct((nvec, nvec), F32),
        scratch_shapes=[pltpu.SemaphoreType.DMA((15,))],
        compiler_params=pltpu.CompilerParams(vmem_limit_bytes=2**20),
        name="place_near",
    )(*own, *other)


def place_far(own, other, whole):
    return pl.pallas_call(
        far_kernel,
        in_specs=[ANY] * 5,
        out_specs=ANY,
        out_shape=jax.ShapeDtypeStruct(whole.shape, F32),
        input_output_aliases={4: 0},
        scratch_shapes=[pltpu.SemaphoreType.DMA((6,))],
        compiler_params=pltpu.CompilerParams(vmem_limit_bytes=2**20),
        name="place_far",
    )(*own, *other, whole)


def body(h_slab, vectors, left_rows):
    nvec = vectors.shape[1]
    wide = nvec // 8
    half = wide // 2
    opening, middle, closing = products(h_slab.T, vectors)

    far, give, h_here, v_next = opening(2, 1)
    other_far = shift(give, "core", 1)
    up, give, v_next = middle(3, h_here, v_next)
    other_up = shift(give, "core", 1)
    far = far + other_far
    from_below = shift(far[:half], "z", 1)
    from_above = shift(far[half:], "z", -1)
    down, give, v_next = middle(0, h_here, v_next)
    other_down = shift(give, "core", 1)
    up, down = up + other_up, down + other_down
    up = jnp.concatenate([up[:half] + from_below, up[half:]])
    down = jnp.concatenate([down[:half], down[half:] + from_above])
    from_below = shift(up, "z", 1)
    from_above = shift(down, "z", -1)
    own, give = closing(h_here, v_next)
    shared = own + shift(give, "core", 1) + from_below + from_above

    local_part = lax.dot_general(
        left_rows.astype(F32),
        shared,
        (((0,), (1,)), ((), ())),
        precision=lax.Precision.HIGHEST,
        preferred_element_type=F32,
    )
    parts = local_part.reshape(16, nvec // 16, wide)
    parts = lax.all_to_all(parts, PLANE, 0, 0, tiled=True)
    summed = jnp.sum(parts, axis=0)
    copies = jnp.broadcast_to(summed, (16, *summed.shape))
    block = lax.all_to_all(
        copies, AXES, 0, 0, tiled=True, axis_index_groups=plane_groups()
    ).reshape(nvec, wide)

    half = nvec // 2
    below = ring_shift(block, 1)
    above = ring_shift(block, -1)
    other = shift(block, "core", 1)
    far_low = ring_shift(below[:half], 1)
    far_high = ring_shift(above[half:], -1)
    other_below = shift(below, "core", 1)
    other_above = shift(above, "core", 1)
    whole = place_near([block, below, above], [other, other_below, other_above], nvec)
    far = [far_low, far_high]
    return place_far(far, [shift(value, "core", 1) for value in far], whole)


def solution(mesh):
    fine = Mesh(mesh.devices.reshape(SIZES), AXES)
    row, col = ("y", "xh"), ("z", "xl", "core")
    in_specs = (P(row, col), P(col, None), P(row, None))
    return jax.shard_map(body, mesh=fine, in_specs=in_specs, out_specs=P(), check_vma=False)
```

profile of v0, /device:TPU:1, one launch (start us, length us, event | category | flops | bytes accessed | tf_op | source)
XLA Modules:
  0.0 88.7 jit_solution(4917386073849488206)
XLA Ops:
  0.0 0.0 copy-start
  0.0 4.8 %shard_map.37 = (f32[128,512]{1,0:T(8,128)S(1)}, f32[128,512]{1,0:T(8,128)S(1)}, bf16[6000,512]{1,0:T(8,128)(2,1)S(1)}, bf16[6000,256]{1,0:T(8,128)(2,1)S(1)}) custom-call(bf16[6000,512]{1,0:T(8,128)(2,1)} %bitcast.10, bf16[6000,1024]{1,0:T(8,128)(2,1)} %v.5), custom_call_target="tpu_custom_call" | custom-call | flops 1572864000 | bytes 3072000 | tf_op jit(solution)/shard_map/pallas_call | solution.py:133
  4.8 1.5 %collective-permute-start.2 = (f32[128,512]{1,0:T(8,128)S(1)}, f32[128,512]{1,0:T(8,128)S(1)}, u32[]{:S(2)}, u32[]{:S(2)}) collective-permute-start(f32[128,512]{1,0:T(8,128)S(1)} %get-tuple-element.26), channel_id=1, source_target_pairs={{0,1},{1,0},{2,3},{3,2},{4,5},{5,4},{6,7},{7,6},{8,9},{9,8},{10,11... | collective-permute-start | bytes 786440 | tf_op jit(solution)/shard_map/ppermute | solution.py:26
  6.3 3.4 %shard_map.38 = (f32[128,512]{1,0:T(8,128)S(1)}, f32[128,512]{1,0:T(8,128)S(1)}, bf16[6000,256]{1,0:T(8,128)(2,1)S(1)}) custom-call(bf16[6000,512]{1,0:T(8,128)(2,1)S(1)} %get-tuple-element.17.h_here, bf16[6000,256]{1,0:T(8,128)(2,1)S(1)} %get-tuple-element.18.v_here, bf16[6000,1024]{1,0:T(8,128)(2,1)} %v.5), custom_call_target="tpu_custom_call" | custom-call | flops 1572864000 | bytes 3072000 | tf_op jit(solution)/shard_map/pallas_call | solution.py:138
  9.7 0.1 collective-permute-start.1
  9.8 3.4 %shard_map.39 = (f32[128,512]{1,0:T(8,128)S(1)}, f32[128,512]{1,0:T(8,128)S(1)}, bf16[6000,256]{1,0:T(8,128)(2,1)S(1)}) custom-call(bf16[6000,512]{1,0:T(8,128)(2,1)S(1)} %get-tuple-element.17.h_here, bf16[6000,256]{1,0:T(8,128)(2,1)S(1)} %get-tuple-element.19.v_here, bf16[6000,1024]{1,0:T(8,128)(2,1)} %v.5), custom_call_target="tpu_custom_call" | custom-call | flops 1572864000 | bytes 3072000 | tf_op jit(solution)/shard_map/pallas_call | solution.py:138
  13.2 0.6 collective-permute-start.5
  13.8 0.0 collective-permute-done.2
  13.9 1.8 %collective-permute-start.3 = (f32[64,512]{1,0:T(8,128)S(1)}, f32[64,512]{1,0:T(8,128)S(1)}, u32[]{:S(2)}, u32[]{:S(2)}) collective-permute-start(f32[64,512]{1,0:T(8,128)S(1)} %get-tuple-element.31), channel_id=1, source_target_pairs={{0,4},{4,8},{8,12},{12,0},{1,5},{5,9},{9,13},{13,1},{2,6},{6,10},{... | collective-permute-start | bytes 393224 | tf_op jit(solution)/shard_map/ppermute | solution.py:26
  15.7 1.9 %shard_map.40 = (f32[128,512]{1,0:T(8,128)S(1)}, f32[128,512]{1,0:T(8,128)S(1)}) custom-call(bf16[6000,512]{1,0:T(8,128)(2,1)S(1)} %get-tuple-element.17.h_here, bf16[6000,256]{1,0:T(8,128)(2,1)S(1)} %get-tuple-element.20.v_here), custom_call_target="tpu_custom_call" | custom-call | flops 1572864000 | bytes 3072000 | tf_op jit(solution)/shard_map/pallas_call | solution.py:142
  17.5 0.4 collective-permute-start
  17.9 1.9 %collective-permute-start.6 = (f32[64,512]{1,0:T(8,128)S(1)}, f32[64,512]{1,0:T(8,128)S(1)}, u32[]{:S(2)}, u32[]{:S(2)}) collective-permute-start(f32[64,512]{1,0:T(8,128)S(1)} %get-tuple-element.32), channel_id=1, source_target_pairs={{0,12},{4,0},{8,4},{12,8},{1,13},{5,1},{9,5},{13,9},{2,14},{6,2},{... | collective-permute-start | bytes 393224 | tf_op jit(solution)/shard_map/ppermute | solution.py:26
  19.8 0.0 collective-permute-done.1
  19.9 0.0 collective-permute-done.5
  19.9 1.7 %collective-permute-done.3 = f32[64,512]{1,0:T(8,128)S(1)} collective-permute-done((f32[64,512]{1,0:T(8,128)S(1)}, f32[64,512]{1,0:T(8,128)S(1)}, u32[]{:S(2)}, u32[]{:S(2)}) %collective-permute-start.3) | collective-permute-done | bytes 131104 | tf_op jit(solution)/shard_map/ppermute | solution.py:26
  21.7 0.1 collective-permute-start.4
  21.8 1.3 %collective-permute-done.6 = f32[64,512]{1,0:T(8,128)S(1)} collective-permute-done((f32[64,512]{1,0:T(8,128)S(1)}, f32[64,512]{1,0:T(8,128)S(1)}, u32[]{:S(2)}, u32[]{:S(2)}) %collective-permute-start.6) | collective-permute-done | bytes 131104 | tf_op jit(solution)/shard_map/ppermute | solution.py:26
  23.2 2.6 %collective-permute-start.7 = (f32[128,512]{1,0:T(8,128)S(1)}, f32[128,512]{1,0:T(8,128)S(1)}, u32[]{:S(2)}, u32[]{:S(2)}) collective-permute-start(f32[128,512]{1,0:T(8,128)S(1)} %pad_maximum_fusion.1), channel_id=1, source_target_pairs={{0,12},{4,0},{8,4},{12,8},{1,13},{5,1},{9,5},{13,9},{2,14},{6,2},{... | collective-permute-start | bytes 786440 | tf_op jit(solution)/shard_map/ppermute | solution.py:26
  25.8 0.0 collective-permute-done
  25.8 4.4 %collective-permute-done.4 = f32[128,512]{1,0:T(8,128)S(1)} collective-permute-done((f32[128,512]{1,0:T(8,128)S(1)}, f32[128,512]{1,0:T(8,128)S(1)}, u32[]{:S(2)}, u32[]{:S(2)}) %collective-permute-start.4) | collective-permute-done | bytes 262176 | tf_op jit(solution)/shard_map/ppermute | solution.py:26
  30.3 0.0 collective-permute-done.7
  30.3 0.0 copy-done
  30.3 0.7 convolution_bitcast_fusion
  30.9 0.2 copy.5
  31.1 15.9 %all_to_all.10 = f32[16,64,128]{2,1,0:T(8,128)S(1)} all-to-all(f32[16,64,128]{2,1,0:T(8,128)S(1)} %bitcast.11), channel_id=1, replica_groups=mesh['y'=4,'xh'=2,'z'=4,'xl'=2,'core'=2] {'y','xh','xl'}, dimensions={0} | all-to-all | bytes 1048576 | tf_op jit(solution)/shard_map/all_to_all | solution.py:243
  47.1 13.8 %all_to_all.11 = f32[16,64,128]{2,1,0:T(8,128)S(1)} all-to-all(f32[16,64,128]{2,1,0:T(8,128)S(1)} %broadcast_in_dim.3), channel_id=1, replica_groups={{0,2,16,18,32,34,48,50,64,66,80,82,96,98,112,114},{4,6,20,22,36,38,52,5..., dimensions={0} | all-to-all | bytes 1048576 | tf_op jit(solution)/shard_map/all_to_all | solution.py:246
  60.9 0.9 collective-permute-start.10
  61.7 0.6 collective-permute-start.8
  62.3 4.8 %collective-permute-start.14 = (f32[1024,128]{1,0:T(8,128)S(1)}, f32[1024,128]{1,0:T(8,128)S(1)}, u32[]{:S(2)}, u32[]{:S(2)}) collective-permute-start(f32[1024,128]{1,0:T(8,128)S(1)} %bitcast.8), channel_id=1, source_target_pairs={{0,1},{1,0},{2,3},{3,2},{4,5},{5,4},{6,7},{7,6},{8,9},{9,8},{10,11... | collective-permute-start | bytes 1572872 | tf_op jit(solution)/shard_map/ppermute | solution.py:26
  67.1 2.1 %collective-permute-done.10.refs_2_ = f32[1024,128]{1,0:T(8,128)S(1)} collective-permute-done((f32[1024,128]{1,0:T(8,128)S(1)}, f32[1024,128]{1,0:T(8,128)S(1)}, u32[]{:S(2)}, u32[]{:S(2)}) %collective-permute-start.10) | collective-permute-done | bytes 524320 | tf_op jit(solution)/shard_map/ppermute | solution.py:36
  69.2 1.8 %collective-permute-start.11 = (f32[512,128]{1,0:T(8,128)S(1)}, f32[512,128]{1,0:T(8,128)S(1)}, u32[]{:S(2)}, u32[]{:S(2)}) collective-permute-start(f32[512,128]{1,0:T(8,128)S(1)} %slice.39), channel_id=1, source_target_pairs={{0,12},{1,97},{4,0},{5,101},{8,4},{9,105},{12,8},{13,109},{2,14},{... | collective-permute-start | bytes 786440 | tf_op jit(solution)/shard_map/ppermute | solution.py:36
  71.1 6.5 %collective-permute-start.16 = (f32[1024,128]{1,0:T(8,128)S(1)}, f32[1024,128]{1,0:T(8,128)S(1)}, u32[]{:S(2)}, u32[]{:S(2)}) collective-permute-start(f32[1024,128]{1,0:T(8,128)S(1)} %collective-permute-done.10.refs_2_), channel_id=1, source_target_pairs={{0,1},{1,0},{2,3},{3,2},{4,5},{5,4},{6,7},{7,6},{8,9},{9,8},{10,11... | collective-permute-start | bytes 1572872 | tf_op jit(solution)/shard_map/ppermute | solution.py:26
  77.6 0.0 collective-permute-done.8.refs_1_
  77.6 0.0 collective-permute-start.15
  77.6 0.1 collective-permute-start.9
  77.7 0.0 collective-permute-done.11.refs_1_
  77.7 3.8 %collective-permute-start.13 = (f32[512,128]{1,0:T(8,128)S(1)}, f32[512,128]{1,0:T(8,128)S(1)}, u32[]{:S(2)}, u32[]{:S(2)}) collective-permute-start(f32[512,128]{1,0:T(8,128)S(1)} %collective-permute-done.11.refs_1_), channel_id=1, source_target_pairs={{0,1},{1,0},{2,3},{3,2},{4,5},{5,4},{6,7},{7,6},{8,9},{9,8},{10,11... | collective-permute-start | bytes 786440 | tf_op jit(solution)/shard_map/ppermute | solution.py:26
  81.5 2.9 %collective-permute-done.9.refs_0_ = f32[512,128]{1,0:T(8,128)S(1)} collective-permute-done((f32[512,128]{1,0:T(8,128)S(1)}, f32[512,128]{1,0:T(8,128)S(1)}, u32[]{:S(2)}, u32[]{:S(2)}) %collective-permute-start.9) | collective-permute-done | bytes 262176 | tf_op jit(solution)/shard_map/ppermute | solution.py:36
  84.4 1.4 %collective-permute-start.12 = (f32[512,128]{1,0:T(8,128)S(1)}, f32[512,128]{1,0:T(8,128)S(1)}, u32[]{:S(2)}, u32[]{:S(2)}) collective-permute-start(f32[512,128]{1,0:T(8,128)S(1)} %collective-permute-done.9.refs_0_), channel_id=1, source_target_pairs={{0,1},{1,0},{2,3},{3,2},{4,5},{5,4},{6,7},{7,6},{8,9},{9,8},{10,11... | collective-permute-start | bytes 786440 | tf_op jit(solution)/shard_map/ppermute | solution.py:26
  85.8 0.0 collective-permute-done.14.refs_3_
  85.8 0.0 collective-permute-done.16.refs_5_
  85.8 0.0 collective-permute-done.15.refs_4_
  85.8 1.8 %place_near.1.refs_4_ = f32[1024,1024]{1,0:T(8,128)} custom-call(f32[1024,128]{1,0:T(8,128)S(1)} %bitcast.9, f32[1024,128]{1,0:T(8,128)S(1)} %collective-permute-done.8.refs_1_, f32[1024,128]{1,0:T(8,128)S(1)} %collective-permute-done.10.refs_2_, f32[1024,128]{1,0:T(8,128)S(1)} %collective-permute-done.14.refs_3_, ...), custom_call_target="tpu_custom_call" | custom-call | tf_op jit(solution)/shard_map/place_near/pallas_call | solution.py:188
  87.6 0.0 collective-permute-done.13.refs_3_
  87.6 0.0 collective-permute-done.12.refs_2_
  87.6 1.0 %place_far.1 = f32[1024,1024]{1,0:T(8,128)} custom-call(f32[512,128]{1,0:T(8,128)S(1)} %collective-permute-done.9.refs_0_, f32[512,128]{1,0:T(8,128)S(1)} %collective-permute-done.11.refs_1_, f32[512,128]{1,0:T(8,128)S(1)} %collective-permute-done.12.refs_2_, f32[512,128]{1,0:T(8,128)S(1)} %collective-permute-done.13.refs_3_, ...), custom_call_target="tpu_custom_call", output_to_operand_aliasing={{}: (4, {})} | custom-call | tf_op jit(solution)/shard_map/place_far/pallas_call | solution.py:200
  (12 shorter events, 0.3 us)
Async XLA Ops:
  0.0 30.3 %copy-start = (bf16[512,1024]{1,0:T(8,128)(2,1)S(1)}, bf16[512,1024]{1,0:T(8,128)(2,1)}, u32[]{:S(2)}) copy-start(bf16[512,1024]{1,0:T(8,128)(2,1)} %param.5) | copy-start | bytes 3145732
  4.8 9.0 %collective-permute-start.2 = (f32[128,512]{1,0:T(8,128)S(1)}, f32[128,512]{1,0:T(8,128)S(1)}, u32[]{:S(2)}, u32[]{:S(2)}) collective-permute-start(f32[128,512]{1,0:T(8,128)S(1)} %get-tuple-element.26), channel_id=1, source_target_pairs={{0,1},{1,0},{2,3},{3,2},{4,5},{5,4},{6,7},{7,6},{8,9},{9,8},{10,11... | collective-permute-start | bytes 786440 | tf_op jit(solution)/shard_map/ppermute | solution.py:26
  9.7 10.2 %collective-permute-start.1 = (f32[128,512]{1,0:T(8,128)S(1)}, f32[128,512]{1,0:T(8,128)S(1)}, u32[]{:S(2)}, u32[]{:S(2)}) collective-permute-start(f32[128,512]{1,0:T(8,128)S(1)} %get-tuple-element.24), channel_id=1, source_target_pairs={{0,1},{1,0},{2,3},{3,2},{4,5},{5,4},{6,7},{7,6},{8,9},{9,8},{10,11... | collective-permute-start | bytes 786440 | tf_op jit(solution)/shard_map/ppermute | solution.py:26
  13.2 6.7 %collective-permute-start.5 = (f32[128,512]{1,0:T(8,128)S(1)}, f32[128,512]{1,0:T(8,128)S(1)}, u32[]{:S(2)}, u32[]{:S(2)}) collective-permute-start(f32[128,512]{1,0:T(8,128)S(1)} %get-tuple-element.28), channel_id=1, source_target_pairs={{0,1},{1,0},{2,3},{3,2},{4,5},{5,4},{6,7},{7,6},{8,9},{9,8},{10,11... | collective-permute-start | bytes 786440 | tf_op jit(solution)/shard_map/ppermute | solution.py:26
  13.9 7.8 %collective-permute-start.3 = (f32[64,512]{1,0:T(8,128)S(1)}, f32[64,512]{1,0:T(8,128)S(1)}, u32[]{:S(2)}, u32[]{:S(2)}) collective-permute-start(f32[64,512]{1,0:T(8,128)S(1)} %get-tuple-element.31), channel_id=1, source_target_pairs={{0,4},{4,8},{8,12},{12,0},{1,5},{5,9},{9,13},{13,1},{2,6},{6,10},{... | collective-permute-start | bytes 393224 | tf_op jit(solution)/shard_map/ppermute | solution.py:26
  17.5 8.3 %collective-permute-start = (f32[128,512]{1,0:T(8,128)S(1)}, f32[128,512]{1,0:T(8,128)S(1)}, u32[]{:S(2)}, u32[]{:S(2)}) collective-permute-start(f32[128,512]{1,0:T(8,128)S(1)} %get-tuple-element.22), channel_id=1, source_target_pairs={{0,1},{1,0},{2,3},{3,2},{4,5},{5,4},{6,7},{7,6},{8,9},{9,8},{10,11... | collective-permute-start | bytes 786440 | tf_op jit(solution)/shard_map/ppermute | solution.py:26
  17.9 5.2 %collective-permute-start.6 = (f32[64,512]{1,0:T(8,128)S(1)}, f32[64,512]{1,0:T(8,128)S(1)}, u32[]{:S(2)}, u32[]{:S(2)}) collective-permute-start(f32[64,512]{1,0:T(8,128)S(1)} %get-tuple-element.32), channel_id=1, source_target_pairs={{0,12},{4,0},{8,4},{12,8},{1,13},{5,1},{9,5},{13,9},{2,14},{6,2},{... | collective-permute-start | bytes 393224 | tf_op jit(solution)/shard_map/ppermute | solution.py:26
  21.7 8.5 %collective-permute-start.4 = (f32[128,512]{1,0:T(8,128)S(1)}, f32[128,512]{1,0:T(8,128)S(1)}, u32[]{:S(2)}, u32[]{:S(2)}) collective-permute-start(f32[128,512]{1,0:T(8,128)S(1)} %pad_maximum_fusion), channel_id=1, source_target_pairs={{0,4},{4,8},{8,12},{12,0},{1,5},{5,9},{9,13},{13,1},{2,6},{6,10},{... | collective-permute-start | bytes 786440 | tf_op jit(solution)/shard_map/ppermute | solution.py:26
  23.2 7.1 %collective-permute-start.7 = (f32[128,512]{1,0:T(8,128)S(1)}, f32[128,512]{1,0:T(8,128)S(1)}, u32[]{:S(2)}, u32[]{:S(2)}) collective-permute-start(f32[128,512]{1,0:T(8,128)S(1)} %pad_maximum_fusion.1), channel_id=1, source_target_pairs={{0,12},{4,0},{8,4},{12,8},{1,13},{5,1},{9,5},{13,9},{2,14},{6,2},{... | collective-permute-start | bytes 786440 | tf_op jit(solution)/shard_map/ppermute | solution.py:26
  60.9 8.3 %collective-permute-start.10 = (f32[1024,128]{1,0:T(8,128)S(1)}, f32[1024,128]{1,0:T(8,128)S(1)}, u32[]{:S(2)}, u32[]{:S(2)}) collective-permute-start(f32[1024,128]{1,0:T(8,128)S(1)} %bitcast.6), channel_id=1, source_target_pairs={{0,12},{1,97},{4,0},{5,101},{8,4},{9,105},{12,8},{13,109},{2,14},{... | collective-permute-start | bytes 1572872 | tf_op jit(solution)/shard_map/ppermute | solution.py:36
  61.7 15.9 %collective-permute-start.8 = (f32[1024,128]{1,0:T(8,128)S(1)}, f32[1024,128]{1,0:T(8,128)S(1)}, u32[]{:S(2)}, u32[]{:S(2)}) collective-permute-start(f32[1024,128]{1,0:T(8,128)S(1)} %bitcast.7), channel_id=1, source_target_pairs={{0,4},{1,33},{4,8},{5,37},{8,12},{9,41},{12,0},{13,45},{2,6},{3,35... | collective-permute-start | bytes 1572872 | tf_op jit(solution)/shard_map/ppermute | solution.py:36
  62.3 23.5 %collective-permute-start.14 = (f32[1024,128]{1,0:T(8,128)S(1)}, f32[1024,128]{1,0:T(8,128)S(1)}, u32[]{:S(2)}, u32[]{:S(2)}) collective-permute-start(f32[1024,128]{1,0:T(8,128)S(1)} %bitcast.8), channel_id=1, source_target_pairs={{0,1},{1,0},{2,3},{3,2},{4,5},{5,4},{6,7},{7,6},{8,9},{9,8},{10,11... | collective-permute-start | bytes 1572872 | tf_op jit(solution)/shard_map/ppermute | solution.py:26
  69.2 8.5 %collective-permute-start.11 = (f32[512,128]{1,0:T(8,128)S(1)}, f32[512,128]{1,0:T(8,128)S(1)}, u32[]{:S(2)}, u32[]{:S(2)}) collective-permute-start(f32[512,128]{1,0:T(8,128)S(1)} %slice.39), channel_id=1, source_target_pairs={{0,12},{1,97},{4,0},{5,101},{8,4},{9,105},{12,8},{13,109},{2,14},{... | collective-permute-start | bytes 786440 | tf_op jit(solution)/shard_map/ppermute | solution.py:36
  71.1 14.7 %collective-permute-start.16 = (f32[1024,128]{1,0:T(8,128)S(1)}, f32[1024,128]{1,0:T(8,128)S(1)}, u32[]{:S(2)}, u32[]{:S(2)}) collective-permute-start(f32[1024,128]{1,0:T(8,128)S(1)} %collective-permute-done.10.refs_2_), channel_id=1, source_target_pairs={{0,1},{1,0},{2,3},{3,2},{4,5},{5,4},{6,7},{7,6},{8,9},{9,8},{10,11... | collective-permute-start | bytes 1572872 | tf_op jit(solution)/shard_map/ppermute | solution.py:26
  77.6 8.2 %collective-permute-start.15 = (f32[1024,128]{1,0:T(8,128)S(1)}, f32[1024,128]{1,0:T(8,128)S(1)}, u32[]{:S(2)}, u32[]{:S(2)}) collective-permute-start(f32[1024,128]{1,0:T(8,128)S(1)} %collective-permute-done.8.refs_1_), channel_id=1, source_target_pairs={{0,1},{1,0},{2,3},{3,2},{4,5},{5,4},{6,7},{7,6},{8,9},{9,8},{10,11... | collective-permute-start | bytes 1572872 | tf_op jit(solution)/shard_map/ppermute | solution.py:26
  77.6 6.8 %collective-permute-start.9 = (f32[512,128]{1,0:T(8,128)S(1)}, f32[512,128]{1,0:T(8,128)S(1)}, u32[]{:S(2)}, u32[]{:S(2)}) collective-permute-start(f32[512,128]{1,0:T(8,128)S(1)} %slice.38), channel_id=1, source_target_pairs={{0,4},{1,33},{4,8},{5,37},{8,12},{9,41},{12,0},{13,45},{2,6},{3,35... | collective-permute-start | bytes 786440 | tf_op jit(solution)/shard_map/ppermute | solution.py:36
  77.7 9.9 %collective-permute-start.13 = (f32[512,128]{1,0:T(8,128)S(1)}, f32[512,128]{1,0:T(8,128)S(1)}, u32[]{:S(2)}, u32[]{:S(2)}) collective-permute-start(f32[512,128]{1,0:T(8,128)S(1)} %collective-permute-done.11.refs_1_), channel_id=1, source_target_pairs={{0,1},{1,0},{2,3},{3,2},{4,5},{5,4},{6,7},{7,6},{8,9},{9,8},{10,11... | collective-permute-start | bytes 786440 | tf_op jit(solution)/shard_map/ppermute | solution.py:26
  84.4 3.2 %collective-permute-start.12 = (f32[512,128]{1,0:T(8,128)S(1)}, f32[512,128]{1,0:T(8,128)S(1)}, u32[]{:S(2)}, u32[]{:S(2)}) collective-permute-start(f32[512,128]{1,0:T(8,128)S(1)} %collective-permute-done.9.refs_0_), channel_id=1, source_target_pairs={{0,1},{1,0},{2,3},{3,2},{4,5},{5,4},{6,7},{7,6},{8,9},{9,8},{10,11... | collective-permute-start | bytes 786440 | tf_op jit(solution)/shard_map/ppermute | solution.py:26
where the time goes:
time: 88.9 us; the launch traced here: 88.7 us
  blocking collectives  29.7 us (33%)
  starting transfers between devices  28.8 us (32%)
  Pallas kernels  16.3 us (18%)
  waiting for transfers between devices  12.5 us (14%)
    ppermute x13, starting transfers between devices, shift(): lax.ppermute(value, axis, [(i, (i + step) % size) for i in range(size)])  25.4 us
    all_to_all x1, blocking collectives, body(): parts = lax.all_to_all(parts, PLANE, 0, 0, tiled=True)  15.9 us
    all_to_all x1, blocking collectives, body(): lax.all_to_all(copies, AXES, 0, 0, tiled=True, axis_index_groups=plane_gr...  13.8 us
    ppermute x13, waiting for transfers between devices, shift(): lax.ppermute(value, axis, [(i, (i + step) % size) for i in range(size)])  7.51 us
    pallas_call x2, Pallas kernels, middle(): return call(resident(h_here), resident(v_here), v)  6.84 us
    ppermute x4, waiting for transfers between devices, ring_shift(): return lax.ppermute(value, AXES, pairs)  5.01 us
    pallas_call x1, Pallas kernels, opening(): kernel_call(kernel, h, v, [HBM, HBM], [slab, block], [block, total, sems])  4.79 us
    ppermute x4, starting transfers between devices, ring_shift(): return lax.ppermute(value, AXES, pairs)  3.39 us
  transfers between devices with their start and end apart: 17, of which 5 were waited for; matrix products, arithmetic and copies ran while one was open for 0% of the time, Pallas kernels for 12%

commit v1 on v0

--- a/solution.py
+++ b/solution.py
@@ -57,10 +57,10 @@
     return lax.dot_general(left, right, (((0,), (0,)), ((), ())), preferred_element_type=F32)
 
 
-def columns_of(v, ahead, rows=None):
+def columns_of(v, ahead, rows):
     width = v.shape[1] // 4
     column = pl.multiple_of(lax.rem(lax.axis_index("z") + ahead, 4) * width, width)
-    return v.at[:, pl.ds(column, width)] if rows is None else v.at[rows, pl.ds(column, width)]
+    return v.at[rows, pl.ds(column, width)]
 
 
 def emit(total, keep, give):
@@ -70,35 +70,61 @@
     give[...] = total[pl.ds(pl.multiple_of((1 - core) * rows, rows), rows), :]
 
 
-def opening_kernel(ahead, following, h, v, keep, give, h_here, v_next, v_here, total, sem):
+def fetch(v, ahead, here, sem, base):
     copies = []
-    for i, (start, size) in enumerate(cuts(h.shape[0])):
+    for i, (start, size) in enumerate(cuts(v.shape[0])):
         rows = pl.ds(start, size)
-        one = pltpu.make_async_copy(h.at[rows], h_here.at[rows], sem.at[2 * i])
-        two = pltpu.make_async_copy(columns_of(v, ahead, rows), v_here.at[rows], sem.at[2 * i + 1])
+        copies.append(pltpu.make_async_copy(columns_of(v, ahead, rows), here.at[rows], sem.at[base + i]))
+    return copies
+
+
+def accumulate(total, v_here, h_here, start, size):
+    part = multiply(v_here[start : start + size], h_here[start : start + size])
+    if start == 0:
+        total[...] = part
+    else:
+        total[...] += part
+
+
+def opening_kernel(ahead, h, v, keep, give, h_here, v_here, total, sem):
+    spans = cuts(h.shape[0])
+    ours = fetch(v, ahead, v_here, sem, 0)
+    slab = []
+    for i, (start, size) in enumerate(spans):
+        rows = pl.ds(start, size)
+        slab.append(pltpu.make_async_copy(h.at[rows], h_here.at[rows], sem.at[len(spans) + i]))
+    for one, two in zip(slab, ours):
         one.start()
         two.start()
-        copies.append((start, size, one, two))
-    fetch = pltpu.make_async_copy(columns_of(v, following), v_next, sem.at[2 * len(copies)])
-    fetch.start()
-    for start, size, one, two in copies:
+    for (start, size), one, two in zip(spans, slab, ours):
         one.wait()
         two.wait()
-        part = multiply(v_here[start : start + size], h_here[start : start + size])
-        if start == 0:
-            total[...] = part
-        else:
-            total[...] += part
-    emit(total, keep, give)
-    fetch.wait()
-
-
-def middle_kernel(following, h_here, v_here, v, keep, give, v_next, total, sem):
-    fetch = pltpu.make_async_copy(columns_of(v, following), v_next, sem)
-    fetch.start()
+        accumulate(total, v_here, h_here, start, size)
+    emit(total, keep, give)
+
+
+def second_kernel(ahead, following, h_here, v, keep, give, v_next, v_here, total, sem):
+    spans = cuts(v.shape[0])
+    ours = fetch(v, ahead, v_here, sem, 0)
+    theirs = fetch(v, following, v_next, sem, len(spans))
+    for copy in (*ours, *theirs):
+        copy.start()
+    for (start, size), copy in zip(spans, ours):
+        copy.wait()
+        accumulate(total, v_here, h_here, start, size)
+    emit(total, keep, give)
+    for copy in theirs:
+        copy.wait()
+
+
+def third_kernel(following, h_here, v_here, v, keep, give, v_next, total, sem):
+    theirs = fetch(v, following, v_next, sem, 0)
+    for copy in theirs:
+        copy.start()
     total[...] = multiply(v_here[...], h_here[...])
     emit(total, keep, give)
-    fetch.wait()
+    for copy in theirs:
+        copy.wait()
 
 
 def closing_kernel(h_here, v_here, keep, give, total):
@@ -126,22 +152,27 @@
     slab = pltpu.VMEM((depth, rows), h.dtype)
     total = pltpu.VMEM((v.shape[1] // 4, rows), F32)
     v = streamed(v)
-    sems = pltpu.SemaphoreType.DMA((2 * len(cuts(depth)) + 1,))
-
-    def opening(ahead, following):
-        kernel = functools.partial(opening_kernel, ahead, following)
-        return kernel_call(kernel, h, v, [HBM, HBM], [slab, block], [block, total, sems])(streamed(h), v)
-
-    def middle(following, h_here, v_here):
-        kernel = functools.partial(middle_kernel, following)
-        call = kernel_call(kernel, h, v, [VMEM, VMEM, HBM], [block], [total, pltpu.SemaphoreType.DMA])
+    sems = pltpu.SemaphoreType.DMA((2 * len(cuts(depth)),))
+
+    def opening(ahead):
+        kernel = functools.partial(opening_kernel, ahead)
+        return kernel_call(kernel, h, v, [HBM, HBM], [slab], [block, total, sems])(streamed(h), v)
+
+    def second(ahead, following, h_here):
+        kernel = functools.partial(second_kernel, ahead, following)
+        call = kernel_call(kernel, h, v, [VMEM, HBM], [block], [block, total, sems])
+        return call(resident(h_here), v)
+
+    def third(following, h_here, v_here):
+        kernel = functools.partial(third_kernel, following)
+        call = kernel_call(kernel, h, v, [VMEM, VMEM, HBM], [block], [total, sems])
         return call(resident(h_here), resident(v_here), v)
 
     def closing(h_here, v_here):
         call = kernel_call(closing_kernel, h, v, [VMEM, VMEM], [], [total])
         return call(resident(h_here), resident(v_here))
 
-    return opening, middle, closing
+    return opening, second, third, closing
 
 
 def near_kernel(*refs):
@@ -213,16 +244,16 @@
     nvec = vectors.shape[1]
     wide = nvec // 8
     half = wide // 2
-    opening, middle, closing = products(h_slab.T, vectors)
-
-    far, give, h_here, v_next = opening(2, 1)
+    opening, second, third, closing = products(h_slab.T, vectors)
+
+    far, give, h_here = opening(2)
     other_far = shift(give, "core", 1)
-    up, give, v_next = middle(3, h_here, v_next)
+    up, give, v_next = second(1, 3, h_here)
     other_up = shift(give, "core", 1)
     far = far + other_far
     from_below = shift(far[:half], "z", 1)
     from_above = shift(far[half:], "z", -1)
-    down, give, v_next = middle(0, h_here, v_next)
+    down, give, v_next = third(0, h_here, v_next)
     other_down = shift(give, "core", 1)
     up, down = up + other_up, down + other_down
     up = jnp.concatenate([up[:half] + from_below, up[half:]])

time: 88.9 us -> 88.5 us (level)
  no operation moved by 1% of the time
where the time goes in v1:
time: 88.5 us; the launch traced here: 88.3 us
  blocking collectives  29.7 us (34%)
  starting transfers between devices  28.8 us (33%)
  Pallas kernels  15.9 us (18%)
  waiting for transfers between devices  12.5 us (14%)
    ppermute x13, starting transfers between devices, shift(): lax.ppermute(value, axis, [(i, (i + step) % size) for i in range(size)])  25.4 us
    all_to_all x1, blocking collectives, body(): parts = lax.all_to_all(parts, PLANE, 0, 0, tiled=True)  15.9 us
    all_to_all x1, blocking collectives, body(): lax.all_to_all(copies, AXES, 0, 0, tiled=True, axis_index_groups=plane_gr...  13.8 us
    ppermute x13, waiting for transfers between devices, shift(): lax.ppermute(value, axis, [(i, (i + step) % size) for i in range(size)])  7.51 us
    ppermute x4, waiting for transfers between devices, ring_shift(): return lax.ppermute(value, AXES, pairs)  5.01 us
    pallas_call x1, Pallas kernels, opening(): kernel_call(kernel, h, v, [HBM, HBM], [slab], [block, total, sems])  4.45 us
    pallas_call x1, Pallas kernels, third(): return call(resident(h_here), resident(v_here), v)  3.47 us
    ppermute x4, starting transfers between devices, ring_shift(): return lax.ppermute(value, AXES, pairs)  3.39 us
  transfers between devices with their start and end apart: 17, of which 5 were waited for; matrix products, arithmetic and copies ran while one was open for 0% of the time, Pallas kernels for 12%

profile of v1, /device:TPU:1, one launch (start us, length us, event | category | flops | bytes accessed | tf_op | source)
XLA Modules:
  0.0 88.3 jit_solution(10969873142527500511)
XLA Ops:
  0.0 0.0 copy-start
  0.0 4.5 %shard_map.37 = (f32[128,512]{1,0:T(8,128)S(1)}, f32[128,512]{1,0:T(8,128)S(1)}, bf16[6000,512]{1,0:T(8,128)(2,1)S(1)}) custom-call(bf16[6000,512]{1,0:T(8,128)(2,1)} %bitcast.10, bf16[6000,1024]{1,0:T(8,128)(2,1)} %v.5), custom_call_target="tpu_custom_call" | custom-call | flops 1572864000 | bytes 3072000 | tf_op jit(solution)/shard_map/pallas_call | solution.py:159
  4.5 1.5 %collective-permute-start.2 = (f32[128,512]{1,0:T(8,128)S(1)}, f32[128,512]{1,0:T(8,128)S(1)}, u32[]{:S(2)}, u32[]{:S(2)}) collective-permute-start(f32[128,512]{1,0:T(8,128)S(1)} %get-tuple-element.24), channel_id=1, source_target_pairs={{0,1},{1,0},{2,3},{3,2},{4,5},{5,4},{6,7},{7,6},{8,9},{9,8},{10,11... | collective-permute-start | bytes 786440 | tf_op jit(solution)/shard_map/ppermute | solution.py:26
  5.9 3.3 %shard_map.38 = (f32[128,512]{1,0:T(8,128)S(1)}, f32[128,512]{1,0:T(8,128)S(1)}, bf16[6000,256]{1,0:T(8,128)(2,1)S(1)}) custom-call(bf16[6000,512]{1,0:T(8,128)(2,1)S(1)} %get-tuple-element.16.h_here, bf16[6000,1024]{1,0:T(8,128)(2,1)} %v.5), custom_call_target="tpu_custom_call" | custom-call | flops 1572864000 | bytes 3072000 | tf_op jit(solution)/shard_map/pallas_call | solution.py:164
  9.3 0.1 collective-permute-start.1
  9.4 3.5 %shard_map.39 = (f32[128,512]{1,0:T(8,128)S(1)}, f32[128,512]{1,0:T(8,128)S(1)}, bf16[6000,256]{1,0:T(8,128)(2,1)S(1)}) custom-call(bf16[6000,512]{1,0:T(8,128)(2,1)S(1)} %get-tuple-element.16.h_here, bf16[6000,256]{1,0:T(8,128)(2,1)S(1)} %get-tuple-element.17.v_here, bf16[6000,1024]{1,0:T(8,128)(2,1)} %v.5), custom_call_target="tpu_custom_call" | custom-call | flops 1572864000 | bytes 3072000 | tf_op jit(solution)/shard_map/pallas_call | solution.py:169
  12.8 0.6 collective-permute-start.5
  13.4 0.0 collective-permute-done.2
  13.5 1.8 %collective-permute-start.3 = (f32[64,512]{1,0:T(8,128)S(1)}, f32[64,512]{1,0:T(8,128)S(1)}, u32[]{:S(2)}, u32[]{:S(2)}) collective-permute-start(f32[64,512]{1,0:T(8,128)S(1)} %get-tuple-element.29), channel_id=1, source_target_pairs={{0,4},{4,8},{8,12},{12,0},{1,5},{5,9},{9,13},{13,1},{2,6},{6,10},{... | collective-permute-start | bytes 393224 | tf_op jit(solution)/shard_map/ppermute | solution.py:26
  15.3 1.9 %shard_map.40 = (f32[128,512]{1,0:T(8,128)S(1)}, f32[128,512]{1,0:T(8,128)S(1)}) custom-call(bf16[6000,512]{1,0:T(8,128)(2,1)S(1)} %get-tuple-element.16.h_here, bf16[6000,256]{1,0:T(8,128)(2,1)S(1)} %get-tuple-element.18.v_here), custom_call_target="tpu_custom_call" | custom-call | flops 1572864000 | bytes 3072000 | tf_op jit(solution)/shard_map/pallas_call | solution.py:173
  17.2 0.4 collective-permute-start
  17.5 1.9 %collective-permute-start.6 = (f32[64,512]{1,0:T(8,128)S(1)}, f32[64,512]{1,0:T(8,128)S(1)}, u32[]{:S(2)}, u32[]{:S(2)}) collective-permute-start(f32[64,512]{1,0:T(8,128)S(1)} %get-tuple-element.30), channel_id=1, source_target_pairs={{0,12},{4,0},{8,4},{12,8},{1,13},{5,1},{9,5},{13,9},{2,14},{6,2},{... | collective-permute-start | bytes 393224 | tf_op jit(solution)/shard_map/ppermute | solution.py:26
  19.5 0.0 collective-permute-done.1
  19.5 0.0 collective-permute-done.5
  19.6 1.7 %collective-permute-done.3 = f32[64,512]{1,0:T(8,128)S(1)} collective-permute-done((f32[64,512]{1,0:T(8,128)S(1)}, f32[64,512]{1,0:T(8,128)S(1)}, u32[]{:S(2)}, u32[]{:S(2)}) %collective-permute-start.3) | collective-permute-done | bytes 131104 | tf_op jit(solution)/shard_map/ppermute | solution.py:26
  21.3 0.1 collective-permute-start.4
  21.4 1.3 %collective-permute-done.6 = f32[64,512]{1,0:T(8,128)S(1)} collective-permute-done((f32[64,512]{1,0:T(8,128)S(1)}, f32[64,512]{1,0:T(8,128)S(1)}, u32[]{:S(2)}, u32[]{:S(2)}) %collective-permute-start.6) | collective-permute-done | bytes 131104 | tf_op jit(solution)/shard_map/ppermute | solution.py:26
  22.8 2.6 %collective-permute-start.7 = (f32[128,512]{1,0:T(8,128)S(1)}, f32[128,512]{1,0:T(8,128)S(1)}, u32[]{:S(2)}, u32[]{:S(2)}) collective-permute-start(f32[128,512]{1,0:T(8,128)S(1)} %pad_maximum_fusion.1), channel_id=1, source_target_pairs={{0,12},{4,0},{8,4},{12,8},{1,13},{5,1},{9,5},{13,9},{2,14},{6,2},{... | collective-permute-start | bytes 786440 | tf_op jit(solution)/shard_map/ppermute | solution.py:26
  25.4 0.0 collective-permute-done
  25.4 4.4 %collective-permute-done.4 = f32[128,512]{1,0:T(8,128)S(1)} collective-permute-done((f32[128,512]{1,0:T(8,128)S(1)}, f32[128,512]{1,0:T(8,128)S(1)}, u32[]{:S(2)}, u32[]{:S(2)}) %collective-permute-start.4) | collective-permute-done | bytes 262176 | tf_op jit(solution)/shard_map/ppermute | solution.py:26
  29.9 0.0 collective-permute-done.7
  29.9 0.0 copy-done
  29.9 0.6 convolution_bitcast_fusion
  30.5 0.2 copy.5
  30.7 15.9 %all_to_all.10 = f32[16,64,128]{2,1,0:T(8,128)S(1)} all-to-all(f32[16,64,128]{2,1,0:T(8,128)S(1)} %bitcast.11), channel_id=1, replica_groups=mesh['y'=4,'xh'=2,'z'=4,'xl'=2,'core'=2] {'y','xh','xl'}, dimensions={0} | all-to-all | bytes 1048576 | tf_op jit(solution)/shard_map/all_to_all | solution.py:274
  46.7 13.8 %all_to_all.11 = f32[16,64,128]{2,1,0:T(8,128)S(1)} all-to-all(f32[16,64,128]{2,1,0:T(8,128)S(1)} %broadcast_in_dim.3), channel_id=1, replica_groups={{0,2,16,18,32,34,48,50,64,66,80,82,96,98,112,114},{4,6,20,22,36,38,52,5..., dimensions={0} | all-to-all | bytes 1048576 | tf_op jit(solution)/shard_map/all_to_all | solution.py:277
  60.5 0.9 collective-permute-start.10
  61.4 0.6 collective-permute-start.8
  62.0 4.8 %collective-permute-start.14 = (f32[1024,128]{1,0:T(8,128)S(1)}, f32[1024,128]{1,0:T(8,128)S(1)}, u32[]{:S(2)}, u32[]{:S(2)}) collective-permute-start(f32[1024,128]{1,0:T(8,128)S(1)} %bitcast.8), channel_id=1, source_target_pairs={{0,1},{1,0},{2,3},{3,2},{4,5},{5,4},{6,7},{7,6},{8,9},{9,8},{10,11... | collective-permute-start | bytes 1572872 | tf_op jit(solution)/shard_map/ppermute | solution.py:26
  66.7 2.1 %collective-permute-done.10.refs_2_ = f32[1024,128]{1,0:T(8,128)S(1)} collective-permute-done((f32[1024,128]{1,0:T(8,128)S(1)}, f32[1024,128]{1,0:T(8,128)S(1)}, u32[]{:S(2)}, u32[]{:S(2)}) %collective-permute-start.10) | collective-permute-done | bytes 524320 | tf_op jit(solution)/shard_map/ppermute | solution.py:36
  68.8 1.8 %collective-permute-start.11 = (f32[512,128]{1,0:T(8,128)S(1)}, f32[512,128]{1,0:T(8,128)S(1)}, u32[]{:S(2)}, u32[]{:S(2)}) collective-permute-start(f32[512,128]{1,0:T(8,128)S(1)} %slice.39), channel_id=1, source_target_pairs={{0,12},{1,97},{4,0},{5,101},{8,4},{9,105},{12,8},{13,109},{2,14},{... | collective-permute-start | bytes 786440 | tf_op jit(solution)/shard_map/ppermute | solution.py:36
  70.7 6.5 %collective-permute-start.16 = (f32[1024,128]{1,0:T(8,128)S(1)}, f32[1024,128]{1,0:T(8,128)S(1)}, u32[]{:S(2)}, u32[]{:S(2)}) collective-permute-start(f32[1024,128]{1,0:T(8,128)S(1)} %collective-permute-done.10.refs_2_), channel_id=1, source_target_pairs={{0,1},{1,0},{2,3},{3,2},{4,5},{5,4},{6,7},{7,6},{8,9},{9,8},{10,11... | collective-permute-start | bytes 1572872 | tf_op jit(solution)/shard_map/ppermute | solution.py:26
  77.2 0.0 collective-permute-done.8.refs_1_
  77.2 0.0 collective-permute-start.15
  77.3 0.1 collective-permute-start.9
  77.3 0.0 collective-permute-done.11.refs_1_
  77.3 3.8 %collective-permute-start.13 = (f32[512,128]{1,0:T(8,128)S(1)}, f32[512,128]{1,0:T(8,128)S(1)}, u32[]{:S(2)}, u32[]{:S(2)}) collective-permute-start(f32[512,128]{1,0:T(8,128)S(1)} %collective-permute-done.11.refs_1_), channel_id=1, source_target_pairs={{0,1},{1,0},{2,3},{3,2},{4,5},{5,4},{6,7},{7,6},{8,9},{9,8},{10,11... | collective-permute-start | bytes 786440 | tf_op jit(solution)/shard_map/ppermute | solution.py:26
  81.1 2.9 %collective-permute-done.9.refs_0_ = f32[512,128]{1,0:T(8,128)S(1)} collective-permute-done((f32[512,128]{1,0:T(8,128)S(1)}, f32[512,128]{1,0:T(8,128)S(1)}, u32[]{:S(2)}, u32[]{:S(2)}) %collective-permute-start.9) | collective-permute-done | bytes 262176 | tf_op jit(solution)/shard_map/ppermute | solution.py:36
  84.1 1.4 %collective-permute-start.12 = (f32[512,128]{1,0:T(8,128)S(1)}, f32[512,128]{1,0:T(8,128)S(1)}, u32[]{:S(2)}, u32[]{:S(2)}) collective-permute-start(f32[512,128]{1,0:T(8,128)S(1)} %collective-permute-done.9.refs_0_), channel_id=1, source_target_pairs={{0,1},{1,0},{2,3},{3,2},{4,5},{5,4},{6,7},{7,6},{8,9},{9,8},{10,11... | collective-permute-start | bytes 786440 | tf_op jit(solution)/shard_map/ppermute | solution.py:26
  85.4 0.0 collective-permute-done.14.refs_3_
  85.4 0.0 collective-permute-done.16.refs_5_
  85.4 0.0 collective-permute-done.15.refs_4_
  85.4 1.8 %place_near.1.refs_4_ = f32[1024,1024]{1,0:T(8,128)} custom-call(f32[1024,128]{1,0:T(8,128)S(1)} %bitcast.9, f32[1024,128]{1,0:T(8,128)S(1)} %collective-permute-done.8.refs_1_, f32[1024,128]{1,0:T(8,128)S(1)} %collective-permute-done.10.refs_2_, f32[1024,128]{1,0:T(8,128)S(1)} %collective-permute-done.14.refs_3_, ...), custom_call_target="tpu_custom_call" | custom-call | tf_op jit(solution)/shard_map/place_near/pallas_call | solution.py:219
  87.2 0.0 collective-permute-done.13.refs_3_
  87.2 0.0 collective-permute-done.12.refs_2_
  87.3 1.0 %place_far.1 = f32[1024,1024]{1,0:T(8,128)} custom-call(f32[512,128]{1,0:T(8,128)S(1)} %collective-permute-done.9.refs_0_, f32[512,128]{1,0:T(8,128)S(1)} %collective-permute-done.11.refs_1_, f32[512,128]{1,0:T(8,128)S(1)} %collective-permute-done.12.refs_2_, f32[512,128]{1,0:T(8,128)S(1)} %collective-permute-done.13.refs_3_, ...), custom_call_target="tpu_custom_call", output_to_operand_aliasing={{}: (4, {})} | custom-call | tf_op jit(solution)/shard_map/place_far/pallas_call | solution.py:231
  (12 shorter events, 0.4 us)
Async XLA Ops:
  0.0 29.9 %copy-start = (bf16[512,1024]{1,0:T(8,128)(2,1)S(1)}, bf16[512,1024]{1,0:T(8,128)(2,1)}, u32[]{:S(2)}) copy-start(bf16[512,1024]{1,0:T(8,128)(2,1)} %param.5) | copy-start | bytes 3145732
  4.5 8.9 %collective-permute-start.2 = (f32[128,512]{1,0:T(8,128)S(1)}, f32[128,512]{1,0:T(8,128)S(1)}, u32[]{:S(2)}, u32[]{:S(2)}) collective-permute-start(f32[128,512]{1,0:T(8,128)S(1)} %get-tuple-element.24), channel_id=1, source_target_pairs={{0,1},{1,0},{2,3},{3,2},{4,5},{5,4},{6,7},{7,6},{8,9},{9,8},{10,11... | collective-permute-start | bytes 786440 | tf_op jit(solution)/shard_map/ppermute | solution.py:26
  9.3 10.2 %collective-permute-start.1 = (f32[128,512]{1,0:T(8,128)S(1)}, f32[128,512]{1,0:T(8,128)S(1)}, u32[]{:S(2)}, u32[]{:S(2)}) collective-permute-start(f32[128,512]{1,0:T(8,128)S(1)} %get-tuple-element.22), channel_id=1, source_target_pairs={{0,1},{1,0},{2,3},{3,2},{4,5},{5,4},{6,7},{7,6},{8,9},{9,8},{10,11... | collective-permute-start | bytes 786440 | tf_op jit(solution)/shard_map/ppermute | solution.py:26
  12.8 6.7 %collective-permute-start.5 = (f32[128,512]{1,0:T(8,128)S(1)}, f32[128,512]{1,0:T(8,128)S(1)}, u32[]{:S(2)}, u32[]{:S(2)}) collective-permute-start(f32[128,512]{1,0:T(8,128)S(1)} %get-tuple-element.26), channel_id=1, source_target_pairs={{0,1},{1,0},{2,3},{3,2},{4,5},{5,4},{6,7},{7,6},{8,9},{9,8},{10,11... | collective-permute-start | bytes 786440 | tf_op jit(solution)/shard_map/ppermute | solution.py:26
  13.5 7.8 %collective-permute-start.3 = (f32[64,512]{1,0:T(8,128)S(1)}, f32[64,512]{1,0:T(8,128)S(1)}, u32[]{:S(2)}, u32[]{:S(2)}) collective-permute-start(f32[64,512]{1,0:T(8,128)S(1)} %get-tuple-element.29), channel_id=1, source_target_pairs={{0,4},{4,8},{8,12},{12,0},{1,5},{5,9},{9,13},{13,1},{2,6},{6,10},{... | collective-permute-start | bytes 393224 | tf_op jit(solution)/shard_map/ppermute | solution.py:26
  17.2 8.3 %collective-permute-start = (f32[128,512]{1,0:T(8,128)S(1)}, f32[128,512]{1,0:T(8,128)S(1)}, u32[]{:S(2)}, u32[]{:S(2)}) collective-permute-start(f32[128,512]{1,0:T(8,128)S(1)} %get-tuple-element.20), channel_id=1, source_target_pairs={{0,1},{1,0},{2,3},{3,2},{4,5},{5,4},{6,7},{7,6},{8,9},{9,8},{10,11... | collective-permute-start | bytes 786440 | tf_op jit(solution)/shard_map/ppermute | solution.py:26
  17.5 5.2 %collective-permute-start.6 = (f32[64,512]{1,0:T(8,128)S(1)}, f32[64,512]{1,0:T(8,128)S(1)}, u32[]{:S(2)}, u32[]{:S(2)}) collective-permute-start(f32[64,512]{1,0:T(8,128)S(1)} %get-tuple-element.30), channel_id=1, source_target_pairs={{0,12},{4,0},{8,4},{12,8},{1,13},{5,1},{9,5},{13,9},{2,14},{6,2},{... | collective-permute-start | bytes 393224 | tf_op jit(solution)/shard_map/ppermute | solution.py:26
  21.3 8.5 %collective-permute-start.4 = (f32[128,512]{1,0:T(8,128)S(1)}, f32[128,512]{1,0:T(8,128)S(1)}, u32[]{:S(2)}, u32[]{:S(2)}) collective-permute-start(f32[128,512]{1,0:T(8,128)S(1)} %pad_maximum_fusion), channel_id=1, source_target_pairs={{0,4},{4,8},{8,12},{12,0},{1,5},{5,9},{9,13},{13,1},{2,6},{6,10},{... | collective-permute-start | bytes 786440 | tf_op jit(solution)/shard_map/ppermute | solution.py:26
  22.8 7.1 %collective-permute-start.7 = (f32[128,512]{1,0:T(8,128)S(1)}, f32[128,512]{1,0:T(8,128)S(1)}, u32[]{:S(2)}, u32[]{:S(2)}) collective-permute-start(f32[128,512]{1,0:T(8,128)S(1)} %pad_maximum_fusion.1), channel_id=1, source_target_pairs={{0,12},{4,0},{8,4},{12,8},{1,13},{5,1},{9,5},{13,9},{2,14},{6,2},{... | collective-permute-start | bytes 786440 | tf_op jit(solution)/shard_map/ppermute | solution.py:26
  60.5 8.3 %collective-permute-start.10 = (f32[1024,128]{1,0:T(8,128)S(1)}, f32[1024,128]{1,0:T(8,128)S(1)}, u32[]{:S(2)}, u32[]{:S(2)}) collective-permute-start(f32[1024,128]{1,0:T(8,128)S(1)} %bitcast.6), channel_id=1, source_target_pairs={{0,12},{1,97},{4,0},{5,101},{8,4},{9,105},{12,8},{13,109},{2,14},{... | collective-permute-start | bytes 1572872 | tf_op jit(solution)/shard_map/ppermute | solution.py:36
  61.4 15.9 %collective-permute-start.8 = (f32[1024,128]{1,0:T(8,128)S(1)}, f32[1024,128]{1,0:T(8,128)S(1)}, u32[]{:S(2)}, u32[]{:S(2)}) collective-permute-start(f32[1024,128]{1,0:T(8,128)S(1)} %bitcast.7), channel_id=1, source_target_pairs={{0,4},{1,33},{4,8},{5,37},{8,12},{9,41},{12,0},{13,45},{2,6},{3,35... | collective-permute-start | bytes 1572872 | tf_op jit(solution)/shard_map/ppermute | solution.py:36
  62.0 23.5 %collective-permute-start.14 = (f32[1024,128]{1,0:T(8,128)S(1)}, f32[1024,128]{1,0:T(8,128)S(1)}, u32[]{:S(2)}, u32[]{:S(2)}) collective-permute-start(f32[1024,128]{1,0:T(8,128)S(1)} %bitcast.8), channel_id=1, source_target_pairs={{0,1},{1,0},{2,3},{3,2},{4,5},{5,4},{6,7},{7,6},{8,9},{9,8},{10,11... | collective-permute-start | bytes 1572872 | tf_op jit(solution)/shard_map/ppermute | solution.py:26
  68.8 8.5 %collective-permute-start.11 = (f32[512,128]{1,0:T(8,128)S(1)}, f32[512,128]{1,0:T(8,128)S(1)}, u32[]{:S(2)}, u32[]{:S(2)}) collective-permute-start(f32[512,128]{1,0:T(8,128)S(1)} %slice.39), channel_id=1, source_target_pairs={{0,12},{1,97},{4,0},{5,101},{8,4},{9,105},{12,8},{13,109},{2,14},{... | collective-permute-start | bytes 786440 | tf_op jit(solution)/shard_map/ppermute | solution.py:36
  70.7 14.7 %collective-permute-start.16 = (f32[1024,128]{1,0:T(8,128)S(1)}, f32[1024,128]{1,0:T(8,128)S(1)}, u32[]{:S(2)}, u32[]{:S(2)}) collective-permute-start(f32[1024,128]{1,0:T(8,128)S(1)} %collective-permute-done.10.refs_2_), channel_id=1, source_target_pairs={{0,1},{1,0},{2,3},{3,2},{4,5},{5,4},{6,7},{7,6},{8,9},{9,8},{10,11... | collective-permute-start | bytes 1572872 | tf_op jit(solution)/shard_map/ppermute | solution.py:26
  77.2 8.2 %collective-permute-start.15 = (f32[1024,128]{1,0:T(8,128)S(1)}, f32[1024,128]{1,0:T(8,128)S(1)}, u32[]{:S(2)}, u32[]{:S(2)}) collective-permute-start(f32[1024,128]{1,0:T(8,128)S(1)} %collective-permute-done.8.refs_1_), channel_id=1, source_target_pairs={{0,1},{1,0},{2,3},{3,2},{4,5},{5,4},{6,7},{7,6},{8,9},{9,8},{10,11... | collective-permute-start | bytes 1572872 | tf_op jit(solution)/shard_map/ppermute | solution.py:26
  77.3 6.8 %collective-permute-start.9 = (f32[512,128]{1,0:T(8,128)S(1)}, f32[512,128]{1,0:T(8,128)S(1)}, u32[]{:S(2)}, u32[]{:S(2)}) collective-permute-start(f32[512,128]{1,0:T(8,128)S(1)} %slice.38), channel_id=1, source_target_pairs={{0,4},{1,33},{4,8},{5,37},{8,12},{9,41},{12,0},{13,45},{2,6},{3,35... | collective-permute-start | bytes 786440 | tf_op jit(solution)/shard_map/ppermute | solution.py:36
  77.3 9.9 %collective-permute-start.13 = (f32[512,128]{1,0:T(8,128)S(1)}, f32[512,128]{1,0:T(8,128)S(1)}, u32[]{:S(2)}, u32[]{:S(2)}) collective-permute-start(f32[512,128]{1,0:T(8,128)S(1)} %collective-permute-done.11.refs_1_), channel_id=1, source_target_pairs={{0,1},{1,0},{2,3},{3,2},{4,5},{5,4},{6,7},{7,6},{8,9},{9,8},{10,11... | collective-permute-start | bytes 786440 | tf_op jit(solution)/shard_map/ppermute | solution.py:26
  84.1 3.2 %collective-permute-start.12 = (f32[512,128]{1,0:T(8,128)S(1)}, f32[512,128]{1,0:T(8,128)S(1)}, u32[]{:S(2)}, u32[]{:S(2)}) collective-permute-start(f32[512,128]{1,0:T(8,128)S(1)} %collective-permute-done.9.refs_0_), channel_id=1, source_target_pairs={{0,1},{1,0},{2,3},{3,2},{4,5},{5,4},{6,7},{7,6},{8,9},{9,8},{10,11... | collective-permute-start | bytes 786440 | tf_op jit(solution)/shard_map/ppermute | solution.py:26

commit v2 on v1

--- a/solution.py
+++ b/solution.py
@@ -57,12 +57,6 @@
     return lax.dot_general(left, right, (((0,), (0,)), ((), ())), preferred_element_type=F32)
 
 
-def columns_of(v, ahead, rows):
-    width = v.shape[1] // 4
-    column = pl.multiple_of(lax.rem(lax.axis_index("z") + ahead, 4) * width, width)
-    return v.at[rows, pl.ds(column, width)]
-
-
 def emit(total, keep, give):
     core = lax.axis_index("core")
     rows = total.shape[0] // 2
@@ -71,10 +65,15 @@
 
 
 def fetch(v, ahead, here, sem, base):
+    wide = here.shape[1] // 2
+    first = pl.multiple_of(lax.rem(lax.axis_index("z") + ahead, 4) * wide, wide)
     copies = []
     for i, (start, size) in enumerate(cuts(v.shape[0])):
         rows = pl.ds(start, size)
-        copies.append(pltpu.make_async_copy(columns_of(v, ahead, rows), here.at[rows], sem.at[base + i]))
+        for k in range(2):
+            source = v.at[rows, pl.ds(pl.multiple_of(first + 4 * wide * k, wide), wide)]
+            place = here.at[rows, pl.ds(k * wide, wide)]
+            copies.append(pltpu.make_async_copy(source, place, sem.at[base + 2 * i + k]))
     return copies
 
 
@@ -92,13 +91,13 @@
     slab = []
     for i, (start, size) in enumerate(spans):
         rows = pl.ds(start, size)
-        slab.append(pltpu.make_async_copy(h.at[rows], h_here.at[rows], sem.at[len(spans) + i]))
-    for one, two in zip(slab, ours):
-        one.start()
-        two.start()
-    for (start, size), one, two in zip(spans, slab, ours):
-        one.wait()
-        two.wait()
+        slab.append(pltpu.make_async_copy(h.at[rows], h_here.at[rows], sem.at[2 * len(spans) + i]))
+    for i in range(len(spans)):
+        for copy in (slab[i], ours[2 * i], ours[2 * i + 1]):
+            copy.start()
+    for i, (start, size) in enumerate(spans):
+        for copy in (slab[i], ours[2 * i], ours[2 * i + 1]):
+            copy.wait()
         accumulate(total, v_here, h_here, start, size)
     emit(total, keep, give)
 
@@ -106,11 +105,12 @@
 def second_kernel(ahead, following, h_here, v, keep, give, v_next, v_here, total, sem):
     spans = cuts(v.shape[0])
     ours = fetch(v, ahead, v_here, sem, 0)
-    theirs = fetch(v, following, v_next, sem, len(spans))
+    theirs = fetch(v, following, v_next, sem, 2 * len(spans))
     for copy in (*ours, *theirs):
         copy.start()
-    for (start, size), copy in zip(spans, ours):
-        copy.wait()
+    for i, (start, size) in enumerate(spans):
+        for copy in (ours[2 * i], ours[2 * i + 1]):
+            copy.wait()
         accumulate(total, v_here, h_here, start, size)
     emit(total, keep, give)
     for copy in theirs:
@@ -152,7 +152,7 @@
     slab = pltpu.VMEM((depth, rows), h.dtype)
     total = pltpu.VMEM((v.shape[1] // 4, rows), F32)
     v = streamed(v)
-    sems = pltpu.SemaphoreType.DMA((2 * len(cuts(depth)),))
+    sems = pltpu.SemaphoreType.DMA((4 * len(cuts(depth)),))
 
     def opening(ahead):
         kernel = functools.partial(opening_kernel, ahead)
@@ -193,12 +193,12 @@
         made = []
         for ref, step, part in first:
             rows = ref.shape[0]
-            column = pl.multiple_of(lax.rem(z + step, 4) * 256, 256)
+            column = pl.multiple_of(lax.rem(z + step, 4) * 128, 128)
             made.append((ref, out.at[pl.ds(part * rows, rows), pl.ds(column, 128)]))
         for ref, step, part in second:
             row = pl.multiple_of(lax.rem(y + step, 4) * 256, 256)
             for k in range(ref.shape[0] // 256):
-                column = (part * 2 + k) * 256 + 128
+                column = 512 + (part * 2 + k) * 128
                 made.append((ref.at[pl.ds(k * 256, 256)], out.at[pl.ds(row, 256), pl.ds(column, 128)]))
         made = [pltpu.make_async_copy(src, dst, sem.at[i]) for i, (src, dst) in enumerate(made)]
         for copy in made:

time: 88.5 us -> 88.8 us (level)
  no operation moved by 1% of the time
where the time goes in v2:
time: 88.8 us; the launch traced here: 88.6 us
  blocking collectives  29.7 us (33%)
  starting transfers between devices  28.8 us (32%)
  Pallas kernels  16.2 us (18%)
  waiting for transfers between devices  12.5 us (14%)
    ppermute x13, starting transfers between devices, shift(): lax.ppermute(value, axis, [(i, (i + step) % size) for i in range(size)])  25.4 us
    all_to_all x1, blocking collectives, body(): parts = lax.all_to_all(parts, PLANE, 0, 0, tiled=True)  15.9 us
    all_to_all x1, blocking collectives, body(): lax.all_to_all(copies, AXES, 0, 0, tiled=True, axis_index_groups=plane_gr...  13.8 us
    ppermute x13, waiting for transfers between devices, shift(): lax.ppermute(value, axis, [(i, (i + step) % size) for i in range(size)])  7.53 us
    ppermute x4, waiting for transfers between devices, ring_shift(): return lax.ppermute(value, AXES, pairs)  5.01 us
    pallas_call x1, Pallas kernels, opening(): kernel_call(kernel, h, v, [HBM, HBM], [slab], [block, total, sems])  4.55 us
    pallas_call x1, Pallas kernels, third(): return call(resident(h_here), resident(v_here), v)  3.57 us
    pallas_call x1, Pallas kernels, second(): return call(resident(h_here), v)  3.4 us
  transfers between devices with their start and end apart: 17, of which 5 were waited for; matrix products, arithmetic and copies ran while one was open for 0% of the time, Pallas kernels for 12%

profile of v2, /device:TPU:1, one launch (start us, length us, event | category | flops | bytes accessed | tf_op | source)
XLA Modules:
  0.0 88.6 jit_solution(14192529141804416652)
XLA Ops:
  0.0 0.0 copy-start
  0.0 4.6 %shard_map.37 = (f32[128,512]{1,0:T(8,128)S(1)}, f32[128,512]{1,0:T(8,128)S(1)}, bf16[6000,512]{1,0:T(8,128)(2,1)S(1)}) custom-call(bf16[6000,512]{1,0:T(8,128)(2,1)} %bitcast.10, bf16[6000,1024]{1,0:T(8,128)(2,1)} %v.5), custom_call_target="tpu_custom_call" | custom-call | flops 1572864000 | bytes 3072000 | tf_op jit(solution)/shard_map/pallas_call | solution.py:159
  4.6 1.5 %collective-permute-start.2 = (f32[128,512]{1,0:T(8,128)S(1)}, f32[128,512]{1,0:T(8,128)S(1)}, u32[]{:S(2)}, u32[]{:S(2)}) collective-permute-start(f32[128,512]{1,0:T(8,128)S(1)} %get-tuple-element.24), channel_id=1, source_target_pairs={{0,1},{1,0},{2,3},{3,2},{4,5},{5,4},{6,7},{7,6},{8,9},{9,8},{10,11... | collective-permute-start | bytes 786440 | tf_op jit(solution)/shard_map/ppermute | solution.py:26
  6.0 3.4 %shard_map.38 = (f32[128,512]{1,0:T(8,128)S(1)}, f32[128,512]{1,0:T(8,128)S(1)}, bf16[6000,256]{1,0:T(8,128)(2,1)S(1)}) custom-call(bf16[6000,512]{1,0:T(8,128)(2,1)S(1)} %get-tuple-element.16.h_here, bf16[6000,1024]{1,0:T(8,128)(2,1)} %v.5), custom_call_target="tpu_custom_call" | custom-call | flops 1572864000 | bytes 3072000 | tf_op jit(solution)/shard_map/pallas_call | solution.py:164
  9.4 0.1 collective-permute-start.1
  9.5 3.6 %shard_map.39 = (f32[128,512]{1,0:T(8,128)S(1)}, f32[128,512]{1,0:T(8,128)S(1)}, bf16[6000,256]{1,0:T(8,128)(2,1)S(1)}) custom-call(bf16[6000,512]{1,0:T(8,128)(2,1)S(1)} %get-tuple-element.16.h_here, bf16[6000,256]{1,0:T(8,128)(2,1)S(1)} %get-tuple-element.17.v_here, bf16[6000,1024]{1,0:T(8,128)(2,1)} %v.5), custom_call_target="tpu_custom_call" | custom-call | flops 1572864000 | bytes 3072000 | tf_op jit(solution)/shard_map/pallas_call | solution.py:169
  13.1 0.6 collective-permute-start.5
  13.7 0.0 collective-permute-done.2
  13.8 1.8 %collective-permute-start.3 = (f32[64,512]{1,0:T(8,128)S(1)}, f32[64,512]{1,0:T(8,128)S(1)}, u32[]{:S(2)}, u32[]{:S(2)}) collective-permute-start(f32[64,512]{1,0:T(8,128)S(1)} %get-tuple-element.29), channel_id=1, source_target_pairs={{0,4},{4,8},{8,12},{12,0},{1,5},{5,9},{9,13},{13,1},{2,6},{6,10},{... | collective-permute-start | bytes 393224 | tf_op jit(solution)/shard_map/ppermute | solution.py:26
  15.6 1.9 %shard_map.40 = (f32[128,512]{1,0:T(8,128)S(1)}, f32[128,512]{1,0:T(8,128)S(1)}) custom-call(bf16[6000,512]{1,0:T(8,128)(2,1)S(1)} %get-tuple-element.16.h_here, bf16[6000,256]{1,0:T(8,128)(2,1)S(1)} %get-tuple-element.18.v_here), custom_call_target="tpu_custom_call" | custom-call | flops 1572864000 | bytes 3072000 | tf_op jit(solution)/shard_map/pallas_call | solution.py:173
  17.4 0.4 collective-permute-start
  17.8 1.9 %collective-permute-start.6 = (f32[64,512]{1,0:T(8,128)S(1)}, f32[64,512]{1,0:T(8,128)S(1)}, u32[]{:S(2)}, u32[]{:S(2)}) collective-permute-start(f32[64,512]{1,0:T(8,128)S(1)} %get-tuple-element.30), channel_id=1, source_target_pairs={{0,12},{4,0},{8,4},{12,8},{1,13},{5,1},{9,5},{13,9},{2,14},{6,2},{... | collective-permute-start | bytes 393224 | tf_op jit(solution)/shard_map/ppermute | solution.py:26
  19.7 0.0 collective-permute-done.1
  19.8 0.0 collective-permute-done.5
  19.8 1.7 %collective-permute-done.3 = f32[64,512]{1,0:T(8,128)S(1)} collective-permute-done((f32[64,512]{1,0:T(8,128)S(1)}, f32[64,512]{1,0:T(8,128)S(1)}, u32[]{:S(2)}, u32[]{:S(2)}) %collective-permute-start.3) | collective-permute-done | bytes 131104 | tf_op jit(solution)/shard_map/ppermute | solution.py:26
  21.6 0.1 collective-permute-start.4
  21.7 1.4 %collective-permute-done.6 = f32[64,512]{1,0:T(8,128)S(1)} collective-permute-done((f32[64,512]{1,0:T(8,128)S(1)}, f32[64,512]{1,0:T(8,128)S(1)}, u32[]{:S(2)}, u32[]{:S(2)}) %collective-permute-start.6) | collective-permute-done | bytes 131104 | tf_op jit(solution)/shard_map/ppermute | solution.py:26
  23.1 2.6 %collective-permute-start.7 = (f32[128,512]{1,0:T(8,128)S(1)}, f32[128,512]{1,0:T(8,128)S(1)}, u32[]{:S(2)}, u32[]{:S(2)}) collective-permute-start(f32[128,512]{1,0:T(8,128)S(1)} %pad_maximum_fusion.1), channel_id=1, source_target_pairs={{0,12},{4,0},{8,4},{12,8},{1,13},{5,1},{9,5},{13,9},{2,14},{6,2},{... | collective-permute-start | bytes 786440 | tf_op jit(solution)/shard_map/ppermute | solution.py:26
  25.7 0.0 collective-permute-done
  25.7 4.4 %collective-permute-done.4 = f32[128,512]{1,0:T(8,128)S(1)} collective-permute-done((f32[128,512]{1,0:T(8,128)S(1)}, f32[128,512]{1,0:T(8,128)S(1)}, u32[]{:S(2)}, u32[]{:S(2)}) %collective-permute-start.4) | collective-permute-done | bytes 262176 | tf_op jit(solution)/shard_map/ppermute | solution.py:26
  30.1 0.0 collective-permute-done.7
  30.1 0.0 copy-done
  30.2 0.6 convolution_bitcast_fusion
  30.8 0.2 copy.5
  31.0 15.9 %all_to_all.10 = f32[16,64,128]{2,1,0:T(8,128)S(1)} all-to-all(f32[16,64,128]{2,1,0:T(8,128)S(1)} %bitcast.11), channel_id=1, replica_groups=mesh['y'=4,'xh'=2,'z'=4,'xl'=2,'core'=2] {'y','xh','xl'}, dimensions={0} | all-to-all | bytes 1048576 | tf_op jit(solution)/shard_map/all_to_all | solution.py:274
  46.9 13.8 %all_to_all.11 = f32[16,64,128]{2,1,0:T(8,128)S(1)} all-to-all(f32[16,64,128]{2,1,0:T(8,128)S(1)} %broadcast_in_dim.3), channel_id=1, replica_groups={{0,2,16,18,32,34,48,50,64,66,80,82,96,98,112,114},{4,6,20,22,36,38,52,5..., dimensions={0} | all-to-all | bytes 1048576 | tf_op jit(solution)/shard_map/all_to_all | solution.py:277
  60.8 0.9 collective-permute-start.10
  61.6 0.6 collective-permute-start.8
  62.2 4.8 %collective-permute-start.14 = (f32[1024,128]{1,0:T(8,128)S(1)}, f32[1024,128]{1,0:T(8,128)S(1)}, u32[]{:S(2)}, u32[]{:S(2)}) collective-permute-start(f32[1024,128]{1,0:T(8,128)S(1)} %bitcast.8), channel_id=1, source_target_pairs={{0,1},{1,0},{2,3},{3,2},{4,5},{5,4},{6,7},{7,6},{8,9},{9,8},{10,11... | collective-permute-start | bytes 1572872 | tf_op jit(solution)/shard_map/ppermute | solution.py:26
  67.0 2.1 %collective-permute-done.10.refs_2_ = f32[1024,128]{1,0:T(8,128)S(1)} collective-permute-done((f32[1024,128]{1,0:T(8,128)S(1)}, f32[1024,128]{1,0:T(8,128)S(1)}, u32[]{:S(2)}, u32[]{:S(2)}) %collective-permute-start.10) | collective-permute-done | bytes 524320 | tf_op jit(solution)/shard_map/ppermute | solution.py:36
  69.1 1.8 %collective-permute-start.11 = (f32[512,128]{1,0:T(8,128)S(1)}, f32[512,128]{1,0:T(8,128)S(1)}, u32[]{:S(2)}, u32[]{:S(2)}) collective-permute-start(f32[512,128]{1,0:T(8,128)S(1)} %slice.39), channel_id=1, source_target_pairs={{0,12},{1,97},{4,0},{5,101},{8,4},{9,105},{12,8},{13,109},{2,14},{... | collective-permute-start | bytes 786440 | tf_op jit(solution)/shard_map/ppermute | solution.py:36
  71.0 6.5 %collective-permute-start.16 = (f32[1024,128]{1,0:T(8,128)S(1)}, f32[1024,128]{1,0:T(8,128)S(1)}, u32[]{:S(2)}, u32[]{:S(2)}) collective-permute-start(f32[1024,128]{1,0:T(8,128)S(1)} %collective-permute-done.10.refs_2_), channel_id=1, source_target_pairs={{0,1},{1,0},{2,3},{3,2},{4,5},{5,4},{6,7},{7,6},{8,9},{9,8},{10,11... | collective-permute-start | bytes 1572872 | tf_op jit(solution)/shard_map/ppermute | solution.py:26
  77.5 0.0 collective-permute-done.8.refs_1_
  77.5 0.0 collective-permute-start.15
  77.5 0.1 collective-permute-start.9
  77.6 0.0 collective-permute-done.11.refs_1_
  77.6 3.8 %collective-permute-start.13 = (f32[512,128]{1,0:T(8,128)S(1)}, f32[512,128]{1,0:T(8,128)S(1)}, u32[]{:S(2)}, u32[]{:S(2)}) collective-permute-start(f32[512,128]{1,0:T(8,128)S(1)} %collective-permute-done.11.refs_1_), channel_id=1, source_target_pairs={{0,1},{1,0},{2,3},{3,2},{4,5},{5,4},{6,7},{7,6},{8,9},{9,8},{10,11... | collective-permute-start | bytes 786440 | tf_op jit(solution)/shard_map/ppermute | solution.py:26
  81.4 2.9 %collective-permute-done.9.refs_0_ = f32[512,128]{1,0:T(8,128)S(1)} collective-permute-done((f32[512,128]{1,0:T(8,128)S(1)}, f32[512,128]{1,0:T(8,128)S(1)}, u32[]{:S(2)}, u32[]{:S(2)}) %collective-permute-start.9) | collective-permute-done | bytes 262176 | tf_op jit(solution)/shard_map/ppermute | solution.py:36
  84.3 1.4 %collective-permute-start.12 = (f32[512,128]{1,0:T(8,128)S(1)}, f32[512,128]{1,0:T(8,128)S(1)}, u32[]{:S(2)}, u32[]{:S(2)}) collective-permute-start(f32[512,128]{1,0:T(8,128)S(1)} %collective-permute-done.9.refs_0_), channel_id=1, source_target_pairs={{0,1},{1,0},{2,3},{3,2},{4,5},{5,4},{6,7},{7,6},{8,9},{9,8},{10,11... | collective-permute-start | bytes 786440 | tf_op jit(solution)/shard_map/ppermute | solution.py:26
  85.7 0.0 collective-permute-done.14.refs_3_
  85.7 0.0 collective-permute-done.16.refs_5_
  85.7 0.0 collective-permute-done.15.refs_4_
  85.7 1.8 %place_near.1.refs_4_ = f32[1024,1024]{1,0:T(8,128)} custom-call(f32[1024,128]{1,0:T(8,128)S(1)} %bitcast.9, f32[1024,128]{1,0:T(8,128)S(1)} %collective-permute-done.8.refs_1_, f32[1024,128]{1,0:T(8,128)S(1)} %collective-permute-done.10.refs_2_, f32[1024,128]{1,0:T(8,128)S(1)} %collective-permute-done.14.refs_3_, ...), custom_call_target="tpu_custom_call" | custom-call | tf_op jit(solution)/shard_map/place_near/pallas_call | solution.py:219
  87.5 0.0 collective-permute-done.13.refs_3_
  87.5 0.0 collective-permute-done.12.refs_2_
  87.5 1.0 %place_far.1 = f32[1024,1024]{1,0:T(8,128)} custom-call(f32[512,128]{1,0:T(8,128)S(1)} %collective-permute-done.9.refs_0_, f32[512,128]{1,0:T(8,128)S(1)} %collective-permute-done.11.refs_1_, f32[512,128]{1,0:T(8,128)S(1)} %collective-permute-done.12.refs_2_, f32[512,128]{1,0:T(8,128)S(1)} %collective-permute-done.13.refs_3_, ...), custom_call_target="tpu_custom_call", output_to_operand_aliasing={{}: (4, {})} | custom-call | tf_op jit(solution)/shard_map/place_far/pallas_call | solution.py:231
  (12 shorter events, 0.4 us)
Async XLA Ops:
  0.0 30.1 %copy-start = (bf16[512,1024]{1,0:T(8,128)(2,1)S(1)}, bf16[512,1024]{1,0:T(8,128)(2,1)}, u32[]{:S(2)}) copy-start(bf16[512,1024]{1,0:T(8,128)(2,1)} %param.5) | copy-start | bytes 3145732
  4.6 9.1 %collective-permute-start.2 = (f32[128,512]{1,0:T(8,128)S(1)}, f32[128,512]{1,0:T(8,128)S(1)}, u32[]{:S(2)}, u32[]{:S(2)}) collective-permute-start(f32[128,512]{1,0:T(8,128)S(1)} %get-tuple-element.24), channel_id=1, source_target_pairs={{0,1},{1,0},{2,3},{3,2},{4,5},{5,4},{6,7},{7,6},{8,9},{9,8},{10,11... | collective-permute-start | bytes 786440 | tf_op jit(solution)/shard_map/ppermute | solution.py:26
  9.4 10.3 %collective-permute-start.1 = (f32[128,512]{1,0:T(8,128)S(1)}, f32[128,512]{1,0:T(8,128)S(1)}, u32[]{:S(2)}, u32[]{:S(2)}) collective-permute-start(f32[128,512]{1,0:T(8,128)S(1)} %get-tuple-element.22), channel_id=1, source_target_pairs={{0,1},{1,0},{2,3},{3,2},{4,5},{5,4},{6,7},{7,6},{8,9},{9,8},{10,11... | collective-permute-start | bytes 786440 | tf_op jit(solution)/shard_map/ppermute | solution.py:26
  13.1 6.7 %collective-permute-start.5 = (f32[128,512]{1,0:T(8,128)S(1)}, f32[128,512]{1,0:T(8,128)S(1)}, u32[]{:S(2)}, u32[]{:S(2)}) collective-permute-start(f32[128,512]{1,0:T(8,128)S(1)} %get-tuple-element.26), channel_id=1, source_target_pairs={{0,1},{1,0},{2,3},{3,2},{4,5},{5,4},{6,7},{7,6},{8,9},{9,8},{10,11... | collective-permute-start | bytes 786440 | tf_op jit(solution)/shard_map/ppermute | solution.py:26
  13.8 7.8 %collective-permute-start.3 = (f32[64,512]{1,0:T(8,128)S(1)}, f32[64,512]{1,0:T(8,128)S(1)}, u32[]{:S(2)}, u32[]{:S(2)}) collective-permute-start(f32[64,512]{1,0:T(8,128)S(1)} %get-tuple-element.29), channel_id=1, source_target_pairs={{0,4},{4,8},{8,12},{12,0},{1,5},{5,9},{9,13},{13,1},{2,6},{6,10},{... | collective-permute-start | bytes 393224 | tf_op jit(solution)/shard_map/ppermute | solution.py:26
  17.4 8.3 %collective-permute-start = (f32[128,512]{1,0:T(8,128)S(1)}, f32[128,512]{1,0:T(8,128)S(1)}, u32[]{:S(2)}, u32[]{:S(2)}) collective-permute-start(f32[128,512]{1,0:T(8,128)S(1)} %get-tuple-element.20), channel_id=1, source_target_pairs={{0,1},{1,0},{2,3},{3,2},{4,5},{5,4},{6,7},{7,6},{8,9},{9,8},{10,11... | collective-permute-start | bytes 786440 | tf_op jit(solution)/shard_map/ppermute | solution.py:26
  17.8 5.2 %collective-permute-start.6 = (f32[64,512]{1,0:T(8,128)S(1)}, f32[64,512]{1,0:T(8,128)S(1)}, u32[]{:S(2)}, u32[]{:S(2)}) collective-permute-start(f32[64,512]{1,0:T(8,128)S(1)} %get-tuple-element.30), channel_id=1, source_target_pairs={{0,12},{4,0},{8,4},{12,8},{1,13},{5,1},{9,5},{13,9},{2,14},{6,2},{... | collective-permute-start | bytes 393224 | tf_op jit(solution)/shard_map/ppermute | solution.py:26
  21.6 8.5 %collective-permute-start.4 = (f32[128,512]{1,0:T(8,128)S(1)}, f32[128,512]{1,0:T(8,128)S(1)}, u32[]{:S(2)}, u32[]{:S(2)}) collective-permute-start(f32[128,512]{1,0:T(8,128)S(1)} %pad_maximum_fusion), channel_id=1, source_target_pairs={{0,4},{4,8},{8,12},{12,0},{1,5},{5,9},{9,13},{13,1},{2,6},{6,10},{... | collective-permute-start | bytes 786440 | tf_op jit(solution)/shard_map/ppermute | solution.py:26
  23.1 7.1 %collective-permute-start.7 = (f32[128,512]{1,0:T(8,128)S(1)}, f32[128,512]{1,0:T(8,128)S(1)}, u32[]{:S(2)}, u32[]{:S(2)}) collective-permute-start(f32[128,512]{1,0:T(8,128)S(1)} %pad_maximum_fusion.1), channel_id=1, source_target_pairs={{0,12},{4,0},{8,4},{12,8},{1,13},{5,1},{9,5},{13,9},{2,14},{6,2},{... | collective-permute-start | bytes 786440 | tf_op jit(solution)/shard_map/ppermute | solution.py:26
  60.8 8.3 %collective-permute-start.10 = (f32[1024,128]{1,0:T(8,128)S(1)}, f32[1024,128]{1,0:T(8,128)S(1)}, u32[]{:S(2)}, u32[]{:S(2)}) collective-permute-start(f32[1024,128]{1,0:T(8,128)S(1)} %bitcast.6), channel_id=1, source_target_pairs={{0,12},{1,97},{4,0},{5,101},{8,4},{9,105},{12,8},{13,109},{2,14},{... | collective-permute-start | bytes 1572872 | tf_op jit(solution)/shard_map/ppermute | solution.py:36
  61.6 15.9 %collective-permute-start.8 = (f32[1024,128]{1,0:T(8,128)S(1)}, f32[1024,128]{1,0:T(8,128)S(1)}, u32[]{:S(2)}, u32[]{:S(2)}) collective-permute-start(f32[1024,128]{1,0:T(8,128)S(1)} %bitcast.7), channel_id=1, source_target_pairs={{0,4},{1,33},{4,8},{5,37},{8,12},{9,41},{12,0},{13,45},{2,6},{3,35... | collective-permute-start | bytes 1572872 | tf_op jit(solution)/shard_map/ppermute | solution.py:36
  62.2 23.5 %collective-permute-start.14 = (f32[1024,128]{1,0:T(8,128)S(1)}, f32[1024,128]{1,0:T(8,128)S(1)}, u32[]{:S(2)}, u32[]{:S(2)}) collective-permute-start(f32[1024,128]{1,0:T(8,128)S(1)} %bitcast.8), channel_id=1, source_target_pairs={{0,1},{1,0},{2,3},{3,2},{4,5},{5,4},{6,7},{7,6},{8,9},{9,8},{10,11... | collective-permute-start | bytes 1572872 | tf_op jit(solution)/shard_map/ppermute | solution.py:26
  69.1 8.5 %collective-permute-start.11 = (f32[512,128]{1,0:T(8,128)S(1)}, f32[512,128]{1,0:T(8,128)S(1)}, u32[]{:S(2)}, u32[]{:S(2)}) collective-permute-start(f32[512,128]{1,0:T(8,128)S(1)} %slice.39), channel_id=1, source_target_pairs={{0,12},{1,97},{4,0},{5,101},{8,4},{9,105},{12,8},{13,109},{2,14},{... | collective-permute-start | bytes 786440 | tf_op jit(solution)/shard_map/ppermute | solution.py:36
  71.0 14.7 %collective-permute-start.16 = (f32[1024,128]{1,0:T(8,128)S(1)}, f32[1024,128]{1,0:T(8,128)S(1)}, u32[]{:S(2)}, u32[]{:S(2)}) collective-permute-start(f32[1024,128]{1,0:T(8,128)S(1)} %collective-permute-done.10.refs_2_), channel_id=1, source_target_pairs={{0,1},{1,0},{2,3},{3,2},{4,5},{5,4},{6,7},{7,6},{8,9},{9,8},{10,11... | collective-permute-start | bytes 1572872 | tf_op jit(solution)/shard_map/ppermute | solution.py:26
  77.5 8.2 %collective-permute-start.15 = (f32[1024,128]{1,0:T(8,128)S(1)}, f32[1024,128]{1,0:T(8,128)S(1)}, u32[]{:S(2)}, u32[]{:S(2)}) collective-permute-start(f32[1024,128]{1,0:T(8,128)S(1)} %collective-permute-done.8.refs_1_), channel_id=1, source_target_pairs={{0,1},{1,0},{2,3},{3,2},{4,5},{5,4},{6,7},{7,6},{8,9},{9,8},{10,11... | collective-permute-start | bytes 1572872 | tf_op jit(solution)/shard_map/ppermute | solution.py:26
  77.5 6.8 %collective-permute-start.9 = (f32[512,128]{1,0:T(8,128)S(1)}, f32[512,128]{1,0:T(8,128)S(1)}, u32[]{:S(2)}, u32[]{:S(2)}) collective-permute-start(f32[512,128]{1,0:T(8,128)S(1)} %slice.38), channel_id=1, source_target_pairs={{0,4},{1,33},{4,8},{5,37},{8,12},{9,41},{12,0},{13,45},{2,6},{3,35... | collective-permute-start | bytes 786440 | tf_op jit(solution)/shard_map/ppermute | solution.py:36
  77.6 9.9 %collective-permute-start.13 = (f32[512,128]{1,0:T(8,128)S(1)}, f32[512,128]{1,0:T(8,128)S(1)}, u32[]{:S(2)}, u32[]{:S(2)}) collective-permute-start(f32[512,128]{1,0:T(8,128)S(1)} %collective-permute-done.11.refs_1_), channel_id=1, source_target_pairs={{0,1},{1,0},{2,3},{3,2},{4,5},{5,4},{6,7},{7,6},{8,9},{9,8},{10,11... | collective-permute-start | bytes 786440 | tf_op jit(solution)/shard_map/ppermute | solution.py:26
  84.3 3.2 %collective-permute-start.12 = (f32[512,128]{1,0:T(8,128)S(1)}, f32[512,128]{1,0:T(8,128)S(1)}, u32[]{:S(2)}, u32[]{:S(2)}) collective-permute-start(f32[512,128]{1,0:T(8,128)S(1)} %collective-permute-done.9.refs_0_), channel_id=1, source_target_pairs={{0,1},{1,0},{2,3},{3,2},{4,5},{5,4},{6,7},{7,6},{8,9},{9,8},{10,11... | collective-permute-start | bytes 786440 | tf_op jit(solution)/shard_map/ppermute | solution.py:26

commit v3 on v1

--- a/solution.py
+++ b/solution.py
@@ -121,7 +121,14 @@
     theirs = fetch(v, following, v_next, sem, 0)
     for copy in theirs:
         copy.start()
-    total[...] = multiply(v_here[...], h_here[...])
+    step = v.shape[0] // 3
+    total[...] = jnp.zeros_like(total)
+
+    @pl.loop(0, 3)
+    def _(i):
+        rows = pl.ds(pl.multiple_of(i * step, 16), step)
+        total[...] += multiply(v_here[rows, :], h_here[rows, :])
+
     emit(total, keep, give)
     for copy in theirs:
         copy.wait()
@@ -176,9 +183,13 @@
 
 
 def near_kernel(*refs):
-    own, other, out, sem = refs[:3], refs[3:6], refs[6], refs[7]
-    steps = (0, 3, 1)
-    write([(ref, step, 0) for ref, step in zip(own, steps)], [(ref, step, 0) for ref, step in zip(other, steps)], out, sem)
+    own, other, out, sem = refs[:5], refs[5:10], refs[10], refs[11]
+    spots = ((0, None), (3, 0), (3, 1), (1, 0), (1, 1))
+
+    def spread(blocks):
+        return [(ref, step, part) for ref, (step, part) in zip(blocks, spots)]
+
+    write(spread(own), spread(other), out, sem)
 
 
 def far_kernel(*refs):
@@ -192,10 +203,11 @@
     def run(first, second):
         made = []
         for ref, step, part in first:
-            rows = ref.shape[0]
+            rows, part = ref.shape[0], part or 0
             column = pl.multiple_of(lax.rem(z + step, 4) * 256, 256)
             made.append((ref, out.at[pl.ds(part * rows, rows), pl.ds(column, 128)]))
         for ref, step, part in second:
+            part = part or 0
             row = pl.multiple_of(lax.rem(y + step, 4) * 256, 256)
             for k in range(ref.shape[0] // 256):
                 column = (part * 2 + k) * 256 + 128
@@ -218,10 +230,10 @@
 def place_near(own, other, nvec):
     return pl.pallas_call(
         near_kernel,
-        in_specs=[ANY] * 6,
+        in_specs=[ANY] * 10,
         out_specs=ANY,
         out_shape=jax.ShapeDtypeStruct((nvec, nvec), F32),
-        scratch_shapes=[pltpu.SemaphoreType.DMA((15,))],
+        scratch_shapes=[pltpu.SemaphoreType.DMA((17,))],
         compiler_params=pltpu.CompilerParams(vmem_limit_bytes=2**20),
         name="place_near",
     )(*own, *other)
@@ -278,15 +290,17 @@
         copies, AXES, 0, 0, tiled=True, axis_index_groups=plane_groups()
     ).reshape(nvec, wide)
 
-    half = nvec // 2
-    below = ring_shift(block, 1)
-    above = ring_shift(block, -1)
+    low, high = block[: nvec // 2], block[nvec // 2 :]
+    below_low = ring_shift(low, 1)
+    above_high = ring_shift(high, -1)
+    below_high = ring_shift(high, 1)
+    above_low = ring_shift(low, -1)
+    far_low = ring_shift(below_low, 1)
+    far_high = ring_shift(above_high, -1)
     other = shift(block, "core", 1)
-    far_low = ring_shift(below[:half], 1)
-    far_high = ring_shift(above[half:], -1)
-    other_below = shift(below, "core", 1)
-    other_above = shift(above, "core", 1)
-    whole = place_near([block, below, above], [other, other_below, other_above], nvec)
+    near = [below_low, below_high, above_low, above_high]
+    other_near = [shift(value, "core", 1) for value in near]
+    whole = place_near([block, *near], [other, *other_near], nvec)
     far = [far_low, far_high]
     return place_far(far, [shift(value, "core", 1) for value in far], whole)
 

time: 88.5 us -> 86.7 us (0.980)
  waiting for transfers between devices: 12.5 us -> 7.83 us
  starting transfers between devices: 28.8 us -> 32.8 us
  Pallas kernels: 15.9 us -> 14.8 us
    ppermute x4 -> x6, waiting for transfers between devices: 5.01 us -> 0.31 us  [ring_shift(): return lax.ppermute(value, AXES, pairs)]
    ppermute x4 -> x6, starting transfers between devices: 3.39 us -> 6.89 us  [ring_shift(): return lax.ppermute(value, AXES, pairs)]
    pallas_call x1, Pallas kernels: 3.47 us -> 2.36 us  [third(): return call(resident(h_here), resident(v_here), v)]
    ppermute x13 -> x15, starting transfers between devices: 25.4 us -> 26 us  [shift(): lax.ppermute(value, axis, [(i, (i + step) % size) for i in range(size)])]
    ppermute x13 -> x15, waiting for transfers between devices: 7.51 us -> 7.52 us  [shift(): lax.ppermute(value, axis, [(i, (i + step) % size) for i in range(size)])]
  transfers between devices with their start and end apart: 17 -> 21, of which waited for: 5 -> 4; matrix products, arithmetic and copies ran while one was open for 0% -> 0% of each run, Pallas kernels for 12% -> 11%
where the time goes in v3:
time: 86.7 us; the launch traced here: 86.6 us
  starting transfers between devices  32.8 us (38%)
  blocking collectives  29.7 us (34%)
  Pallas kernels  14.8 us (17%)
  waiting for transfers between devices  7.83 us (9%)
    ppermute x15, starting transfers between devices, shift(): lax.ppermute(value, axis, [(i, (i + step) % size) for i in range(size)])  26 us
    all_to_all x1, blocking collectives, body(): parts = lax.all_to_all(parts, PLANE, 0, 0, tiled=True)  15.9 us
    all_to_all x1, blocking collectives, body(): lax.all_to_all(copies, AXES, 0, 0, tiled=True, axis_index_groups=plane_gr...  13.8 us
    ppermute x15, waiting for transfers between devices, shift(): lax.ppermute(value, axis, [(i, (i + step) % size) for i in range(size)])  7.52 us
    ppermute x6, starting transfers between devices, ring_shift(): return lax.ppermute(value, AXES, pairs)  6.89 us
    pallas_call x1, Pallas kernels, opening(): kernel_call(kernel, h, v, [HBM, HBM], [slab], [block, total, sems])  4.45 us
    pallas_call x1, Pallas kernels, second(): return call(resident(h_here), v)  3.32 us
    pallas_call x1, Pallas kernels, third(): return call(resident(h_here), resident(v_here), v)  2.36 us
  transfers between devices with their start and end apart: 21, of which 4 were waited for; matrix products, arithmetic and copies ran while one was open for 0% of the time, Pallas kernels for 11%

profile of v3, /device:TPU:1, one launch (start us, length us, event | category | flops | bytes accessed | tf_op | source)
XLA Modules:
  0.0 86.6 jit_solution(10916920080465136408)
XLA Ops:
  0.0 0.0 copy-start
  0.0 4.5 %shard_map.37 = (f32[128,512]{1,0:T(8,128)S(1)}, f32[128,512]{1,0:T(8,128)S(1)}, bf16[6000,512]{1,0:T(8,128)(2,1)S(1)}) custom-call(bf16[6000,512]{1,0:T(8,128)(2,1)} %bitcast.10, bf16[6000,1024]{1,0:T(8,128)(2,1)} %v.5), custom_call_target="tpu_custom_call" | custom-call | flops 1572864000 | bytes 3072000 | tf_op jit(solution)/shard_map/pallas_call | solution.py:166
  4.5 1.5 %collective-permute-start.2 = (f32[128,512]{1,0:T(8,128)S(1)}, f32[128,512]{1,0:T(8,128)S(1)}, u32[]{:S(2)}, u32[]{:S(2)}) collective-permute-start(f32[128,512]{1,0:T(8,128)S(1)} %get-tuple-element.24), channel_id=1, source_target_pairs={{0,1},{1,0},{2,3},{3,2},{4,5},{5,4},{6,7},{7,6},{8,9},{9,8},{10,11... | collective-permute-start | bytes 786440 | tf_op jit(solution)/shard_map/ppermute | solution.py:26
  5.9 3.3 %shard_map.38 = (f32[128,512]{1,0:T(8,128)S(1)}, f32[128,512]{1,0:T(8,128)S(1)}, bf16[6000,256]{1,0:T(8,128)(2,1)S(1)}) custom-call(bf16[6000,512]{1,0:T(8,128)(2,1)S(1)} %get-tuple-element.16.h_here, bf16[6000,1024]{1,0:T(8,128)(2,1)} %v.5), custom_call_target="tpu_custom_call" | custom-call | flops 1572864000 | bytes 3072000 | tf_op jit(solution)/shard_map/pallas_call | solution.py:171
  9.3 0.1 collective-permute-start.1
  9.4 2.4 %shard_map.39 = (f32[128,512]{1,0:T(8,128)S(1)}, f32[128,512]{1,0:T(8,128)S(1)}, bf16[6000,256]{1,0:T(8,128)(2,1)S(1)}) custom-call(bf16[6000,512]{1,0:T(8,128)(2,1)S(1)} %get-tuple-element.16.h_here, bf16[6000,256]{1,0:T(8,128)(2,1)S(1)} %get-tuple-element.17.v_here, bf16[6000,1024]{1,0:T(8,128)(2,1)} %v.5), custom_call_target="tpu_custom_call" | custom-call | flops 1572864000 | bytes 3072000 | tf_op jit(solution)/shard_map/pallas_call | solution.py:176
  11.7 0.6 collective-permute-start.5
  12.3 0.0 collective-permute-done.2
  12.4 1.8 %collective-permute-start.3 = (f32[64,512]{1,0:T(8,128)S(1)}, f32[64,512]{1,0:T(8,128)S(1)}, u32[]{:S(2)}, u32[]{:S(2)}) collective-permute-start(f32[64,512]{1,0:T(8,128)S(1)} %get-tuple-element.31), channel_id=1, source_target_pairs={{0,4},{4,8},{8,12},{12,0},{1,5},{5,9},{9,13},{13,1},{2,6},{6,10},{... | collective-permute-start | bytes 393224 | tf_op jit(solution)/shard_map/ppermute | solution.py:26
  14.2 1.9 %shard_map.40 = (f32[128,512]{1,0:T(8,128)S(1)}, f32[128,512]{1,0:T(8,128)S(1)}) custom-call(bf16[6000,512]{1,0:T(8,128)(2,1)S(1)} %get-tuple-element.16.h_here, bf16[6000,256]{1,0:T(8,128)(2,1)S(1)} %get-tuple-element.18.v_here), custom_call_target="tpu_custom_call" | custom-call | flops 1572864000 | bytes 3072000 | tf_op jit(solution)/shard_map/pallas_call | solution.py:180
  16.0 0.4 collective-permute-start
  16.4 1.9 %collective-permute-start.6 = (f32[64,512]{1,0:T(8,128)S(1)}, f32[64,512]{1,0:T(8,128)S(1)}, u32[]{:S(2)}, u32[]{:S(2)}) collective-permute-start(f32[64,512]{1,0:T(8,128)S(1)} %get-tuple-element.32), channel_id=1, source_target_pairs={{0,12},{4,0},{8,4},{12,8},{1,13},{5,1},{9,5},{13,9},{2,14},{6,2},{... | collective-permute-start | bytes 393224 | tf_op jit(solution)/shard_map/ppermute | solution.py:26
  18.4 0.0 collective-permute-done.1
  18.4 0.0 collective-permute-done.5
  18.5 1.7 %collective-permute-done.3 = f32[64,512]{1,0:T(8,128)S(1)} collective-permute-done((f32[64,512]{1,0:T(8,128)S(1)}, f32[64,512]{1,0:T(8,128)S(1)}, u32[]{:S(2)}, u32[]{:S(2)}) %collective-permute-start.3) | collective-permute-done | bytes 131104 | tf_op jit(solution)/shard_map/ppermute | solution.py:26
  20.2 0.1 collective-permute-start.4
  20.3 1.3 %collective-permute-done.6 = f32[64,512]{1,0:T(8,128)S(1)} collective-permute-done((f32[64,512]{1,0:T(8,128)S(1)}, f32[64,512]{1,0:T(8,128)S(1)}, u32[]{:S(2)}, u32[]{:S(2)}) %collective-permute-start.6) | collective-permute-done | bytes 131104 | tf_op jit(solution)/shard_map/ppermute | solution.py:26
  21.7 2.6 %collective-permute-start.7 = (f32[128,512]{1,0:T(8,128)S(1)}, f32[128,512]{1,0:T(8,128)S(1)}, u32[]{:S(2)}, u32[]{:S(2)}) collective-permute-start(f32[128,512]{1,0:T(8,128)S(1)} %pad_maximum_fusion.1), channel_id=1, source_target_pairs={{0,12},{4,0},{8,4},{12,8},{1,13},{5,1},{9,5},{13,9},{2,14},{6,2},{... | collective-permute-start | bytes 786440 | tf_op jit(solution)/shard_map/ppermute | solution.py:26
  24.3 0.0 collective-permute-done
  24.3 4.4 %collective-permute-done.4 = f32[128,512]{1,0:T(8,128)S(1)} collective-permute-done((f32[128,512]{1,0:T(8,128)S(1)}, f32[128,512]{1,0:T(8,128)S(1)}, u32[]{:S(2)}, u32[]{:S(2)}) %collective-permute-start.4) | collective-permute-done | bytes 262176 | tf_op jit(solution)/shard_map/ppermute | solution.py:26
  28.8 0.0 collective-permute-done.7
  28.8 0.0 copy-done
  28.8 0.6 convolution_bitcast_fusion
  29.4 0.2 copy.5
  29.6 15.9 %all_to_all.10 = f32[16,64,128]{2,1,0:T(8,128)S(1)} all-to-all(f32[16,64,128]{2,1,0:T(8,128)S(1)} %bitcast.11), channel_id=1, replica_groups=mesh['y'=4,'xh'=2,'z'=4,'xl'=2,'core'=2] {'y','xh','xl'}, dimensions={0} | all-to-all | bytes 1048576 | tf_op jit(solution)/shard_map/all_to_all | solution.py:286
  45.6 13.8 %all_to_all.11 = f32[16,64,128]{2,1,0:T(8,128)S(1)} all-to-all(f32[16,64,128]{2,1,0:T(8,128)S(1)} %broadcast_in_dim.3), channel_id=1, replica_groups={{0,2,16,18,32,34,48,50,64,66,80,82,96,98,112,114},{4,6,20,22,36,38,52,5..., dimensions={0} | all-to-all | bytes 1048576 | tf_op jit(solution)/shard_map/all_to_all | solution.py:289
  59.4 0.9 %collective-permute-start.15 = (f32[512,128]{1,0:T(8,128)S(1)}, f32[512,128]{1,0:T(8,128)S(1)}, u32[]{:S(2)}, u32[]{:S(2)}) collective-permute-start(f32[512,128]{1,0:T(8,128)S(1)} %bitcast.14), channel_id=1, source_target_pairs={{0,12},{1,97},{4,0},{5,101},{8,4},{9,105},{12,8},{13,109},{2,14},{... | collective-permute-start | bytes 786440 | tf_op jit(solution)/shard_map/ppermute | solution.py:36
  60.4 0.6 collective-permute-start.8
  61.0 0.2 collective-permute-start.14
  61.2 2.5 %collective-permute-start.10 = (f32[512,128]{1,0:T(8,128)S(1)}, f32[512,128]{1,0:T(8,128)S(1)}, u32[]{:S(2)}, u32[]{:S(2)}) collective-permute-start(f32[512,128]{1,0:T(8,128)S(1)} %bitcast.13), channel_id=1, source_target_pairs={{0,12},{1,97},{4,0},{5,101},{8,4},{9,105},{12,8},{13,109},{2,14},{... | collective-permute-start | bytes 786440 | tf_op jit(solution)/shard_map/ppermute | solution.py:36
  63.6 5.3 %collective-permute-start.16 = (f32[1024,128]{1,0:T(8,128)S(1)}, f32[1024,128]{1,0:T(8,128)S(1)}, u32[]{:S(2)}, u32[]{:S(2)}) collective-permute-start(f32[1024,128]{1,0:T(8,128)S(1)} %bitcast.8), channel_id=1, source_target_pairs={{0,1},{1,0},{2,3},{3,2},{4,5},{5,4},{6,7},{7,6},{8,9},{9,8},{10,11... | collective-permute-start | bytes 1572872 | tf_op jit(solution)/shard_map/ppermute | solution.py:26
  68.9 0.0 collective-permute-done.15.refs_3_
  68.9 0.6 collective-permute-start.19
  69.6 0.0 collective-permute-done.8.refs_1_
  69.6 3.7 %collective-permute-start.17 = (f32[512,128]{1,0:T(8,128)S(1)}, f32[512,128]{1,0:T(8,128)S(1)}, u32[]{:S(2)}, u32[]{:S(2)}) collective-permute-start(f32[512,128]{1,0:T(8,128)S(1)} %collective-permute-done.8.refs_1_), channel_id=1, source_target_pairs={{0,1},{1,0},{2,3},{3,2},{4,5},{5,4},{6,7},{7,6},{8,9},{9,8},{10,11... | collective-permute-start | bytes 786440 | tf_op jit(solution)/shard_map/ppermute | solution.py:26
  73.3 0.0 collective-permute-done.14.refs_2_
  73.3 0.0 collective-permute-start.9
  73.3 0.0 collective-permute-done.10.refs_4_
  73.3 2.7 %collective-permute-start.11 = (f32[512,128]{1,0:T(8,128)S(1)}, f32[512,128]{1,0:T(8,128)S(1)}, u32[]{:S(2)}, u32[]{:S(2)}) collective-permute-start(f32[512,128]{1,0:T(8,128)S(1)} %collective-permute-done.10.refs_4_), channel_id=1, source_target_pairs={{0,12},{1,97},{4,0},{5,101},{8,4},{9,105},{12,8},{13,109},{2,14},{... | collective-permute-start | bytes 786440 | tf_op jit(solution)/shard_map/ppermute | solution.py:36
  75.9 0.0 collective-permute-done.19.refs_8_
  75.9 3.4 %collective-permute-start.18 = (f32[512,128]{1,0:T(8,128)S(1)}, f32[512,128]{1,0:T(8,128)S(1)}, u32[]{:S(2)}, u32[]{:S(2)}) collective-permute-start(f32[512,128]{1,0:T(8,128)S(1)} %collective-permute-done.14.refs_2_), channel_id=1, source_target_pairs={{0,1},{1,0},{2,3},{3,2},{4,5},{5,4},{6,7},{7,6},{8,9},{9,8},{10,11... | collective-permute-start | bytes 786440 | tf_op jit(solution)/shard_map/ppermute | solution.py:26
  79.3 0.0 collective-permute-done.17.refs_6_
  79.3 0.1 collective-permute-start.20
  79.4 0.3 collective-permute-done.9.refs_0_
  79.7 4.0 %collective-permute-start.12 = (f32[512,128]{1,0:T(8,128)S(1)}, f32[512,128]{1,0:T(8,128)S(1)}, u32[]{:S(2)}, u32[]{:S(2)}) collective-permute-start(f32[512,128]{1,0:T(8,128)S(1)} %collective-permute-done.9.refs_0_), channel_id=1, source_target_pairs={{0,1},{1,0},{2,3},{3,2},{4,5},{5,4},{6,7},{7,6},{8,9},{9,8},{10,11... | collective-permute-start | bytes 786440 | tf_op jit(solution)/shard_map/ppermute | solution.py:26
  83.7 0.0 collective-permute-done.11.refs_1_
  83.7 0.0 collective-permute-start.13
  83.7 0.0 collective-permute-done.18.refs_7_
  83.7 0.0 collective-permute-done.20.refs_9_
  83.7 0.0 collective-permute-done.16.refs_5_
  83.7 1.8 %place_near.1.refs_4_ = f32[1024,1024]{1,0:T(8,128)} custom-call(f32[1024,128]{1,0:T(8,128)S(1)} %bitcast.9, f32[512,128]{1,0:T(8,128)S(1)} %collective-permute-done.8.refs_1_, f32[512,128]{1,0:T(8,128)S(1)} %collective-permute-done.14.refs_2_, f32[512,128]{1,0:T(8,128)S(1)} %collective-permute-done.15.refs_3_, ...), custom_call_target="tpu_custom_call" | custom-call | tf_op jit(solution)/shard_map/place_near/pallas_call | solution.py:231
  85.5 0.0 collective-permute-done.12.refs_2_
  85.5 0.0 collective-permute-done.13.refs_3_
  85.5 1.0 %place_far.1 = f32[1024,1024]{1,0:T(8,128)} custom-call(f32[512,128]{1,0:T(8,128)S(1)} %collective-permute-done.9.refs_0_, f32[512,128]{1,0:T(8,128)S(1)} %collective-permute-done.11.refs_1_, f32[512,128]{1,0:T(8,128)S(1)} %collective-permute-done.12.refs_2_, f32[512,128]{1,0:T(8,128)S(1)} %collective-permute-done.13.refs_3_, ...), custom_call_target="tpu_custom_call", output_to_operand_aliasing={{}: (4, {})} | custom-call | tf_op jit(solution)/shard_map/place_far/pallas_call | solution.py:243
  (11 shorter events, 0.4 us)
Async XLA Ops:
  0.0 28.8 %copy-start = (bf16[512,1024]{1,0:T(8,128)(2,1)S(1)}, bf16[512,1024]{1,0:T(8,128)(2,1)}, u32[]{:S(2)}) copy-start(bf16[512,1024]{1,0:T(8,128)(2,1)} %param.5) | copy-start | bytes 3145732
  4.5 7.8 %collective-permute-start.2 = (f32[128,512]{1,0:T(8,128)S(1)}, f32[128,512]{1,0:T(8,128)S(1)}, u32[]{:S(2)}, u32[]{:S(2)}) collective-permute-start(f32[128,512]{1,0:T(8,128)S(1)} %get-tuple-element.24), channel_id=1, source_target_pairs={{0,1},{1,0},{2,3},{3,2},{4,5},{5,4},{6,7},{7,6},{8,9},{9,8},{10,11... | collective-permute-start | bytes 786440 | tf_op jit(solution)/shard_map/ppermute | solution.py:26
  9.3 9.1 %collective-permute-start.1 = (f32[128,512]{1,0:T(8,128)S(1)}, f32[128,512]{1,0:T(8,128)S(1)}, u32[]{:S(2)}, u32[]{:S(2)}) collective-permute-start(f32[128,512]{1,0:T(8,128)S(1)} %get-tuple-element.22), channel_id=1, source_target_pairs={{0,1},{1,0},{2,3},{3,2},{4,5},{5,4},{6,7},{7,6},{8,9},{9,8},{10,11... | collective-permute-start | bytes 786440 | tf_op jit(solution)/shard_map/ppermute | solution.py:26
  11.7 6.7 %collective-permute-start.5 = (f32[128,512]{1,0:T(8,128)S(1)}, f32[128,512]{1,0:T(8,128)S(1)}, u32[]{:S(2)}, u32[]{:S(2)}) collective-permute-start(f32[128,512]{1,0:T(8,128)S(1)} %get-tuple-element.26), channel_id=1, source_target_pairs={{0,1},{1,0},{2,3},{3,2},{4,5},{5,4},{6,7},{7,6},{8,9},{9,8},{10,11... | collective-permute-start | bytes 786440 | tf_op jit(solution)/shard_map/ppermute | solution.py:26
  12.4 7.8 %collective-permute-start.3 = (f32[64,512]{1,0:T(8,128)S(1)}, f32[64,512]{1,0:T(8,128)S(1)}, u32[]{:S(2)}, u32[]{:S(2)}) collective-permute-start(f32[64,512]{1,0:T(8,128)S(1)} %get-tuple-element.31), channel_id=1, source_target_pairs={{0,4},{4,8},{8,12},{12,0},{1,5},{5,9},{9,13},{13,1},{2,6},{6,10},{... | collective-permute-start | bytes 393224 | tf_op jit(solution)/shard_map/ppermute | solution.py:26
  16.0 8.3 %collective-permute-start = (f32[128,512]{1,0:T(8,128)S(1)}, f32[128,512]{1,0:T(8,128)S(1)}, u32[]{:S(2)}, u32[]{:S(2)}) collective-permute-start(f32[128,512]{1,0:T(8,128)S(1)} %get-tuple-element.20), channel_id=1, source_target_pairs={{0,1},{1,0},{2,3},{3,2},{4,5},{5,4},{6,7},{7,6},{8,9},{9,8},{10,11... | collective-permute-start | bytes 786440 | tf_op jit(solution)/shard_map/ppermute | solution.py:26
  16.4 5.2 %collective-permute-start.6 = (f32[64,512]{1,0:T(8,128)S(1)}, f32[64,512]{1,0:T(8,128)S(1)}, u32[]{:S(2)}, u32[]{:S(2)}) collective-permute-start(f32[64,512]{1,0:T(8,128)S(1)} %get-tuple-element.32), channel_id=1, source_target_pairs={{0,12},{4,0},{8,4},{12,8},{1,13},{5,1},{9,5},{13,9},{2,14},{6,2},{... | collective-permute-start | bytes 393224 | tf_op jit(solution)/shard_map/ppermute | solution.py:26
  20.2 8.5 %collective-permute-start.4 = (f32[128,512]{1,0:T(8,128)S(1)}, f32[128,512]{1,0:T(8,128)S(1)}, u32[]{:S(2)}, u32[]{:S(2)}) collective-permute-start(f32[128,512]{1,0:T(8,128)S(1)} %pad_maximum_fusion), channel_id=1, source_target_pairs={{0,4},{4,8},{8,12},{12,0},{1,5},{5,9},{9,13},{13,1},{2,6},{6,10},{... | collective-permute-start | bytes 786440 | tf_op jit(solution)/shard_map/ppermute | solution.py:26
  21.7 7.1 %collective-permute-start.7 = (f32[128,512]{1,0:T(8,128)S(1)}, f32[128,512]{1,0:T(8,128)S(1)}, u32[]{:S(2)}, u32[]{:S(2)}) collective-permute-start(f32[128,512]{1,0:T(8,128)S(1)} %pad_maximum_fusion.1), channel_id=1, source_target_pairs={{0,12},{4,0},{8,4},{12,8},{1,13},{5,1},{9,5},{13,9},{2,14},{6,2},{... | collective-permute-start | bytes 786440 | tf_op jit(solution)/shard_map/ppermute | solution.py:26
  59.4 9.5 %collective-permute-start.15 = (f32[512,128]{1,0:T(8,128)S(1)}, f32[512,128]{1,0:T(8,128)S(1)}, u32[]{:S(2)}, u32[]{:S(2)}) collective-permute-start(f32[512,128]{1,0:T(8,128)S(1)} %bitcast.14), channel_id=1, source_target_pairs={{0,12},{1,97},{4,0},{5,101},{8,4},{9,105},{12,8},{13,109},{2,14},{... | collective-permute-start | bytes 786440 | tf_op jit(solution)/shard_map/ppermute | solution.py:36
  60.4 9.2 %collective-permute-start.8 = (f32[512,128]{1,0:T(8,128)S(1)}, f32[512,128]{1,0:T(8,128)S(1)}, u32[]{:S(2)}, u32[]{:S(2)}) collective-permute-start(f32[512,128]{1,0:T(8,128)S(1)} %bitcast.15), channel_id=1, source_target_pairs={{0,4},{1,33},{4,8},{5,37},{8,12},{9,41},{12,0},{13,45},{2,6},{3,35... | collective-permute-start | bytes 786440 | tf_op jit(solution)/shard_map/ppermute | solution.py:36
  61.0 12.3 %collective-permute-start.14 = (f32[512,128]{1,0:T(8,128)S(1)}, f32[512,128]{1,0:T(8,128)S(1)}, u32[]{:S(2)}, u32[]{:S(2)}) collective-permute-start(f32[512,128]{1,0:T(8,128)S(1)} %bitcast.12), channel_id=1, source_target_pairs={{0,4},{1,33},{4,8},{5,37},{8,12},{9,41},{12,0},{13,45},{2,6},{3,35... | collective-permute-start | bytes 786440 | tf_op jit(solution)/shard_map/ppermute | solution.py:36
  61.2 12.1 %collective-permute-start.10 = (f32[512,128]{1,0:T(8,128)S(1)}, f32[512,128]{1,0:T(8,128)S(1)}, u32[]{:S(2)}, u32[]{:S(2)}) collective-permute-start(f32[512,128]{1,0:T(8,128)S(1)} %bitcast.13), channel_id=1, source_target_pairs={{0,12},{1,97},{4,0},{5,101},{8,4},{9,105},{12,8},{13,109},{2,14},{... | collective-permute-start | bytes 786440 | tf_op jit(solution)/shard_map/ppermute | solution.py:36
  63.6 20.0 %collective-permute-start.16 = (f32[1024,128]{1,0:T(8,128)S(1)}, f32[1024,128]{1,0:T(8,128)S(1)}, u32[]{:S(2)}, u32[]{:S(2)}) collective-permute-start(f32[1024,128]{1,0:T(8,128)S(1)} %bitcast.8), channel_id=1, source_target_pairs={{0,1},{1,0},{2,3},{3,2},{4,5},{5,4},{6,7},{7,6},{8,9},{9,8},{10,11... | collective-permute-start | bytes 1572872 | tf_op jit(solution)/shard_map/ppermute | solution.py:26
  68.9 7.0 %collective-permute-start.19 = (f32[512,128]{1,0:T(8,128)S(1)}, f32[512,128]{1,0:T(8,128)S(1)}, u32[]{:S(2)}, u32[]{:S(2)}) collective-permute-start(f32[512,128]{1,0:T(8,128)S(1)} %collective-permute-done.15.refs_3_), channel_id=1, source_target_pairs={{0,1},{1,0},{2,3},{3,2},{4,5},{5,4},{6,7},{7,6},{8,9},{9,8},{10,11... | collective-permute-start | bytes 786440 | tf_op jit(solution)/shard_map/ppermute | solution.py:26
  69.6 9.7 %collective-permute-start.17 = (f32[512,128]{1,0:T(8,128)S(1)}, f32[512,128]{1,0:T(8,128)S(1)}, u32[]{:S(2)}, u32[]{:S(2)}) collective-permute-start(f32[512,128]{1,0:T(8,128)S(1)} %collective-permute-done.8.refs_1_), channel_id=1, source_target_pairs={{0,1},{1,0},{2,3},{3,2},{4,5},{5,4},{6,7},{7,6},{8,9},{9,8},{10,11... | collective-permute-start | bytes 786440 | tf_op jit(solution)/shard_map/ppermute | solution.py:26
  73.3 6.4 %collective-permute-start.9 = (f32[512,128]{1,0:T(8,128)S(1)}, f32[512,128]{1,0:T(8,128)S(1)}, u32[]{:S(2)}, u32[]{:S(2)}) collective-permute-start(f32[512,128]{1,0:T(8,128)S(1)} %collective-permute-done.8.refs_1_), channel_id=1, source_target_pairs={{0,4},{1,33},{4,8},{5,37},{8,12},{9,41},{12,0},{13,45},{2,6},{3,35... | collective-permute-start | bytes 786440 | tf_op jit(solution)/shard_map/ppermute | solution.py:36
  73.3 10.4 %collective-permute-start.11 = (f32[512,128]{1,0:T(8,128)S(1)}, f32[512,128]{1,0:T(8,128)S(1)}, u32[]{:S(2)}, u32[]{:S(2)}) collective-permute-start(f32[512,128]{1,0:T(8,128)S(1)} %collective-permute-done.10.refs_4_), channel_id=1, source_target_pairs={{0,12},{1,97},{4,0},{5,101},{8,4},{9,105},{12,8},{13,109},{2,14},{... | collective-permute-start | bytes 786440 | tf_op jit(solution)/shard_map/ppermute | solution.py:36
  75.9 7.7 %collective-permute-start.18 = (f32[512,128]{1,0:T(8,128)S(1)}, f32[512,128]{1,0:T(8,128)S(1)}, u32[]{:S(2)}, u32[]{:S(2)}) collective-permute-start(f32[512,128]{1,0:T(8,128)S(1)} %collective-permute-done.14.refs_2_), channel_id=1, source_target_pairs={{0,1},{1,0},{2,3},{3,2},{4,5},{5,4},{6,7},{7,6},{8,9},{9,8},{10,11... | collective-permute-start | bytes 786440 | tf_op jit(solution)/shard_map/ppermute | solution.py:26
  79.3 4.3 %collective-permute-start.20 = (f32[512,128]{1,0:T(8,128)S(1)}, f32[512,128]{1,0:T(8,128)S(1)}, u32[]{:S(2)}, u32[]{:S(2)}) collective-permute-start(f32[512,128]{1,0:T(8,128)S(1)} %collective-permute-done.10.refs_4_), channel_id=1, source_target_pairs={{0,1},{1,0},{2,3},{3,2},{4,5},{5,4},{6,7},{7,6},{8,9},{9,8},{10,11... | collective-permute-start | bytes 786440 | tf_op jit(solution)/shard_map/ppermute | solution.py:26
  79.7 5.8 %collective-permute-start.12 = (f32[512,128]{1,0:T(8,128)S(1)}, f32[512,128]{1,0:T(8,128)S(1)}, u32[]{:S(2)}, u32[]{:S(2)}) collective-permute-start(f32[512,128]{1,0:T(8,128)S(1)} %collective-permute-done.9.refs_0_), channel_id=1, source_target_pairs={{0,1},{1,0},{2,3},{3,2},{4,5},{5,4},{6,7},{7,6},{8,9},{9,8},{10,11... | collective-permute-start | bytes 786440 | tf_op jit(solution)/shard_map/ppermute | solution.py:26
  83.7 1.9 %collective-permute-start.13 = (f32[512,128]{1,0:T(8,128)S(1)}, f32[512,128]{1,0:T(8,128)S(1)}, u32[]{:S(2)}, u32[]{:S(2)}) collective-permute-start(f32[512,128]{1,0:T(8,128)S(1)} %collective-permute-done.11.refs_1_), channel_id=1, source_target_pairs={{0,1},{1,0},{2,3},{3,2},{4,5},{5,4},{6,7},{7,6},{8,9},{9,8},{10,11... | collective-permute-start | bytes 786440 | tf_op jit(solution)/shard_map/ppermute | solution.py:26

commit v4 on v3

--- a/solution.py
+++ b/solution.py
@@ -26,13 +26,23 @@
     return lax.ppermute(value, axis, [(i, (i + step) % size) for i in range(size)])
 
 
-def ring_shift(value, step):
+def cross_z(value, step):
     pairs = []
     for y in range(4):
         for x in range(4):
             for z in range(4):
-                pairs.append((rank(y, x, z, 0), rank(y, x, (z + step) % 4, 0)))
-                pairs.append((rank(y, x, z, 1), rank((y + step) % 4, x, z, 1)))
+                for core in range(2):
+                    pairs.append((rank(y, x, z, core), rank(y, x, (z + step) % 4, 1 - core)))
+    return lax.ppermute(value, AXES, pairs)
+
+
+def ring_shift(value, step, holder):
+    pairs = []
+    for y in range(4):
+        for x in range(4):
+            for z in range(4):
+                pairs.append((rank(y, x, z, holder), rank(y, x, (z + step) % 4, 1 - holder)))
+                pairs.append((rank(y, x, z, 1 - holder), rank((y + step) % 4, x, z, holder)))
     return lax.ppermute(value, AXES, pairs)
 
 
@@ -64,10 +74,10 @@
 
 
 def emit(total, keep, give):
-    core = lax.axis_index("core")
+    side = lax.rem(lax.axis_index("core") + lax.axis_index("z"), 2)
     rows = total.shape[0] // 2
-    keep[...] = total[pl.ds(pl.multiple_of(core * rows, rows), rows), :]
-    give[...] = total[pl.ds(pl.multiple_of((1 - core) * rows, rows), rows), :]
+    keep[...] = total[pl.ds(pl.multiple_of(side * rows, rows), rows), :]
+    give[...] = total[pl.ds(pl.multiple_of((1 - side) * rows, rows), rows), :]
 
 
 def fetch(v, ahead, here, sem, base):
@@ -204,13 +214,15 @@
         made = []
         for ref, step, part in first:
             rows, part = ref.shape[0], part or 0
-            column = pl.multiple_of(lax.rem(z + step, 4) * 256, 256)
+            there = lax.rem(z + step, 4)
+            column = pl.multiple_of(there * 256 + lax.rem(there, 2) * 128, 128)
             made.append((ref, out.at[pl.ds(part * rows, rows), pl.ds(column, 128)]))
         for ref, step, part in second:
             part = part or 0
             row = pl.multiple_of(lax.rem(y + step, 4) * 256, 256)
             for k in range(ref.shape[0] // 256):
-                column = (part * 2 + k) * 256 + 128
+                there = part * 2 + k
+                column = there * 256 + (1 - there % 2) * 128
                 made.append((ref.at[pl.ds(k * 256, 256)], out.at[pl.ds(row, 256), pl.ds(column, 128)]))
         made = [pltpu.make_async_copy(src, dst, sem.at[i]) for i, (src, dst) in enumerate(made)]
         for copy in made:
@@ -263,15 +275,15 @@
     up, give, v_next = second(1, 3, h_here)
     other_up = shift(give, "core", 1)
     far = far + other_far
-    from_below = shift(far[:half], "z", 1)
-    from_above = shift(far[half:], "z", -1)
+    from_below = cross_z(far[:half], 1)
+    from_above = cross_z(far[half:], -1)
     down, give, v_next = third(0, h_here, v_next)
     other_down = shift(give, "core", 1)
     up, down = up + other_up, down + other_down
     up = jnp.concatenate([up[:half] + from_below, up[half:]])
     down = jnp.concatenate([down[:half], down[half:] + from_above])
-    from_below = shift(up, "z", 1)
-    from_above = shift(down, "z", -1)
+    from_below = cross_z(up, 1)
+    from_above = cross_z(down, -1)
     own, give = closing(h_here, v_next)
     shared = own + shift(give, "core", 1) + from_below + from_above
 
@@ -291,16 +303,16 @@
     ).reshape(nvec, wide)
 
     low, high = block[: nvec // 2], block[nvec // 2 :]
-    below_low = ring_shift(low, 1)
-    above_high = ring_shift(high, -1)
-    below_high = ring_shift(high, 1)
-    above_low = ring_shift(low, -1)
-    far_low = ring_shift(below_low, 1)
-    far_high = ring_shift(above_high, -1)
+    below_low = ring_shift(low, 1, 0)
+    above_high = ring_shift(high, -1, 0)
+    below_high = ring_shift(high, 1, 0)
+    above_low = ring_shift(low, -1, 0)
+    far_low = ring_shift(below_low, 1, 1)
+    far_high = ring_shift(above_high, -1, 1)
     other = shift(block, "core", 1)
     near = [below_low, below_high, above_low, above_high]
     other_near = [shift(value, "core", 1) for value in near]
-    whole = place_near([block, *near], [other, *other_near], nvec)
+    whole = place_near([block, *other_near], [other, *near], nvec)
     far = [far_low, far_high]
     return place_far(far, [shift(value, "core", 1) for value in far], whole)
 

time: 86.7 us -> 87.2 us (level)
  starting transfers between devices: 32.8 us -> 17.6 us
  waiting for transfers between devices: 7.83 us -> 18.9 us
  blocking collectives: 29.7 us -> 34.3 us
    ppermute x15 -> x11, starting transfers between devices: 26 us -> 3.55 us  [shift(): lax.ppermute(value, axis, [(i, (i + step) % size) for i in range(size)])]
    ppermute x6, waiting for transfers between devices: 0.31 us -> 10.1 us  [ring_shift(): return lax.ppermute(value, AXES, pairs)]
    ppermute x0 -> x4, waiting for transfers between devices: none -> 8.85 us  [cross_z(): return lax.ppermute(value, AXES, pairs)]
    ppermute x15 -> x11, waiting for transfers between devices: 7.52 us -> 0.03 us  [shift(): lax.ppermute(value, axis, [(i, (i + step) % size) for i in range(size)])]
    ppermute x0 -> x4, starting transfers between devices: none -> 7.48 us  [cross_z(): return lax.ppermute(value, AXES, pairs)]
    all_to_all x1, blocking collectives: 13.8 us -> 17.3 us  [body(): lax.all_to_all(copies, AXES, 0, 0, tiled=True, axis_index_groups=plane_gr...]
    all_to_all x1, blocking collectives: 15.9 us -> 17 us  [body(): parts = lax.all_to_all(parts, PLANE, 0, 0, tiled=True)]
  transfers between devices with their start and end apart: 21 -> 21, of which waited for: 4 -> 9; matrix products, arithmetic and copies ran while one was open for 0% -> 0% of each run, Pallas kernels for 11% -> 11%
where the time goes in v4:
time: 87.2 us; the launch traced here: 87 us
  blocking collectives  34.3 us (39%)
  waiting for transfers between devices  18.9 us (22%)
  starting transfers between devices  17.6 us (20%)
  Pallas kernels  14.9 us (17%)
    all_to_all x1, blocking collectives, body(): lax.all_to_all(copies, AXES, 0, 0, tiled=True, axis_index_groups=plane_gr...  17.3 us
    all_to_all x1, blocking collectives, body(): parts = lax.all_to_all(parts, PLANE, 0, 0, tiled=True)  17 us
    ppermute x6, waiting for transfers between devices, ring_shift(): return lax.ppermute(value, AXES, pairs)  10.1 us
    ppermute x4, waiting for transfers between devices, cross_z(): return lax.ppermute(value, AXES, pairs)  8.85 us
    ppermute x4, starting transfers between devices, cross_z(): return lax.ppermute(value, AXES, pairs)  7.48 us
    ppermute x6, starting transfers between devices, ring_shift(): return lax.ppermute(value, AXES, pairs)  6.55 us
    pallas_call x1, Pallas kernels, opening(): kernel_call(kernel, h, v, [HBM, HBM], [slab], [block, total, sems])  4.45 us
    ppermute x11, starting transfers between devices, shift(): lax.ppermute(value, axis, [(i, (i + step) % size) for i in range(size)])  3.55 us
  transfers between devices with their start and end apart: 21, of which 9 were waited for; matrix products, arithmetic and copies ran while one was open for 0% of the time, Pallas kernels for 11%

profile of v4, /device:TPU:1, one launch (start us, length us, event | category | flops | bytes accessed | tf_op | source)
XLA Modules:
  0.0 87.0 jit_solution(11867228374798499850)
XLA Ops:
  0.0 0.0 copy-start
  0.0 4.5 %shard_map.37 = (f32[128,512]{1,0:T(8,128)S(1)}, f32[128,512]{1,0:T(8,128)S(1)}, bf16[6000,512]{1,0:T(8,128)(2,1)S(1)}) custom-call(bf16[6000,512]{1,0:T(8,128)(2,1)} %bitcast.10, bf16[6000,1024]{1,0:T(8,128)(2,1)} %v.5), custom_call_target="tpu_custom_call" | custom-call | flops 1572864000 | bytes 3072000 | tf_op jit(solution)/shard_map/pallas_call | solution.py:176
  4.5 1.5 %collective-permute-start.2 = (f32[128,512]{1,0:T(8,128)S(1)}, f32[128,512]{1,0:T(8,128)S(1)}, u32[]{:S(2)}, u32[]{:S(2)}) collective-permute-start(f32[128,512]{1,0:T(8,128)S(1)} %get-tuple-element.24), channel_id=1, source_target_pairs={{0,1},{1,0},{2,3},{3,2},{4,5},{5,4},{6,7},{7,6},{8,9},{9,8},{10,11... | collective-permute-start | bytes 786440 | tf_op jit(solution)/shard_map/ppermute | solution.py:26
  5.9 3.3 %shard_map.38 = (f32[128,512]{1,0:T(8,128)S(1)}, f32[128,512]{1,0:T(8,128)S(1)}, bf16[6000,256]{1,0:T(8,128)(2,1)S(1)}) custom-call(bf16[6000,512]{1,0:T(8,128)(2,1)S(1)} %get-tuple-element.16.h_here, bf16[6000,1024]{1,0:T(8,128)(2,1)} %v.5), custom_call_target="tpu_custom_call" | custom-call | flops 1572864000 | bytes 3072000 | tf_op jit(solution)/shard_map/pallas_call | solution.py:181
  9.3 0.1 collective-permute-start.1
  9.4 2.4 %shard_map.39 = (f32[128,512]{1,0:T(8,128)S(1)}, f32[128,512]{1,0:T(8,128)S(1)}, bf16[6000,256]{1,0:T(8,128)(2,1)S(1)}) custom-call(bf16[6000,512]{1,0:T(8,128)(2,1)S(1)} %get-tuple-element.16.h_here, bf16[6000,256]{1,0:T(8,128)(2,1)S(1)} %get-tuple-element.17.v_here, bf16[6000,1024]{1,0:T(8,128)(2,1)} %v.5), custom_call_target="tpu_custom_call" | custom-call | flops 1572864000 | bytes 3072000 | tf_op jit(solution)/shard_map/pallas_call | solution.py:186
  11.7 0.6 collective-permute-start.5
  12.3 0.0 collective-permute-done.2
  12.4 1.7 %collective-permute-start.3 = (f32[64,512]{1,0:T(8,128)S(1)}, f32[64,512]{1,0:T(8,128)S(1)}, u32[]{:S(2)}, u32[]{:S(2)}) collective-permute-start(f32[64,512]{1,0:T(8,128)S(1)} %get-tuple-element.31), channel_id=1, source_target_pairs={{0,5},{1,4},{4,9},{5,8},{8,13},{9,12},{12,1},{13,0},{2,7},{3,6},{6... | collective-permute-start | bytes 393224 | tf_op jit(solution)/shard_map/ppermute | solution.py:36
  14.1 1.9 %shard_map.40 = (f32[128,512]{1,0:T(8,128)S(1)}, f32[128,512]{1,0:T(8,128)S(1)}) custom-call(bf16[6000,512]{1,0:T(8,128)(2,1)S(1)} %get-tuple-element.16.h_here, bf16[6000,256]{1,0:T(8,128)(2,1)S(1)} %get-tuple-element.18.v_here), custom_call_target="tpu_custom_call" | custom-call | flops 1572864000 | bytes 3072000 | tf_op jit(solution)/shard_map/pallas_call | solution.py:190
  16.0 0.6 collective-permute-start
  16.5 2.1 %collective-permute-start.6 = (f32[64,512]{1,0:T(8,128)S(1)}, f32[64,512]{1,0:T(8,128)S(1)}, u32[]{:S(2)}, u32[]{:S(2)}) collective-permute-start(f32[64,512]{1,0:T(8,128)S(1)} %get-tuple-element.32), channel_id=1, source_target_pairs={{0,13},{1,12},{4,1},{5,0},{8,5},{9,4},{12,9},{13,8},{2,15},{3,14},... | collective-permute-start | bytes 393224 | tf_op jit(solution)/shard_map/ppermute | solution.py:36
  18.7 0.0 collective-permute-done.1
  18.7 0.0 collective-permute-done.5
  18.8 1.4 %collective-permute-done.3 = f32[64,512]{1,0:T(8,128)S(1)} collective-permute-done((f32[64,512]{1,0:T(8,128)S(1)}, f32[64,512]{1,0:T(8,128)S(1)}, u32[]{:S(2)}, u32[]{:S(2)}) %collective-permute-start.3) | collective-permute-done | bytes 131104 | tf_op jit(solution)/shard_map/ppermute | solution.py:36
  20.2 0.1 collective-permute-start.4
  20.3 1.6 %collective-permute-done.6 = f32[64,512]{1,0:T(8,128)S(1)} collective-permute-done((f32[64,512]{1,0:T(8,128)S(1)}, f32[64,512]{1,0:T(8,128)S(1)}, u32[]{:S(2)}, u32[]{:S(2)}) %collective-permute-start.6) | collective-permute-done | bytes 131104 | tf_op jit(solution)/shard_map/ppermute | solution.py:36
  22.0 3.5 %collective-permute-start.7 = (f32[128,512]{1,0:T(8,128)S(1)}, f32[128,512]{1,0:T(8,128)S(1)}, u32[]{:S(2)}, u32[]{:S(2)}) collective-permute-start(f32[128,512]{1,0:T(8,128)S(1)} %pad_maximum_fusion.1), channel_id=1, source_target_pairs={{0,13},{1,12},{4,1},{5,0},{8,5},{9,4},{12,9},{13,8},{2,15},{3,14},... | collective-permute-start | bytes 786440 | tf_op jit(solution)/shard_map/ppermute | solution.py:36
  25.5 0.0 collective-permute-done
  25.5 4.3 %collective-permute-done.4 = f32[128,512]{1,0:T(8,128)S(1)} collective-permute-done((f32[128,512]{1,0:T(8,128)S(1)}, f32[128,512]{1,0:T(8,128)S(1)}, u32[]{:S(2)}, u32[]{:S(2)}) %collective-permute-start.4) | collective-permute-done | bytes 262176 | tf_op jit(solution)/shard_map/ppermute | solution.py:36
  29.8 1.6 %collective-permute-done.7 = f32[128,512]{1,0:T(8,128)S(1)} collective-permute-done((f32[128,512]{1,0:T(8,128)S(1)}, f32[128,512]{1,0:T(8,128)S(1)}, u32[]{:S(2)}, u32[]{:S(2)}) %collective-permute-start.7) | collective-permute-done | bytes 262176 | tf_op jit(solution)/shard_map/ppermute | solution.py:36
  31.4 0.0 copy-done
  31.4 0.6 convolution_bitcast_fusion
  32.0 0.2 copy.5
  32.2 17.0 %all_to_all.10 = f32[16,64,128]{2,1,0:T(8,128)S(1)} all-to-all(f32[16,64,128]{2,1,0:T(8,128)S(1)} %bitcast.11), channel_id=1, replica_groups=mesh['y'=4,'xh'=2,'z'=4,'xl'=2,'core'=2] {'y','xh','xl'}, dimensions={0} | all-to-all | bytes 1048576 | tf_op jit(solution)/shard_map/all_to_all | solution.py:298
  49.3 17.3 %all_to_all.11 = f32[16,64,128]{2,1,0:T(8,128)S(1)} all-to-all(f32[16,64,128]{2,1,0:T(8,128)S(1)} %broadcast_in_dim.3), channel_id=1, replica_groups={{0,2,16,18,32,34,48,50,64,66,80,82,96,98,112,114},{4,6,20,22,36,38,52,5..., dimensions={0} | all-to-all | bytes 1048576 | tf_op jit(solution)/shard_map/all_to_all | solution.py:301
  66.7 0.1 collective-permute-start.17
  66.7 1.0 %collective-permute-start.8 = (f32[512,128]{1,0:T(8,128)S(1)}, f32[512,128]{1,0:T(8,128)S(1)}, u32[]{:S(2)}, u32[]{:S(2)}) collective-permute-start(f32[512,128]{1,0:T(8,128)S(1)} %bitcast.15), channel_id=1, source_target_pairs={{0,5},{1,32},{4,9},{5,36},{8,13},{9,40},{12,1},{13,44},{2,7},{3,34... | collective-permute-start | bytes 786440 | tf_op jit(solution)/shard_map/ppermute | solution.py:46
  67.7 0.8 collective-permute-start.15
  68.5 2.9 %collective-permute-start.10 = (f32[512,128]{1,0:T(8,128)S(1)}, f32[512,128]{1,0:T(8,128)S(1)}, u32[]{:S(2)}, u32[]{:S(2)}) collective-permute-start(f32[512,128]{1,0:T(8,128)S(1)} %bitcast.13), channel_id=1, source_target_pairs={{0,13},{1,96},{4,1},{5,100},{8,5},{9,104},{12,9},{13,108},{2,15},{... | collective-permute-start | bytes 786440 | tf_op jit(solution)/shard_map/ppermute | solution.py:46
  71.4 0.0 collective-permute-start.20
  71.4 1.4 %collective-permute-done.17.refs_8_ = f32[512,128]{1,0:T(8,128)S(1)} collective-permute-done((f32[512,128]{1,0:T(8,128)S(1)}, f32[512,128]{1,0:T(8,128)S(1)}, u32[]{:S(2)}, u32[]{:S(2)}) %collective-permute-start.17) | collective-permute-done | bytes 262176 | tf_op jit(solution)/shard_map/ppermute | solution.py:46
  72.8 0.0 collective-permute-start.18
  72.8 1.3 %collective-permute-done.8.refs_6_ = f32[512,128]{1,0:T(8,128)S(1)} collective-permute-done((f32[512,128]{1,0:T(8,128)S(1)}, f32[512,128]{1,0:T(8,128)S(1)}, u32[]{:S(2)}, u32[]{:S(2)}) %collective-permute-start.8) | collective-permute-done | bytes 262176 | tf_op jit(solution)/shard_map/ppermute | solution.py:46
  74.1 0.0 collective-permute-start.14
  74.1 2.5 %collective-permute-done.15.refs_7_ = f32[512,128]{1,0:T(8,128)S(1)} collective-permute-done((f32[512,128]{1,0:T(8,128)S(1)}, f32[512,128]{1,0:T(8,128)S(1)}, u32[]{:S(2)}, u32[]{:S(2)}) %collective-permute-start.15) | collective-permute-done | bytes 262176 | tf_op jit(solution)/shard_map/ppermute | solution.py:46
  76.6 1.7 %collective-permute-start.9 = (f32[512,128]{1,0:T(8,128)S(1)}, f32[512,128]{1,0:T(8,128)S(1)}, u32[]{:S(2)}, u32[]{:S(2)}) collective-permute-start(f32[512,128]{1,0:T(8,128)S(1)} %collective-permute-done.8.refs_6_), channel_id=1, source_target_pairs={{1,4},{0,33},{5,8},{4,37},{9,12},{8,41},{13,0},{12,45},{3,6},{2,35... | collective-permute-start | bytes 786440 | tf_op jit(solution)/shard_map/ppermute | solution.py:46
  78.3 0.0 collective-permute-done.10.refs_9_
  78.3 0.1 collective-permute-start.11
  78.4 0.0 collective-permute-done.18.refs_3_
  78.4 0.0 collective-permute-start.16
  78.4 0.0 collective-permute-done.14.refs_1_
  78.4 0.5 collective-permute-start.19
  78.9 4.7 %collective-permute-done.9.refs_0_ = f32[512,128]{1,0:T(8,128)S(1)} collective-permute-done((f32[512,128]{1,0:T(8,128)S(1)}, f32[512,128]{1,0:T(8,128)S(1)}, u32[]{:S(2)}, u32[]{:S(2)}) %collective-permute-start.9) | collective-permute-done | bytes 262176 | tf_op jit(solution)/shard_map/ppermute | solution.py:46
  83.6 0.3 collective-permute-start.12
  83.9 0.2 collective-permute-done.11.refs_1_
  84.1 0.1 collective-permute-start.13
  84.1 0.0 collective-permute-done.16.refs_2_
  84.1 0.0 collective-permute-done.19.refs_4_
  84.1 0.0 collective-permute-done.20.refs_5_
  84.2 1.8 %place_near.1.refs_4_ = f32[1024,1024]{1,0:T(8,128)} custom-call(f32[1024,128]{1,0:T(8,128)S(1)} %bitcast.9, f32[512,128]{1,0:T(8,128)S(1)} %collective-permute-done.14.refs_1_, f32[512,128]{1,0:T(8,128)S(1)} %collective-permute-done.16.refs_2_, f32[512,128]{1,0:T(8,128)S(1)} %collective-permute-done.18.refs_3_, ...), custom_call_target="tpu_custom_call" | custom-call | tf_op jit(solution)/shard_map/place_near/pallas_call | solution.py:243
  86.0 0.0 collective-permute-done.12.refs_2_
  86.0 0.0 collective-permute-done.13.refs_3_
  86.0 1.0 %place_far.1 = f32[1024,1024]{1,0:T(8,128)} custom-call(f32[512,128]{1,0:T(8,128)S(1)} %collective-permute-done.9.refs_0_, f32[512,128]{1,0:T(8,128)S(1)} %collective-permute-done.11.refs_1_, f32[512,128]{1,0:T(8,128)S(1)} %collective-permute-done.12.refs_2_, f32[512,128]{1,0:T(8,128)S(1)} %collective-permute-done.13.refs_3_, ...), custom_call_target="tpu_custom_call", output_to_operand_aliasing={{}: (4, {})} | custom-call | tf_op jit(solution)/shard_map/place_far/pallas_call | solution.py:255
  (11 shorter events, 0.4 us)
Async XLA Ops:
  0.0 31.4 %copy-start = (bf16[512,1024]{1,0:T(8,128)(2,1)S(1)}, bf16[512,1024]{1,0:T(8,128)(2,1)}, u32[]{:S(2)}) copy-start(bf16[512,1024]{1,0:T(8,128)(2,1)} %param.5) | copy-start | bytes 3145732
  4.5 7.8 %collective-permute-start.2 = (f32[128,512]{1,0:T(8,128)S(1)}, f32[128,512]{1,0:T(8,128)S(1)}, u32[]{:S(2)}, u32[]{:S(2)}) collective-permute-start(f32[128,512]{1,0:T(8,128)S(1)} %get-tuple-element.24), channel_id=1, source_target_pairs={{0,1},{1,0},{2,3},{3,2},{4,5},{5,4},{6,7},{7,6},{8,9},{9,8},{10,11... | collective-permute-start | bytes 786440 | tf_op jit(solution)/shard_map/ppermute | solution.py:26
  9.3 9.4 %collective-permute-start.1 = (f32[128,512]{1,0:T(8,128)S(1)}, f32[128,512]{1,0:T(8,128)S(1)}, u32[]{:S(2)}, u32[]{:S(2)}) collective-permute-start(f32[128,512]{1,0:T(8,128)S(1)} %get-tuple-element.22), channel_id=1, source_target_pairs={{0,1},{1,0},{2,3},{3,2},{4,5},{5,4},{6,7},{7,6},{8,9},{9,8},{10,11... | collective-permute-start | bytes 786440 | tf_op jit(solution)/shard_map/ppermute | solution.py:26
  11.7 7.0 %collective-permute-start.5 = (f32[128,512]{1,0:T(8,128)S(1)}, f32[128,512]{1,0:T(8,128)S(1)}, u32[]{:S(2)}, u32[]{:S(2)}) collective-permute-start(f32[128,512]{1,0:T(8,128)S(1)} %get-tuple-element.26), channel_id=1, source_target_pairs={{0,1},{1,0},{2,3},{3,2},{4,5},{5,4},{6,7},{7,6},{8,9},{9,8},{10,11... | collective-permute-start | bytes 786440 | tf_op jit(solution)/shard_map/ppermute | solution.py:26
  12.4 7.8 %collective-permute-start.3 = (f32[64,512]{1,0:T(8,128)S(1)}, f32[64,512]{1,0:T(8,128)S(1)}, u32[]{:S(2)}, u32[]{:S(2)}) collective-permute-start(f32[64,512]{1,0:T(8,128)S(1)} %get-tuple-element.31), channel_id=1, source_target_pairs={{0,5},{1,4},{4,9},{5,8},{8,13},{9,12},{12,1},{13,0},{2,7},{3,6},{6... | collective-permute-start | bytes 393224 | tf_op jit(solution)/shard_map/ppermute | solution.py:36
  16.0 9.6 %collective-permute-start = (f32[128,512]{1,0:T(8,128)S(1)}, f32[128,512]{1,0:T(8,128)S(1)}, u32[]{:S(2)}, u32[]{:S(2)}) collective-permute-start(f32[128,512]{1,0:T(8,128)S(1)} %get-tuple-element.20), channel_id=1, source_target_pairs={{0,1},{1,0},{2,3},{3,2},{4,5},{5,4},{6,7},{7,6},{8,9},{9,8},{10,11... | collective-permute-start | bytes 786440 | tf_op jit(solution)/shard_map/ppermute | solution.py:26
  16.5 5.4 %collective-permute-start.6 = (f32[64,512]{1,0:T(8,128)S(1)}, f32[64,512]{1,0:T(8,128)S(1)}, u32[]{:S(2)}, u32[]{:S(2)}) collective-permute-start(f32[64,512]{1,0:T(8,128)S(1)} %get-tuple-element.32), channel_id=1, source_target_pairs={{0,13},{1,12},{4,1},{5,0},{8,5},{9,4},{12,9},{13,8},{2,15},{3,14},... | collective-permute-start | bytes 393224 | tf_op jit(solution)/shard_map/ppermute | solution.py:36
  20.2 9.6 %collective-permute-start.4 = (f32[128,512]{1,0:T(8,128)S(1)}, f32[128,512]{1,0:T(8,128)S(1)}, u32[]{:S(2)}, u32[]{:S(2)}) collective-permute-start(f32[128,512]{1,0:T(8,128)S(1)} %pad_maximum_fusion), channel_id=1, source_target_pairs={{0,5},{1,4},{4,9},{5,8},{8,13},{9,12},{12,1},{13,0},{2,7},{3,6},{6... | collective-permute-start | bytes 786440 | tf_op jit(solution)/shard_map/ppermute | solution.py:36
  22.0 9.4 %collective-permute-start.7 = (f32[128,512]{1,0:T(8,128)S(1)}, f32[128,512]{1,0:T(8,128)S(1)}, u32[]{:S(2)}, u32[]{:S(2)}) collective-permute-start(f32[128,512]{1,0:T(8,128)S(1)} %pad_maximum_fusion.1), channel_id=1, source_target_pairs={{0,13},{1,12},{4,1},{5,0},{8,5},{9,4},{12,9},{13,8},{2,15},{3,14},... | collective-permute-start | bytes 786440 | tf_op jit(solution)/shard_map/ppermute | solution.py:36
  66.7 6.2 %collective-permute-start.17 = (f32[512,128]{1,0:T(8,128)S(1)}, f32[512,128]{1,0:T(8,128)S(1)}, u32[]{:S(2)}, u32[]{:S(2)}) collective-permute-start(f32[512,128]{1,0:T(8,128)S(1)} %bitcast.14), channel_id=1, source_target_pairs={{0,13},{1,96},{4,1},{5,100},{8,5},{9,104},{12,9},{13,108},{2,15},{... | collective-permute-start | bytes 786440 | tf_op jit(solution)/shard_map/ppermute | solution.py:46
  66.7 7.4 %collective-permute-start.8 = (f32[512,128]{1,0:T(8,128)S(1)}, f32[512,128]{1,0:T(8,128)S(1)}, u32[]{:S(2)}, u32[]{:S(2)}) collective-permute-start(f32[512,128]{1,0:T(8,128)S(1)} %bitcast.15), channel_id=1, source_target_pairs={{0,5},{1,32},{4,9},{5,36},{8,13},{9,40},{12,1},{13,44},{2,7},{3,34... | collective-permute-start | bytes 786440 | tf_op jit(solution)/shard_map/ppermute | solution.py:46
  67.7 8.9 %collective-permute-start.15 = (f32[512,128]{1,0:T(8,128)S(1)}, f32[512,128]{1,0:T(8,128)S(1)}, u32[]{:S(2)}, u32[]{:S(2)}) collective-permute-start(f32[512,128]{1,0:T(8,128)S(1)} %bitcast.12), channel_id=1, source_target_pairs={{0,5},{1,32},{4,9},{5,36},{8,13},{9,40},{12,1},{13,44},{2,7},{3,34... | collective-permute-start | bytes 786440 | tf_op jit(solution)/shard_map/ppermute | solution.py:46
  68.5 9.7 %collective-permute-start.10 = (f32[512,128]{1,0:T(8,128)S(1)}, f32[512,128]{1,0:T(8,128)S(1)}, u32[]{:S(2)}, u32[]{:S(2)}) collective-permute-start(f32[512,128]{1,0:T(8,128)S(1)} %bitcast.13), channel_id=1, source_target_pairs={{0,13},{1,96},{4,1},{5,100},{8,5},{9,104},{12,9},{13,108},{2,15},{... | collective-permute-start | bytes 786440 | tf_op jit(solution)/shard_map/ppermute | solution.py:46
  71.4 12.7 %collective-permute-start.20 = (f32[1024,128]{1,0:T(8,128)S(1)}, f32[1024,128]{1,0:T(8,128)S(1)}, u32[]{:S(2)}, u32[]{:S(2)}) collective-permute-start(f32[1024,128]{1,0:T(8,128)S(1)} %bitcast.8), channel_id=1, source_target_pairs={{0,1},{1,0},{2,3},{3,2},{4,5},{5,4},{6,7},{7,6},{8,9},{9,8},{10,11... | collective-permute-start | bytes 1572872 | tf_op jit(solution)/shard_map/ppermute | solution.py:26
  72.8 5.6 %collective-permute-start.18 = (f32[512,128]{1,0:T(8,128)S(1)}, f32[512,128]{1,0:T(8,128)S(1)}, u32[]{:S(2)}, u32[]{:S(2)}) collective-permute-start(f32[512,128]{1,0:T(8,128)S(1)} %collective-permute-done.17.refs_8_), channel_id=1, source_target_pairs={{0,1},{1,0},{2,3},{3,2},{4,5},{5,4},{6,7},{7,6},{8,9},{9,8},{10,11... | collective-permute-start | bytes 786440 | tf_op jit(solution)/shard_map/ppermute | solution.py:26
  74.1 4.3 %collective-permute-start.14 = (f32[512,128]{1,0:T(8,128)S(1)}, f32[512,128]{1,0:T(8,128)S(1)}, u32[]{:S(2)}, u32[]{:S(2)}) collective-permute-start(f32[512,128]{1,0:T(8,128)S(1)} %collective-permute-done.8.refs_6_), channel_id=1, source_target_pairs={{0,1},{1,0},{2,3},{3,2},{4,5},{5,4},{6,7},{7,6},{8,9},{9,8},{10,11... | collective-permute-start | bytes 786440 | tf_op jit(solution)/shard_map/ppermute | solution.py:26
  76.6 7.0 %collective-permute-start.9 = (f32[512,128]{1,0:T(8,128)S(1)}, f32[512,128]{1,0:T(8,128)S(1)}, u32[]{:S(2)}, u32[]{:S(2)}) collective-permute-start(f32[512,128]{1,0:T(8,128)S(1)} %collective-permute-done.8.refs_6_), channel_id=1, source_target_pairs={{1,4},{0,33},{5,8},{4,37},{9,12},{8,41},{13,0},{12,45},{3,6},{2,35... | collective-permute-start | bytes 786440 | tf_op jit(solution)/shard_map/ppermute | solution.py:46
  78.3 5.8 %collective-permute-start.11 = (f32[512,128]{1,0:T(8,128)S(1)}, f32[512,128]{1,0:T(8,128)S(1)}, u32[]{:S(2)}, u32[]{:S(2)}) collective-permute-start(f32[512,128]{1,0:T(8,128)S(1)} %collective-permute-done.10.refs_9_), channel_id=1, source_target_pairs={{1,12},{0,97},{5,0},{4,101},{9,4},{8,105},{13,8},{12,109},{3,14},{... | collective-permute-start | bytes 786440 | tf_op jit(solution)/shard_map/ppermute | solution.py:46
  78.4 5.7 %collective-permute-start.16 = (f32[512,128]{1,0:T(8,128)S(1)}, f32[512,128]{1,0:T(8,128)S(1)}, u32[]{:S(2)}, u32[]{:S(2)}) collective-permute-start(f32[512,128]{1,0:T(8,128)S(1)} %collective-permute-done.15.refs_7_), channel_id=1, source_target_pairs={{0,1},{1,0},{2,3},{3,2},{4,5},{5,4},{6,7},{7,6},{8,9},{9,8},{10,11... | collective-permute-start | bytes 786440 | tf_op jit(solution)/shard_map/ppermute | solution.py:26
  78.4 5.7 %collective-permute-start.19 = (f32[512,128]{1,0:T(8,128)S(1)}, f32[512,128]{1,0:T(8,128)S(1)}, u32[]{:S(2)}, u32[]{:S(2)}) collective-permute-start(f32[512,128]{1,0:T(8,128)S(1)} %collective-permute-done.10.refs_9_), channel_id=1, source_target_pairs={{0,1},{1,0},{2,3},{3,2},{4,5},{5,4},{6,7},{7,6},{8,9},{9,8},{10,11... | collective-permute-start | bytes 786440 | tf_op jit(solution)/shard_map/ppermute | solution.py:26
  83.6 2.4 %collective-permute-start.12 = (f32[512,128]{1,0:T(8,128)S(1)}, f32[512,128]{1,0:T(8,128)S(1)}, u32[]{:S(2)}, u32[]{:S(2)}) collective-permute-start(f32[512,128]{1,0:T(8,128)S(1)} %collective-permute-done.9.refs_0_), channel_id=1, source_target_pairs={{0,1},{1,0},{2,3},{3,2},{4,5},{5,4},{6,7},{7,6},{8,9},{9,8},{10,11... | collective-permute-start | bytes 786440 | tf_op jit(solution)/shard_map/ppermute | solution.py:26
  84.1 1.9 %collective-permute-start.13 = (f32[512,128]{1,0:T(8,128)S(1)}, f32[512,128]{1,0:T(8,128)S(1)}, u32[]{:S(2)}, u32[]{:S(2)}) collective-permute-start(f32[512,128]{1,0:T(8,128)S(1)} %collective-permute-done.11.refs_1_), channel_id=1, source_target_pairs={{0,1},{1,0},{2,3},{3,2},{4,5},{5,4},{6,7},{7,6},{8,9},{9,8},{10,11... | collective-permute-start | bytes 786440 | tf_op jit(solution)/shard_map/ppermute | solution.py:26

commit v5 on v3

--- a/solution.py
+++ b/solution.py
@@ -117,25 +117,19 @@
         copy.wait()
 
 
-def third_kernel(following, h_here, v_here, v, keep, give, v_next, total, sem):
-    theirs = fetch(v, following, v_next, sem, 0)
-    for copy in theirs:
+def third_kernel(h_here, v_here, keep, give, total):
+    total[...] = multiply(v_here[...], h_here[...])
+    emit(total, keep, give)
+
+
+def closing_kernel(ahead, h_here, v, keep, give, v_here, total, sem):
+    spans = cuts(v.shape[0])
+    ours = fetch(v, ahead, v_here, sem, 0)
+    for copy in ours:
         copy.start()
-    step = v.shape[0] // 3
-    total[...] = jnp.zeros_like(total)
-
-    @pl.loop(0, 3)
-    def _(i):
-        rows = pl.ds(pl.multiple_of(i * step, 16), step)
-        total[...] += multiply(v_here[rows, :], h_here[rows, :])
-
-    emit(total, keep, give)
-    for copy in theirs:
+    for (start, size), copy in zip(spans, ours):
         copy.wait()
-
-
-def closing_kernel(h_here, v_here, keep, give, total):
-    total[...] = multiply(v_here[...], h_here[...])
+        accumulate(total, v_here, h_here, start, size)
     emit(total, keep, give)
 
 
@@ -170,31 +164,22 @@
         call = kernel_call(kernel, h, v, [VMEM, HBM], [block], [block, total, sems])
         return call(resident(h_here), v)
 
-    def third(following, h_here, v_here):
-        kernel = functools.partial(third_kernel, following)
-        call = kernel_call(kernel, h, v, [VMEM, VMEM, HBM], [block], [total, sems])
-        return call(resident(h_here), resident(v_here), v)
-
-    def closing(h_here, v_here):
-        call = kernel_call(closing_kernel, h, v, [VMEM, VMEM], [], [total])
+    def third(h_here, v_here):
+        call = kernel_call(third_kernel, h, v, [VMEM, VMEM], [], [total])
         return call(resident(h_here), resident(v_here))
 
+    def closing(ahead, h_here):
+        kernel = functools.partial(closing_kernel, ahead)
+        call = kernel_call(kernel, h, v, [VMEM, HBM], [], [block, total, sems])
+        return call(resident(h_here), v)
+
     return opening, second, third, closing
 
 
-def near_kernel(*refs):
-    own, other, out, sem = refs[:5], refs[5:10], refs[10], refs[11]
-    spots = ((0, None), (3, 0), (3, 1), (1, 0), (1, 1))
-
-    def spread(blocks):
-        return [(ref, step, part) for ref, (step, part) in zip(blocks, spots)]
-
-    write(spread(own), spread(other), out, sem)
-
-
-def far_kernel(*refs):
-    own, other, out, sem = refs[:2], refs[2:4], refs[5], refs[6]
-    write([(own[0], 2, 0), (own[1], 2, 1)], [(other[0], 2, 0), (other[1], 2, 1)], out, sem)
+def place_kernel(own_spots, other_spots, count, *refs):
+    own = list(zip(refs[: len(own_spots)], own_spots))
+    other = list(zip(refs[len(own_spots) : len(own_spots) + len(other_spots)], other_spots))
+    write([(ref, *spot) for ref, spot in own], [(ref, *spot) for ref, spot in other], refs[count], refs[count + 1])
 
 
 def write(own, other, out, sem):
@@ -203,11 +188,10 @@
     def run(first, second):
         made = []
         for ref, step, part in first:
-            rows, part = ref.shape[0], part or 0
+            rows = ref.shape[0]
             column = pl.multiple_of(lax.rem(z + step, 4) * 256, 256)
             made.append((ref, out.at[pl.ds(part * rows, rows), pl.ds(column, 128)]))
         for ref, step, part in second:
-            part = part or 0
             row = pl.multiple_of(lax.rem(y + step, 4) * 256, 256)
             for k in range(ref.shape[0] // 256):
                 column = (part * 2 + k) * 256 + 128
@@ -227,29 +211,22 @@
         run(other, own)
 
 
-def place_near(own, other, nvec):
+def place(own, other, whole, nvec):
+    blocks = [block for block, *_ in (*own, *other)]
+    earlier = [] if whole is None else [whole]
+    count = len(blocks) + len(earlier)
+    kernel = functools.partial(
+        place_kernel, [tuple(spot) for _, *spot in own], [tuple(spot) for _, *spot in other], count
+    )
     return pl.pallas_call(
-        near_kernel,
-        in_specs=[ANY] * 10,
+        kernel,
+        in_specs=[ANY] * count,
         out_specs=ANY,
         out_shape=jax.ShapeDtypeStruct((nvec, nvec), F32),
-        scratch_shapes=[pltpu.SemaphoreType.DMA((17,))],
+        input_output_aliases={len(blocks): 0} if earlier else {},
+        scratch_shapes=[pltpu.SemaphoreType.DMA((24,))],
         compiler_params=pltpu.CompilerParams(vmem_limit_bytes=2**20),
-        name="place_near",
-    )(*own, *other)
-
-
-def place_far(own, other, whole):
-    return pl.pallas_call(
-        far_kernel,
-        in_specs=[ANY] * 5,
-        out_specs=ANY,
-        out_shape=jax.ShapeDtypeStruct(whole.shape, F32),
-        input_output_aliases={4: 0},
-        scratch_shapes=[pltpu.SemaphoreType.DMA((6,))],
-        compiler_params=pltpu.CompilerParams(vmem_limit_bytes=2**20),
-        name="place_far",
-    )(*own, *other, whole)
+    )(*blocks, *earlier)
 
 
 def body(h_slab, vectors, left_rows):
@@ -265,14 +242,14 @@
     far = far + other_far
     from_below = shift(far[:half], "z", 1)
     from_above = shift(far[half:], "z", -1)
-    down, give, v_next = third(0, h_here, v_next)
+    down, give = third(h_here, v_next)
     other_down = shift(give, "core", 1)
     up, down = up + other_up, down + other_down
     up = jnp.concatenate([up[:half] + from_below, up[half:]])
     down = jnp.concatenate([down[:half], down[half:] + from_above])
     from_below = shift(up, "z", 1)
     from_above = shift(down, "z", -1)
-    own, give = closing(h_here, v_next)
+    own, give = closing(0, h_here)
     shared = own + shift(give, "core", 1) + from_below + from_above
 
     local_part = lax.dot_general(
@@ -298,11 +275,17 @@
     far_low = ring_shift(below_low, 1)
     far_high = ring_shift(above_high, -1)
     other = shift(block, "core", 1)
-    near = [below_low, below_high, above_low, above_high]
-    other_near = [shift(value, "core", 1) for value in near]
-    whole = place_near([block, *near], [other, *other_near], nvec)
-    far = [far_low, far_high]
-    return place_far(far, [shift(value, "core", 1) for value in far], whole)
+    other_below_low = shift(below_low, "core", 1)
+    other_above_high = shift(above_high, "core", 1)
+    other_below_high = shift(below_high, "core", 1)
+    other_above_low = shift(above_low, "core", 1)
+    whole = place([(block, 0, 0), (below_low, 3, 0), (above_high, 1, 1)], [(other, 0, 0)], None, nvec)
+    other_far_low = shift(far_low, "core", 1)
+    other_far_high = shift(far_high, "core", 1)
+    own = [(below_high, 3, 1), (above_low, 1, 0)]
+    others = [(other_below_low, 3, 0), (other_above_high, 1, 1), (other_below_high, 3, 1), (other_above_low, 1, 0)]
+    whole = place(own, others, whole, nvec)
+    return place([(far_low, 2, 0), (far_high, 2, 1)], [(other_far_low, 2, 0), (other_far_high, 2, 1)], whole, nvec)
 
 
 def solution(mesh):

time: 86.7 us -> 88.4 us (1.020)
  starting transfers between devices: 32.8 us -> 24 us
  waiting for transfers between devices: 7.83 us -> 15.7 us
  Pallas kernels: 14.8 us -> 16.9 us
    ppermute x15, starting transfers between devices: 26 us -> 18.1 us  [shift(): lax.ppermute(value, axis, [(i, (i + step) % size) for i in range(size)])]
    ppermute x6, waiting for transfers between devices: 0.31 us -> 4.38 us  [ring_shift(): return lax.ppermute(value, AXES, pairs)]
    ppermute x15, waiting for transfers between devices: 7.52 us -> 11.3 us  [shift(): lax.ppermute(value, axis, [(i, (i + step) % size) for i in range(size)])]
    pallas_call x4 -> x5, Pallas kernels: 7.08 us -> 9.1 us  [the longest x3 3.93 us: place(): pl.pallas_call(kernel, in_specs=[ANY] * count, out_specs=ANY, out_shape=j...]
    ppermute x6, starting transfers between devices: 6.89 us -> 5.99 us  [ring_shift(): return lax.ppermute(value, AXES, pairs)]
  transfers between devices with their start and end apart: 21 -> 21, of which waited for: 4 -> 5; matrix products, arithmetic and copies ran while one was open for 0% -> 0% of each run, Pallas kernels for 11% -> 13%
where the time goes in v5:
time: 88.4 us; the launch traced here: 88.2 us
  blocking collectives  30.2 us (34%)
  starting transfers between devices  24 us (27%)
  Pallas kernels  16.9 us (19%)
  waiting for transfers between devices  15.7 us (18%)
    ppermute x15, starting transfers between devices, shift(): lax.ppermute(value, axis, [(i, (i + step) % size) for i in range(size)])  18.1 us
    all_to_all x1, blocking collectives, body(): parts = lax.all_to_all(parts, PLANE, 0, 0, tiled=True)  16.1 us
    all_to_all x1, blocking collectives, body(): lax.all_to_all(copies, AXES, 0, 0, tiled=True, axis_index_groups=plane_gr...  14.1 us
    ppermute x15, waiting for transfers between devices, shift(): lax.ppermute(value, axis, [(i, (i + step) % size) for i in range(size)])  11.3 us
    ppermute x6, starting transfers between devices, ring_shift(): return lax.ppermute(value, AXES, pairs)  5.99 us
    pallas_call x1, Pallas kernels, opening(): kernel_call(kernel, h, v, [HBM, HBM], [slab], [block, total, sems])  4.45 us
    ppermute x6, waiting for transfers between devices, ring_shift(): return lax.ppermute(value, AXES, pairs)  4.38 us
    pallas_call x3, Pallas kernels, place(): pl.pallas_call(kernel, in_specs=[ANY] * count, out_specs=ANY, out_shape=j...  3.93 us
  transfers between devices with their start and end apart: 21, of which 5 were waited for; matrix products, arithmetic and copies ran while one was open for 0% of the time, Pallas kernels for 13%

profile of v5, /device:TPU:1, one launch (start us, length us, event | category | flops | bytes accessed | tf_op | source)
XLA Modules:
  0.0 88.2 jit_solution(10750270334400234890)
XLA Ops:
  0.0 0.0 copy-start
  0.0 4.5 %shard_map.37 = (f32[128,512]{1,0:T(8,128)S(1)}, f32[128,512]{1,0:T(8,128)S(1)}, bf16[6000,512]{1,0:T(8,128)(2,1)S(1)}) custom-call(bf16[6000,512]{1,0:T(8,128)(2,1)} %bitcast.10, bf16[6000,1024]{1,0:T(8,128)(2,1)} %v.5), custom_call_target="tpu_custom_call" | custom-call | flops 1572864000 | bytes 3072000 | tf_op jit(solution)/shard_map/pallas_call | solution.py:160
  4.5 1.5 %collective-permute-start.2 = (f32[128,512]{1,0:T(8,128)S(1)}, f32[128,512]{1,0:T(8,128)S(1)}, u32[]{:S(2)}, u32[]{:S(2)}) collective-permute-start(f32[128,512]{1,0:T(8,128)S(1)} %get-tuple-element.21), channel_id=1, source_target_pairs={{0,1},{1,0},{2,3},{3,2},{4,5},{5,4},{6,7},{7,6},{8,9},{9,8},{10,11... | collective-permute-start | bytes 786440 | tf_op jit(solution)/shard_map/ppermute | solution.py:26
  5.9 3.3 %shard_map.39 = (f32[128,512]{1,0:T(8,128)S(1)}, f32[128,512]{1,0:T(8,128)S(1)}, bf16[6000,256]{1,0:T(8,128)(2,1)S(1)}) custom-call(bf16[6000,512]{1,0:T(8,128)(2,1)S(1)} %get-tuple-element.15.h_here, bf16[6000,1024]{1,0:T(8,128)(2,1)} %v.5), custom_call_target="tpu_custom_call" | custom-call | flops 1572864000 | bytes 3072000 | tf_op jit(solution)/shard_map/pallas_call | solution.py:165
  9.3 1.9 %shard_map.40 = (f32[128,512]{1,0:T(8,128)S(1)}, f32[128,512]{1,0:T(8,128)S(1)}) custom-call(bf16[6000,512]{1,0:T(8,128)(2,1)S(1)} %get-tuple-element.15.h_here, bf16[6000,256]{1,0:T(8,128)(2,1)S(1)} %get-tuple-element.22.v_here), custom_call_target="tpu_custom_call" | custom-call | flops 1572864000 | bytes 3072000 | tf_op jit(solution)/shard_map/pallas_call | solution.py:169
  11.1 0.1 collective-permute-start.5
  11.2 0.5 collective-permute-start.1
  11.7 0.0 collective-permute-done.2
  11.8 3.9 %collective-permute-start.6 = (f32[64,512]{1,0:T(8,128)S(1)}, f32[64,512]{1,0:T(8,128)S(1)}, u32[]{:S(2)}, u32[]{:S(2)}) collective-permute-start(f32[64,512]{1,0:T(8,128)S(1)} %get-tuple-element.30), channel_id=1, source_target_pairs={{0,12},{4,0},{8,4},{12,8},{1,13},{5,1},{9,5},{13,9},{2,14},{6,2},{... | collective-permute-start | bytes 393224 | tf_op jit(solution)/shard_map/ppermute | solution.py:26
  15.7 3.3 %shard_map.38 = (f32[128,512]{1,0:T(8,128)S(1)}, f32[128,512]{1,0:T(8,128)S(1)}) custom-call(bf16[6000,512]{1,0:T(8,128)(2,1)S(1)} %get-tuple-element.15.h_here, bf16[6000,1024]{1,0:T(8,128)(2,1)} %v.5), custom_call_target="tpu_custom_call" | custom-call | flops 1572864000 | bytes 3072000 | tf_op jit(solution)/shard_map/pallas_call | solution.py:174
  19.0 0.4 collective-permute-start
  19.5 0.0 collective-permute-start.3
  19.5 0.0 collective-permute-done.5
  19.5 0.0 collective-permute-done.1
  19.6 0.0 collective-permute-done.6
  19.7 2.7 %collective-permute-start.7 = (f32[128,512]{1,0:T(8,128)S(1)}, f32[128,512]{1,0:T(8,128)S(1)}, u32[]{:S(2)}, u32[]{:S(2)}) collective-permute-start(f32[128,512]{1,0:T(8,128)S(1)} %pad_maximum_fusion.1), channel_id=1, source_target_pairs={{0,12},{4,0},{8,4},{12,8},{1,13},{5,1},{9,5},{13,9},{2,14},{6,2},{... | collective-permute-start | bytes 786440 | tf_op jit(solution)/shard_map/ppermute | solution.py:26
  22.4 3.2 %collective-permute-done.3 = f32[64,512]{1,0:T(8,128)S(1)} collective-permute-done((f32[64,512]{1,0:T(8,128)S(1)}, f32[64,512]{1,0:T(8,128)S(1)}, u32[]{:S(2)}, u32[]{:S(2)}) %collective-permute-start.3) | collective-permute-done | bytes 131104 | tf_op jit(solution)/shard_map/ppermute | solution.py:26
  25.7 0.1 collective-permute-start.4
  25.8 0.0 collective-permute-done
  25.8 1.7 %collective-permute-done.7 = f32[128,512]{1,0:T(8,128)S(1)} collective-permute-done((f32[128,512]{1,0:T(8,128)S(1)}, f32[128,512]{1,0:T(8,128)S(1)}, u32[]{:S(2)}, u32[]{:S(2)}) %collective-permute-start.7) | collective-permute-done | bytes 262176 | tf_op jit(solution)/shard_map/ppermute | solution.py:26
  27.5 6.3 %collective-permute-done.4 = f32[128,512]{1,0:T(8,128)S(1)} collective-permute-done((f32[128,512]{1,0:T(8,128)S(1)}, f32[128,512]{1,0:T(8,128)S(1)}, u32[]{:S(2)}, u32[]{:S(2)}) %collective-permute-start.4) | collective-permute-done | bytes 262176 | tf_op jit(solution)/shard_map/ppermute | solution.py:26
  33.8 0.0 copy-done
  33.8 0.6 convolution_bitcast_fusion
  34.5 0.2 copy.6
  34.7 16.1 %all_to_all.10 = f32[16,64,128]{2,1,0:T(8,128)S(1)} all-to-all(f32[16,64,128]{2,1,0:T(8,128)S(1)} %bitcast.11), channel_id=1, replica_groups=mesh['y'=4,'xh'=2,'z'=4,'xl'=2,'core'=2] {'y','xh','xl'}, dimensions={0} | all-to-all | bytes 1048576 | tf_op jit(solution)/shard_map/all_to_all | solution.py:263
  50.9 14.1 %all_to_all.11 = f32[16,64,128]{2,1,0:T(8,128)S(1)} all-to-all(f32[16,64,128]{2,1,0:T(8,128)S(1)} %broadcast_in_dim.3), channel_id=1, replica_groups={{0,2,16,18,32,34,48,50,64,66,80,82,96,98,112,114},{4,6,20,22,36,38,52,5..., dimensions={0} | all-to-all | bytes 1048576 | tf_op jit(solution)/shard_map/all_to_all | solution.py:266
  65.0 0.1 collective-permute-start.8
  65.1 2.7 %collective-permute-start.10 = (f32[512,128]{1,0:T(8,128)S(1)}, f32[512,128]{1,0:T(8,128)S(1)}, u32[]{:S(2)}, u32[]{:S(2)}) collective-permute-start(f32[512,128]{1,0:T(8,128)S(1)} %bitcast.14), channel_id=1, source_target_pairs={{0,12},{1,97},{4,0},{5,101},{8,4},{9,105},{12,8},{13,109},{2,14},{... | collective-permute-start | bytes 786440 | tf_op jit(solution)/shard_map/ppermute | solution.py:36
  67.8 0.0 collective-permute-start.14
  67.8 2.5 %collective-permute-start.20 = (f32[1024,128]{1,0:T(8,128)S(1)}, f32[1024,128]{1,0:T(8,128)S(1)}, u32[]{:S(2)}, u32[]{:S(2)}) collective-permute-start(f32[1024,128]{1,0:T(8,128)S(1)} %bitcast.8), channel_id=1, source_target_pairs={{0,1},{1,0},{2,3},{3,2},{4,5},{5,4},{6,7},{7,6},{8,9},{9,8},{10,11... | collective-permute-start | bytes 1572872 | tf_op jit(solution)/shard_map/ppermute | solution.py:26
  70.3 0.6 collective-permute-start.15
  70.8 1.0 %collective-permute-done.8.refs_1_ = f32[512,128]{1,0:T(8,128)S(1)} collective-permute-done((f32[512,128]{1,0:T(8,128)S(1)}, f32[512,128]{1,0:T(8,128)S(1)}, u32[]{:S(2)}, u32[]{:S(2)}) %collective-permute-start.8) | collective-permute-done | bytes 262176 | tf_op jit(solution)/shard_map/ppermute | solution.py:36
  71.8 2.8 %collective-permute-start.16 = (f32[512,128]{1,0:T(8,128)S(1)}, f32[512,128]{1,0:T(8,128)S(1)}, u32[]{:S(2)}, u32[]{:S(2)}) collective-permute-start(f32[512,128]{1,0:T(8,128)S(1)} %collective-permute-done.8.refs_1_), channel_id=1, source_target_pairs={{0,1},{1,0},{2,3},{3,2},{4,5},{5,4},{6,7},{7,6},{8,9},{9,8},{10,11... | collective-permute-start | bytes 786440 | tf_op jit(solution)/shard_map/ppermute | solution.py:26
  74.6 0.0 collective-permute-done.10.refs_2_
  74.6 0.0 collective-permute-start.9
  74.6 0.0 collective-permute-done.14.refs_0_
  74.6 2.7 %collective-permute-start.11 = (f32[512,128]{1,0:T(8,128)S(1)}, f32[512,128]{1,0:T(8,128)S(1)}, u32[]{:S(2)}, u32[]{:S(2)}) collective-permute-start(f32[512,128]{1,0:T(8,128)S(1)} %collective-permute-done.10.refs_2_), channel_id=1, source_target_pairs={{0,12},{1,97},{4,0},{5,101},{8,4},{9,105},{12,8},{13,109},{2,14},{... | collective-permute-start | bytes 786440 | tf_op jit(solution)/shard_map/ppermute | solution.py:36
  77.3 0.0 collective-permute-done.15.refs_1_
  77.3 0.6 collective-permute-start.17
  77.9 0.0 collective-permute-done.16.refs_2_
  77.9 0.1 collective-permute-start.18
  77.9 3.4 %collective-permute-done.9.refs_0_ = f32[512,128]{1,0:T(8,128)S(1)} collective-permute-done((f32[512,128]{1,0:T(8,128)S(1)}, f32[512,128]{1,0:T(8,128)S(1)}, u32[]{:S(2)}, u32[]{:S(2)}) %collective-permute-start.9) | collective-permute-done | bytes 262176 | tf_op jit(solution)/shard_map/ppermute | solution.py:36
  81.3 0.9 collective-permute-start.19
  82.2 0.0 collective-permute-done.11.refs_1_
  82.2 2.0 %collective-permute-start.12 = (f32[512,128]{1,0:T(8,128)S(1)}, f32[512,128]{1,0:T(8,128)S(1)}, u32[]{:S(2)}, u32[]{:S(2)}) collective-permute-start(f32[512,128]{1,0:T(8,128)S(1)} %collective-permute-done.9.refs_0_), channel_id=1, source_target_pairs={{0,1},{1,0},{2,3},{3,2},{4,5},{5,4},{6,7},{7,6},{8,9},{9,8},{10,11... | collective-permute-start | bytes 786440 | tf_op jit(solution)/shard_map/ppermute | solution.py:26
  84.2 0.0 collective-permute-done.20.refs_3_
  84.2 0.0 collective-permute-start.13
  84.2 1.3 %shard_map.41.refs_6_ = f32[1024,1024]{1,0:T(8,128)} custom-call(f32[1024,128]{1,0:T(8,128)S(1)} %bitcast.9, f32[512,128]{1,0:T(8,128)S(1)} %collective-permute-done.8.refs_1_, f32[512,128]{1,0:T(8,128)S(1)} %collective-permute-done.10.refs_2_, f32[1024,128]{1,0:T(8,128)S(1)} %collective-permute-done.20.refs_3_), custom_call_target="tpu_custom_call" | custom-call | tf_op jit(solution)/shard_map/pallas_call | solution.py:221
  85.6 0.0 collective-permute-done.17.refs_3_
  85.6 0.0 collective-permute-done.18.refs_4_
  85.6 0.0 collective-permute-done.19.refs_5_
  85.6 1.4 %shard_map.42.refs_4_ = f32[1024,1024]{1,0:T(8,128)} custom-call(f32[512,128]{1,0:T(8,128)S(1)} %collective-permute-done.14.refs_0_, f32[512,128]{1,0:T(8,128)S(1)} %collective-permute-done.15.refs_1_, f32[512,128]{1,0:T(8,128)S(1)} %collective-permute-done.16.refs_2_, ...), custom_call_target="tpu_custom_call", output_to_operand_aliasing={{}: (6, {})} | custom-call | tf_op jit(solution)/shard_map/pallas_call | solution.py:221
  87.0 0.0 collective-permute-done.12.refs_2_
  87.0 0.0 collective-permute-done.13.refs_3_
  87.0 1.2 %shard_map.43 = f32[1024,1024]{1,0:T(8,128)} custom-call(f32[512,128]{1,0:T(8,128)S(1)} %collective-permute-done.9.refs_0_, f32[512,128]{1,0:T(8,128)S(1)} %collective-permute-done.11.refs_1_, f32[512,128]{1,0:T(8,128)S(1)} %collective-permute-done.12.refs_2_, f32[512,128]{1,0:T(8,128)S(1)} %collective-permute-done.13.refs_3_, ...), custom_call_target="tpu_custom_call", output_to_operand_aliasing={{}: (4, {})} | custom-call | tf_op jit(solution)/shard_map/pallas_call | solution.py:221
  (11 shorter events, 0.4 us)
Async XLA Ops:
  0.0 33.8 %copy-start = (bf16[512,1024]{1,0:T(8,128)(2,1)S(1)}, bf16[512,1024]{1,0:T(8,128)(2,1)}, u32[]{:S(2)}) copy-start(bf16[512,1024]{1,0:T(8,128)(2,1)} %param.5) | copy-start | bytes 3145732
  4.5 7.2 %collective-permute-start.2 = (f32[128,512]{1,0:T(8,128)S(1)}, f32[128,512]{1,0:T(8,128)S(1)}, u32[]{:S(2)}, u32[]{:S(2)}) collective-permute-start(f32[128,512]{1,0:T(8,128)S(1)} %get-tuple-element.21), channel_id=1, source_target_pairs={{0,1},{1,0},{2,3},{3,2},{4,5},{5,4},{6,7},{7,6},{8,9},{9,8},{10,11... | collective-permute-start | bytes 786440 | tf_op jit(solution)/shard_map/ppermute | solution.py:26
  11.1 8.4 %collective-permute-start.5 = (f32[128,512]{1,0:T(8,128)S(1)}, f32[128,512]{1,0:T(8,128)S(1)}, u32[]{:S(2)}, u32[]{:S(2)}) collective-permute-start(f32[128,512]{1,0:T(8,128)S(1)} %get-tuple-element.24), channel_id=1, source_target_pairs={{0,1},{1,0},{2,3},{3,2},{4,5},{5,4},{6,7},{7,6},{8,9},{9,8},{10,11... | collective-permute-start | bytes 786440 | tf_op jit(solution)/shard_map/ppermute | solution.py:26
  11.2 8.3 %collective-permute-start.1 = (f32[128,512]{1,0:T(8,128)S(1)}, f32[128,512]{1,0:T(8,128)S(1)}, u32[]{:S(2)}, u32[]{:S(2)}) collective-permute-start(f32[128,512]{1,0:T(8,128)S(1)} %get-tuple-element.19), channel_id=1, source_target_pairs={{0,1},{1,0},{2,3},{3,2},{4,5},{5,4},{6,7},{7,6},{8,9},{9,8},{10,11... | collective-permute-start | bytes 786440 | tf_op jit(solution)/shard_map/ppermute | solution.py:26
  11.8 7.8 %collective-permute-start.6 = (f32[64,512]{1,0:T(8,128)S(1)}, f32[64,512]{1,0:T(8,128)S(1)}, u32[]{:S(2)}, u32[]{:S(2)}) collective-permute-start(f32[64,512]{1,0:T(8,128)S(1)} %get-tuple-element.30), channel_id=1, source_target_pairs={{0,12},{4,0},{8,4},{12,8},{1,13},{5,1},{9,5},{13,9},{2,14},{6,2},{... | collective-permute-start | bytes 393224 | tf_op jit(solution)/shard_map/ppermute | solution.py:26
  19.0 6.7 %collective-permute-start = (f32[128,512]{1,0:T(8,128)S(1)}, f32[128,512]{1,0:T(8,128)S(1)}, u32[]{:S(2)}, u32[]{:S(2)}) collective-permute-start(f32[128,512]{1,0:T(8,128)S(1)} %get-tuple-element.17), channel_id=1, source_target_pairs={{0,1},{1,0},{2,3},{3,2},{4,5},{5,4},{6,7},{7,6},{8,9},{9,8},{10,11... | collective-permute-start | bytes 786440 | tf_op jit(solution)/shard_map/ppermute | solution.py:26
  19.5 6.1 %collective-permute-start.3 = (f32[64,512]{1,0:T(8,128)S(1)}, f32[64,512]{1,0:T(8,128)S(1)}, u32[]{:S(2)}, u32[]{:S(2)}) collective-permute-start(f32[64,512]{1,0:T(8,128)S(1)} %get-tuple-element.29), channel_id=1, source_target_pairs={{0,4},{4,8},{8,12},{12,0},{1,5},{5,9},{9,13},{13,1},{2,6},{6,10},{... | collective-permute-start | bytes 393224 | tf_op jit(solution)/shard_map/ppermute | solution.py:26
  19.7 7.8 %collective-permute-start.7 = (f32[128,512]{1,0:T(8,128)S(1)}, f32[128,512]{1,0:T(8,128)S(1)}, u32[]{:S(2)}, u32[]{:S(2)}) collective-permute-start(f32[128,512]{1,0:T(8,128)S(1)} %pad_maximum_fusion.1), channel_id=1, source_target_pairs={{0,12},{4,0},{8,4},{12,8},{1,13},{5,1},{9,5},{13,9},{2,14},{6,2},{... | collective-permute-start | bytes 786440 | tf_op jit(solution)/shard_map/ppermute | solution.py:26
  25.7 8.1 %collective-permute-start.4 = (f32[128,512]{1,0:T(8,128)S(1)}, f32[128,512]{1,0:T(8,128)S(1)}, u32[]{:S(2)}, u32[]{:S(2)}) collective-permute-start(f32[128,512]{1,0:T(8,128)S(1)} %pad_maximum_fusion), channel_id=1, source_target_pairs={{0,4},{4,8},{8,12},{12,0},{1,5},{5,9},{9,13},{13,1},{2,6},{6,10},{... | collective-permute-start | bytes 786440 | tf_op jit(solution)/shard_map/ppermute | solution.py:26
  65.0 6.8 %collective-permute-start.8 = (f32[512,128]{1,0:T(8,128)S(1)}, f32[512,128]{1,0:T(8,128)S(1)}, u32[]{:S(2)}, u32[]{:S(2)}) collective-permute-start(f32[512,128]{1,0:T(8,128)S(1)} %bitcast.12), channel_id=1, source_target_pairs={{0,4},{1,33},{4,8},{5,37},{8,12},{9,41},{12,0},{13,45},{2,6},{3,35... | collective-permute-start | bytes 786440 | tf_op jit(solution)/shard_map/ppermute | solution.py:36
  65.1 9.5 %collective-permute-start.10 = (f32[512,128]{1,0:T(8,128)S(1)}, f32[512,128]{1,0:T(8,128)S(1)}, u32[]{:S(2)}, u32[]{:S(2)}) collective-permute-start(f32[512,128]{1,0:T(8,128)S(1)} %bitcast.14), channel_id=1, source_target_pairs={{0,12},{1,97},{4,0},{5,101},{8,4},{9,105},{12,8},{13,109},{2,14},{... | collective-permute-start | bytes 786440 | tf_op jit(solution)/shard_map/ppermute | solution.py:36
  67.8 6.8 %collective-permute-start.14 = (f32[512,128]{1,0:T(8,128)S(1)}, f32[512,128]{1,0:T(8,128)S(1)}, u32[]{:S(2)}, u32[]{:S(2)}) collective-permute-start(f32[512,128]{1,0:T(8,128)S(1)} %bitcast.15), channel_id=1, source_target_pairs={{0,4},{1,33},{4,8},{5,37},{8,12},{9,41},{12,0},{13,45},{2,6},{3,35... | collective-permute-start | bytes 786440 | tf_op jit(solution)/shard_map/ppermute | solution.py:36
  67.8 16.4 %collective-permute-start.20 = (f32[1024,128]{1,0:T(8,128)S(1)}, f32[1024,128]{1,0:T(8,128)S(1)}, u32[]{:S(2)}, u32[]{:S(2)}) collective-permute-start(f32[1024,128]{1,0:T(8,128)S(1)} %bitcast.8), channel_id=1, source_target_pairs={{0,1},{1,0},{2,3},{3,2},{4,5},{5,4},{6,7},{7,6},{8,9},{9,8},{10,11... | collective-permute-start | bytes 1572872 | tf_op jit(solution)/shard_map/ppermute | solution.py:26
  70.3 7.0 %collective-permute-start.15 = (f32[512,128]{1,0:T(8,128)S(1)}, f32[512,128]{1,0:T(8,128)S(1)}, u32[]{:S(2)}, u32[]{:S(2)}) collective-permute-start(f32[512,128]{1,0:T(8,128)S(1)} %bitcast.13), channel_id=1, source_target_pairs={{0,12},{1,97},{4,0},{5,101},{8,4},{9,105},{12,8},{13,109},{2,14},{... | collective-permute-start | bytes 786440 | tf_op jit(solution)/shard_map/ppermute | solution.py:36
  71.8 6.0 %collective-permute-start.16 = (f32[512,128]{1,0:T(8,128)S(1)}, f32[512,128]{1,0:T(8,128)S(1)}, u32[]{:S(2)}, u32[]{:S(2)}) collective-permute-start(f32[512,128]{1,0:T(8,128)S(1)} %collective-permute-done.8.refs_1_), channel_id=1, source_target_pairs={{0,1},{1,0},{2,3},{3,2},{4,5},{5,4},{6,7},{7,6},{8,9},{9,8},{10,11... | collective-permute-start | bytes 786440 | tf_op jit(solution)/shard_map/ppermute | solution.py:26
  74.6 6.7 %collective-permute-start.9 = (f32[512,128]{1,0:T(8,128)S(1)}, f32[512,128]{1,0:T(8,128)S(1)}, u32[]{:S(2)}, u32[]{:S(2)}) collective-permute-start(f32[512,128]{1,0:T(8,128)S(1)} %collective-permute-done.8.refs_1_), channel_id=1, source_target_pairs={{0,4},{1,33},{4,8},{5,37},{8,12},{9,41},{12,0},{13,45},{2,6},{3,35... | collective-permute-start | bytes 786440 | tf_op jit(solution)/shard_map/ppermute | solution.py:36
  74.6 7.6 %collective-permute-start.11 = (f32[512,128]{1,0:T(8,128)S(1)}, f32[512,128]{1,0:T(8,128)S(1)}, u32[]{:S(2)}, u32[]{:S(2)}) collective-permute-start(f32[512,128]{1,0:T(8,128)S(1)} %collective-permute-done.10.refs_2_), channel_id=1, source_target_pairs={{0,12},{1,97},{4,0},{5,101},{8,4},{9,105},{12,8},{13,109},{2,14},{... | collective-permute-start | bytes 786440 | tf_op jit(solution)/shard_map/ppermute | solution.py:36
  77.3 8.3 %collective-permute-start.17 = (f32[512,128]{1,0:T(8,128)S(1)}, f32[512,128]{1,0:T(8,128)S(1)}, u32[]{:S(2)}, u32[]{:S(2)}) collective-permute-start(f32[512,128]{1,0:T(8,128)S(1)} %collective-permute-done.10.refs_2_), channel_id=1, source_target_pairs={{0,1},{1,0},{2,3},{3,2},{4,5},{5,4},{6,7},{7,6},{8,9},{9,8},{10,11... | collective-permute-start | bytes 786440 | tf_op jit(solution)/shard_map/ppermute | solution.py:26
  77.9 7.7 %collective-permute-start.18 = (f32[512,128]{1,0:T(8,128)S(1)}, f32[512,128]{1,0:T(8,128)S(1)}, u32[]{:S(2)}, u32[]{:S(2)}) collective-permute-start(f32[512,128]{1,0:T(8,128)S(1)} %collective-permute-done.14.refs_0_), channel_id=1, source_target_pairs={{0,1},{1,0},{2,3},{3,2},{4,5},{5,4},{6,7},{7,6},{8,9},{9,8},{10,11... | collective-permute-start | bytes 786440 | tf_op jit(solution)/shard_map/ppermute | solution.py:26
  81.3 4.3 %collective-permute-start.19 = (f32[512,128]{1,0:T(8,128)S(1)}, f32[512,128]{1,0:T(8,128)S(1)}, u32[]{:S(2)}, u32[]{:S(2)}) collective-permute-start(f32[512,128]{1,0:T(8,128)S(1)} %collective-permute-done.15.refs_1_), channel_id=1, source_target_pairs={{0,1},{1,0},{2,3},{3,2},{4,5},{5,4},{6,7},{7,6},{8,9},{9,8},{10,11... | collective-permute-start | bytes 786440 | tf_op jit(solution)/shard_map/ppermute | solution.py:26
  82.2 4.8 %collective-permute-start.12 = (f32[512,128]{1,0:T(8,128)S(1)}, f32[512,128]{1,0:T(8,128)S(1)}, u32[]{:S(2)}, u32[]{:S(2)}) collective-permute-start(f32[512,128]{1,0:T(8,128)S(1)} %collective-permute-done.9.refs_0_), channel_id=1, source_target_pairs={{0,1},{1,0},{2,3},{3,2},{4,5},{5,4},{6,7},{7,6},{8,9},{9,8},{10,11... | collective-permute-start | bytes 786440 | tf_op jit(solution)/shard_map/ppermute | solution.py:26
  84.2 2.8 %collective-permute-start.13 = (f32[512,128]{1,0:T(8,128)S(1)}, f32[512,128]{1,0:T(8,128)S(1)}, u32[]{:S(2)}, u32[]{:S(2)}) collective-permute-start(f32[512,128]{1,0:T(8,128)S(1)} %collective-permute-done.11.refs_1_), channel_id=1, source_target_pairs={{0,1},{1,0},{2,3},{3,2},{4,5},{5,4},{6,7},{7,6},{8,9},{9,8},{10,11... | collective-permute-start | bytes 786440 | tf_op jit(solution)/shard_map/ppermute | solution.py:26

commit v6 on v3

--- a/solution.py
+++ b/solution.py
@@ -26,14 +26,21 @@
     return lax.ppermute(value, axis, [(i, (i + step) % size) for i in range(size)])
 
 
-def ring_shift(value, step):
+def pair_up(value, turn):
+    peer = [[1, 0, 3, 2], [3, 2, 1, 0]][turn]
     pairs = []
     for y in range(4):
         for x in range(4):
             for z in range(4):
-                pairs.append((rank(y, x, z, 0), rank(y, x, (z + step) % 4, 0)))
-                pairs.append((rank(y, x, z, 1), rank((y + step) % 4, x, z, 1)))
+                pairs.append((rank(y, x, z, 0), rank(y, x, peer[z], 0)))
+                pairs.append((rank(y, x, z, 1), rank(peer[y], x, z, 1)))
     return lax.ppermute(value, AXES, pairs)
+
+
+def found(here, step):
+    if step in (1, 3):
+        step = step + (2 - step) * 2 * lax.rem(here, 2)
+    return lax.rem(here + step, 4)
 
 
 def plane_groups():
@@ -184,7 +191,7 @@
 
 def near_kernel(*refs):
     own, other, out, sem = refs[:5], refs[5:10], refs[10], refs[11]
-    spots = ((0, None), (3, 0), (3, 1), (1, 0), (1, 1))
+    spots = ((0, None), (1, 0), (1, 1), (3, 0), (3, 1))
 
     def spread(blocks):
         return [(ref, step, part) for ref, (step, part) in zip(blocks, spots)]
@@ -204,11 +211,11 @@
         made = []
         for ref, step, part in first:
             rows, part = ref.shape[0], part or 0
-            column = pl.multiple_of(lax.rem(z + step, 4) * 256, 256)
+            column = pl.multiple_of(found(z, step) * 256, 256)
             made.append((ref, out.at[pl.ds(part * rows, rows), pl.ds(column, 128)]))
         for ref, step, part in second:
             part = part or 0
-            row = pl.multiple_of(lax.rem(y + step, 4) * 256, 256)
+            row = pl.multiple_of(found(y, step) * 256, 256)
             for k in range(ref.shape[0] // 256):
                 column = (part * 2 + k) * 256 + 128
                 made.append((ref.at[pl.ds(k * 256, 256)], out.at[pl.ds(row, 256), pl.ds(column, 128)]))
@@ -291,14 +298,14 @@
     ).reshape(nvec, wide)
 
     low, high = block[: nvec // 2], block[nvec // 2 :]
-    below_low = ring_shift(low, 1)
-    above_high = ring_shift(high, -1)
-    below_high = ring_shift(high, 1)
-    above_low = ring_shift(low, -1)
-    far_low = ring_shift(below_low, 1)
-    far_high = ring_shift(above_high, -1)
+    one_low = pair_up(low, 0)
+    two_high = pair_up(high, 1)
+    one_high = pair_up(high, 0)
+    two_low = pair_up(low, 1)
+    far_low = pair_up(one_low, 1)
+    far_high = pair_up(two_high, 0)
     other = shift(block, "core", 1)
-    near = [below_low, below_high, above_low, above_high]
+    near = [one_low, one_high, two_low, two_high]
     other_near = [shift(value, "core", 1) for value in near]
     whole = place_near([block, *near], [other, *other_near], nvec)
     far = [far_low, far_high]

time: 86.7 us -> 85.6 us (0.987)
  starting transfers between devices: 32.8 us -> 28.9 us
  waiting for transfers between devices: 7.83 us -> 10.6 us
    ppermute x6, waiting for transfers between devices: 0.31 us -> 3.11 us  [pair_up(): return lax.ppermute(value, AXES, pairs)]
    ppermute x6, starting transfers between devices: 6.89 us -> 4.7 us  [pair_up(): return lax.ppermute(value, AXES, pairs)]
    ppermute x15, starting transfers between devices: 26 us -> 24.2 us  [shift(): lax.ppermute(value, axis, [(i, (i + step) % size) for i in range(size)])]
where the time goes in v6:
time: 85.6 us; the launch traced here: 85.4 us
  blocking collectives  29.7 us (35%)
  starting transfers between devices  28.9 us (34%)
  Pallas kernels  14.8 us (17%)
  waiting for transfers between devices  10.6 us (12%)
    ppermute x15, starting transfers between devices, shift(): lax.ppermute(value, axis, [(i, (i + step) % size) for i in range(size)])  24.2 us
    all_to_all x1, blocking collectives, body(): parts = lax.all_to_all(parts, PLANE, 0, 0, tiled=True)  15.9 us
    all_to_all x1, blocking collectives, body(): lax.all_to_all(copies, AXES, 0, 0, tiled=True, axis_index_groups=plane_gr...  13.8 us
    ppermute x15, waiting for transfers between devices, shift(): lax.ppermute(value, axis, [(i, (i + step) % size) for i in range(size)])  7.52 us
    ppermute x6, starting transfers between devices, pair_up(): return lax.ppermute(value, AXES, pairs)  4.7 us
    pallas_call x1, Pallas kernels, opening(): kernel_call(kernel, h, v, [HBM, HBM], [slab], [block, total, sems])  4.45 us
    pallas_call x1, Pallas kernels, second(): return call(resident(h_here), v)  3.32 us
    ppermute x6, waiting for transfers between devices, pair_up(): return lax.ppermute(value, AXES, pairs)  3.11 us
  transfers between devices with their start and end apart: 21, of which 4 were waited for; matrix products, arithmetic and copies ran while one was open for 0% of the time, Pallas kernels for 11%

profile of v6, /device:TPU:1, one launch (start us, length us, event | category | flops | bytes accessed | tf_op | source)
XLA Modules:
  0.0 85.4 jit_solution(8026777067694340445)
XLA Ops:
  0.0 0.0 copy-start
  0.0 4.5 %shard_map.37 = (f32[128,512]{1,0:T(8,128)S(1)}, f32[128,512]{1,0:T(8,128)S(1)}, bf16[6000,512]{1,0:T(8,128)(2,1)S(1)}) custom-call(bf16[6000,512]{1,0:T(8,128)(2,1)} %bitcast.10, bf16[6000,1024]{1,0:T(8,128)(2,1)} %v.5), custom_call_target="tpu_custom_call" | custom-call | flops 1572864000 | bytes 3072000 | tf_op jit(solution)/shard_map/pallas_call | solution.py:173
  4.5 1.5 %collective-permute-start.2 = (f32[128,512]{1,0:T(8,128)S(1)}, f32[128,512]{1,0:T(8,128)S(1)}, u32[]{:S(2)}, u32[]{:S(2)}) collective-permute-start(f32[128,512]{1,0:T(8,128)S(1)} %get-tuple-element.24), channel_id=1, source_target_pairs={{0,1},{1,0},{2,3},{3,2},{4,5},{5,4},{6,7},{7,6},{8,9},{9,8},{10,11... | collective-permute-start | bytes 786440 | tf_op jit(solution)/shard_map/ppermute | solution.py:26
  5.9 3.3 %shard_map.38 = (f32[128,512]{1,0:T(8,128)S(1)}, f32[128,512]{1,0:T(8,128)S(1)}, bf16[6000,256]{1,0:T(8,128)(2,1)S(1)}) custom-call(bf16[6000,512]{1,0:T(8,128)(2,1)S(1)} %get-tuple-element.16.h_here, bf16[6000,1024]{1,0:T(8,128)(2,1)} %v.5), custom_call_target="tpu_custom_call" | custom-call | flops 1572864000 | bytes 3072000 | tf_op jit(solution)/shard_map/pallas_call | solution.py:178
  9.3 0.1 collective-permute-start.1
  9.4 2.4 %shard_map.39 = (f32[128,512]{1,0:T(8,128)S(1)}, f32[128,512]{1,0:T(8,128)S(1)}, bf16[6000,256]{1,0:T(8,128)(2,1)S(1)}) custom-call(bf16[6000,512]{1,0:T(8,128)(2,1)S(1)} %get-tuple-element.16.h_here, bf16[6000,256]{1,0:T(8,128)(2,1)S(1)} %get-tuple-element.17.v_here, bf16[6000,1024]{1,0:T(8,128)(2,1)} %v.5), custom_call_target="tpu_custom_call" | custom-call | flops 1572864000 | bytes 3072000 | tf_op jit(solution)/shard_map/pallas_call | solution.py:183
  11.7 0.6 collective-permute-start.5
  12.3 0.0 collective-permute-done.2
  12.4 1.8 %collective-permute-start.3 = (f32[64,512]{1,0:T(8,128)S(1)}, f32[64,512]{1,0:T(8,128)S(1)}, u32[]{:S(2)}, u32[]{:S(2)}) collective-permute-start(f32[64,512]{1,0:T(8,128)S(1)} %get-tuple-element.31), channel_id=1, source_target_pairs={{0,4},{4,8},{8,12},{12,0},{1,5},{5,9},{9,13},{13,1},{2,6},{6,10},{... | collective-permute-start | bytes 393224 | tf_op jit(solution)/shard_map/ppermute | solution.py:26
  14.2 1.9 %shard_map.40 = (f32[128,512]{1,0:T(8,128)S(1)}, f32[128,512]{1,0:T(8,128)S(1)}) custom-call(bf16[6000,512]{1,0:T(8,128)(2,1)S(1)} %get-tuple-element.16.h_here, bf16[6000,256]{1,0:T(8,128)(2,1)S(1)} %get-tuple-element.18.v_here), custom_call_target="tpu_custom_call" | custom-call | flops 1572864000 | bytes 3072000 | tf_op jit(solution)/shard_map/pallas_call | solution.py:187
  16.0 0.4 collective-permute-start
  16.4 1.9 %collective-permute-start.6 = (f32[64,512]{1,0:T(8,128)S(1)}, f32[64,512]{1,0:T(8,128)S(1)}, u32[]{:S(2)}, u32[]{:S(2)}) collective-permute-start(f32[64,512]{1,0:T(8,128)S(1)} %get-tuple-element.32), channel_id=1, source_target_pairs={{0,12},{4,0},{8,4},{12,8},{1,13},{5,1},{9,5},{13,9},{2,14},{6,2},{... | collective-permute-start | bytes 393224 | tf_op jit(solution)/shard_map/ppermute | solution.py:26
  18.4 0.0 collective-permute-done.1
  18.4 0.0 collective-permute-done.5
  18.5 1.7 %collective-permute-done.3 = f32[64,512]{1,0:T(8,128)S(1)} collective-permute-done((f32[64,512]{1,0:T(8,128)S(1)}, f32[64,512]{1,0:T(8,128)S(1)}, u32[]{:S(2)}, u32[]{:S(2)}) %collective-permute-start.3) | collective-permute-done | bytes 131104 | tf_op jit(solution)/shard_map/ppermute | solution.py:26
  20.2 0.1 collective-permute-start.4
  20.3 1.3 %collective-permute-done.6 = f32[64,512]{1,0:T(8,128)S(1)} collective-permute-done((f32[64,512]{1,0:T(8,128)S(1)}, f32[64,512]{1,0:T(8,128)S(1)}, u32[]{:S(2)}, u32[]{:S(2)}) %collective-permute-start.6) | collective-permute-done | bytes 131104 | tf_op jit(solution)/shard_map/ppermute | solution.py:26
  21.7 2.6 %collective-permute-start.7 = (f32[128,512]{1,0:T(8,128)S(1)}, f32[128,512]{1,0:T(8,128)S(1)}, u32[]{:S(2)}, u32[]{:S(2)}) collective-permute-start(f32[128,512]{1,0:T(8,128)S(1)} %pad_maximum_fusion.1), channel_id=1, source_target_pairs={{0,12},{4,0},{8,4},{12,8},{1,13},{5,1},{9,5},{13,9},{2,14},{6,2},{... | collective-permute-start | bytes 786440 | tf_op jit(solution)/shard_map/ppermute | solution.py:26
  24.3 0.0 collective-permute-done
  24.3 4.4 %collective-permute-done.4 = f32[128,512]{1,0:T(8,128)S(1)} collective-permute-done((f32[128,512]{1,0:T(8,128)S(1)}, f32[128,512]{1,0:T(8,128)S(1)}, u32[]{:S(2)}, u32[]{:S(2)}) %collective-permute-start.4) | collective-permute-done | bytes 262176 | tf_op jit(solution)/shard_map/ppermute | solution.py:26
  28.8 0.0 collective-permute-done.7
  28.8 0.0 copy-done
  28.8 0.6 convolution_bitcast_fusion
  29.4 0.2 copy.5
  29.6 15.9 %all_to_all.10 = f32[16,64,128]{2,1,0:T(8,128)S(1)} all-to-all(f32[16,64,128]{2,1,0:T(8,128)S(1)} %bitcast.11), channel_id=1, replica_groups=mesh['y'=4,'xh'=2,'z'=4,'xl'=2,'core'=2] {'y','xh','xl'}, dimensions={0} | all-to-all | bytes 1048576 | tf_op jit(solution)/shard_map/all_to_all | solution.py:293
  45.6 13.8 %all_to_all.11 = f32[16,64,128]{2,1,0:T(8,128)S(1)} all-to-all(f32[16,64,128]{2,1,0:T(8,128)S(1)} %broadcast_in_dim.3), channel_id=1, replica_groups={{0,2,16,18,32,34,48,50,64,66,80,82,96,98,112,114},{4,6,20,22,36,38,52,5..., dimensions={0} | all-to-all | bytes 1048576 | tf_op jit(solution)/shard_map/all_to_all | solution.py:296
  59.4 0.9 %collective-permute-start.15 = (f32[512,128]{1,0:T(8,128)S(1)}, f32[512,128]{1,0:T(8,128)S(1)}, u32[]{:S(2)}, u32[]{:S(2)}) collective-permute-start(f32[512,128]{1,0:T(8,128)S(1)} %bitcast.14), channel_id=1, source_target_pairs={{0,12},{1,97},{4,8},{5,101},{8,4},{9,105},{12,0},{13,109},{2,14},{... | collective-permute-start | bytes 786440 | tf_op jit(solution)/shard_map/ppermute | solution.py:37
  60.4 0.0 collective-permute-start.8
  60.4 1.5 %collective-permute-start.14 = (f32[512,128]{1,0:T(8,128)S(1)}, f32[512,128]{1,0:T(8,128)S(1)}, u32[]{:S(2)}, u32[]{:S(2)}) collective-permute-start(f32[512,128]{1,0:T(8,128)S(1)} %bitcast.12), channel_id=1, source_target_pairs={{0,4},{1,33},{4,0},{5,37},{8,12},{9,41},{12,8},{13,45},{2,6},{3,35... | collective-permute-start | bytes 786440 | tf_op jit(solution)/shard_map/ppermute | solution.py:37
  61.8 1.8 %collective-permute-start.10 = (f32[512,128]{1,0:T(8,128)S(1)}, f32[512,128]{1,0:T(8,128)S(1)}, u32[]{:S(2)}, u32[]{:S(2)}) collective-permute-start(f32[512,128]{1,0:T(8,128)S(1)} %bitcast.13), channel_id=1, source_target_pairs={{0,12},{1,97},{4,8},{5,101},{8,4},{9,105},{12,0},{13,109},{2,14},{... | collective-permute-start | bytes 786440 | tf_op jit(solution)/shard_map/ppermute | solution.py:37
  63.7 4.2 %collective-permute-start.16 = (f32[1024,128]{1,0:T(8,128)S(1)}, f32[1024,128]{1,0:T(8,128)S(1)}, u32[]{:S(2)}, u32[]{:S(2)}) collective-permute-start(f32[1024,128]{1,0:T(8,128)S(1)} %bitcast.8), channel_id=1, source_target_pairs={{0,1},{1,0},{2,3},{3,2},{4,5},{5,4},{6,7},{7,6},{8,9},{9,8},{10,11... | collective-permute-start | bytes 1572872 | tf_op jit(solution)/shard_map/ppermute | solution.py:26
  67.9 0.0 collective-permute-done.15.refs_3_
  67.9 2.2 %collective-permute-start.19 = (f32[512,128]{1,0:T(8,128)S(1)}, f32[512,128]{1,0:T(8,128)S(1)}, u32[]{:S(2)}, u32[]{:S(2)}) collective-permute-start(f32[512,128]{1,0:T(8,128)S(1)} %collective-permute-done.15.refs_3_), channel_id=1, source_target_pairs={{0,1},{1,0},{2,3},{3,2},{4,5},{5,4},{6,7},{7,6},{8,9},{9,8},{10,11... | collective-permute-start | bytes 786440 | tf_op jit(solution)/shard_map/ppermute | solution.py:26
  70.1 0.0 collective-permute-done.8.refs_1_
  70.1 2.0 %collective-permute-start.17 = (f32[512,128]{1,0:T(8,128)S(1)}, f32[512,128]{1,0:T(8,128)S(1)}, u32[]{:S(2)}, u32[]{:S(2)}) collective-permute-start(f32[512,128]{1,0:T(8,128)S(1)} %collective-permute-done.8.refs_1_), channel_id=1, source_target_pairs={{0,1},{1,0},{2,3},{3,2},{4,5},{5,4},{6,7},{7,6},{8,9},{9,8},{10,11... | collective-permute-start | bytes 786440 | tf_op jit(solution)/shard_map/ppermute | solution.py:26
  72.1 0.0 collective-permute-done.14.refs_2_
  72.1 0.5 collective-permute-start.9
  72.6 0.0 collective-permute-done.10.refs_4_
  72.6 0.0 collective-permute-start.11
  72.6 0.0 collective-permute-done.19.refs_8_
  72.6 2.8 %collective-permute-start.18 = (f32[512,128]{1,0:T(8,128)S(1)}, f32[512,128]{1,0:T(8,128)S(1)}, u32[]{:S(2)}, u32[]{:S(2)}) collective-permute-start(f32[512,128]{1,0:T(8,128)S(1)} %collective-permute-done.14.refs_2_), channel_id=1, source_target_pairs={{0,1},{1,0},{2,3},{3,2},{4,5},{5,4},{6,7},{7,6},{8,9},{9,8},{10,11... | collective-permute-start | bytes 786440 | tf_op jit(solution)/shard_map/ppermute | solution.py:26
  75.4 0.0 collective-permute-done.17.refs_6_
  75.4 0.1 collective-permute-start.20
  75.5 3.1 %collective-permute-done.9.refs_0_ = f32[512,128]{1,0:T(8,128)S(1)} collective-permute-done((f32[512,128]{1,0:T(8,128)S(1)}, f32[512,128]{1,0:T(8,128)S(1)}, u32[]{:S(2)}, u32[]{:S(2)}) %collective-permute-start.9) | collective-permute-done | bytes 262176 | tf_op jit(solution)/shard_map/ppermute | solution.py:37
  78.6 4.0 %collective-permute-start.12 = (f32[512,128]{1,0:T(8,128)S(1)}, f32[512,128]{1,0:T(8,128)S(1)}, u32[]{:S(2)}, u32[]{:S(2)}) collective-permute-start(f32[512,128]{1,0:T(8,128)S(1)} %collective-permute-done.9.refs_0_), channel_id=1, source_target_pairs={{0,1},{1,0},{2,3},{3,2},{4,5},{5,4},{6,7},{7,6},{8,9},{9,8},{10,11... | collective-permute-start | bytes 786440 | tf_op jit(solution)/shard_map/ppermute | solution.py:26
  82.5 0.0 collective-permute-done.11.refs_1_
  82.5 0.0 collective-permute-start.13
  82.5 0.0 collective-permute-done.18.refs_7_
  82.5 0.0 collective-permute-done.20.refs_9_
  82.5 0.0 collective-permute-done.16.refs_5_
  82.6 1.8 %place_near.1.refs_4_ = f32[1024,1024]{1,0:T(8,128)} custom-call(f32[1024,128]{1,0:T(8,128)S(1)} %bitcast.9, f32[512,128]{1,0:T(8,128)S(1)} %collective-permute-done.8.refs_1_, f32[512,128]{1,0:T(8,128)S(1)} %collective-permute-done.14.refs_2_, f32[512,128]{1,0:T(8,128)S(1)} %collective-permute-done.15.refs_3_, ...), custom_call_target="tpu_custom_call" | custom-call | tf_op jit(solution)/shard_map/place_near/pallas_call | solution.py:238
  84.4 0.0 collective-permute-done.12.refs_2_
  84.4 0.0 collective-permute-done.13.refs_3_
  84.4 1.0 %place_far.1 = f32[1024,1024]{1,0:T(8,128)} custom-call(f32[512,128]{1,0:T(8,128)S(1)} %collective-permute-done.9.refs_0_, f32[512,128]{1,0:T(8,128)S(1)} %collective-permute-done.11.refs_1_, f32[512,128]{1,0:T(8,128)S(1)} %collective-permute-done.12.refs_2_, f32[512,128]{1,0:T(8,128)S(1)} %collective-permute-done.13.refs_3_, ...), custom_call_target="tpu_custom_call", output_to_operand_aliasing={{}: (4, {})} | custom-call | tf_op jit(solution)/shard_map/place_far/pallas_call | solution.py:250
  (11 shorter events, 0.4 us)
Async XLA Ops:
  0.0 28.8 %copy-start = (bf16[512,1024]{1,0:T(8,128)(2,1)S(1)}, bf16[512,1024]{1,0:T(8,128)(2,1)}, u32[]{:S(2)}) copy-start(bf16[512,1024]{1,0:T(8,128)(2,1)} %param.5) | copy-start | bytes 3145732
  4.5 7.8 %collective-permute-start.2 = (f32[128,512]{1,0:T(8,128)S(1)}, f32[128,512]{1,0:T(8,128)S(1)}, u32[]{:S(2)}, u32[]{:S(2)}) collective-permute-start(f32[128,512]{1,0:T(8,128)S(1)} %get-tuple-element.24), channel_id=1, source_target_pairs={{0,1},{1,0},{2,3},{3,2},{4,5},{5,4},{6,7},{7,6},{8,9},{9,8},{10,11... | collective-permute-start | bytes 786440 | tf_op jit(solution)/shard_map/ppermute | solution.py:26
  9.3 9.1 %collective-permute-start.1 = (f32[128,512]{1,0:T(8,128)S(1)}, f32[128,512]{1,0:T(8,128)S(1)}, u32[]{:S(2)}, u32[]{:S(2)}) collective-permute-start(f32[128,512]{1,0:T(8,128)S(1)} %get-tuple-element.22), channel_id=1, source_target_pairs={{0,1},{1,0},{2,3},{3,2},{4,5},{5,4},{6,7},{7,6},{8,9},{9,8},{10,11... | collective-permute-start | bytes 786440 | tf_op jit(solution)/shard_map/ppermute | solution.py:26
  11.7 6.7 %collective-permute-start.5 = (f32[128,512]{1,0:T(8,128)S(1)}, f32[128,512]{1,0:T(8,128)S(1)}, u32[]{:S(2)}, u32[]{:S(2)}) collective-permute-start(f32[128,512]{1,0:T(8,128)S(1)} %get-tuple-element.26), channel_id=1, source_target_pairs={{0,1},{1,0},{2,3},{3,2},{4,5},{5,4},{6,7},{7,6},{8,9},{9,8},{10,11... | collective-permute-start | bytes 786440 | tf_op jit(solution)/shard_map/ppermute | solution.py:26
  12.4 7.8 %collective-permute-start.3 = (f32[64,512]{1,0:T(8,128)S(1)}, f32[64,512]{1,0:T(8,128)S(1)}, u32[]{:S(2)}, u32[]{:S(2)}) collective-permute-start(f32[64,512]{1,0:T(8,128)S(1)} %get-tuple-element.31), channel_id=1, source_target_pairs={{0,4},{4,8},{8,12},{12,0},{1,5},{5,9},{9,13},{13,1},{2,6},{6,10},{... | collective-permute-start | bytes 393224 | tf_op jit(solution)/shard_map/ppermute | solution.py:26
  16.0 8.3 %collective-permute-start = (f32[128,512]{1,0:T(8,128)S(1)}, f32[128,512]{1,0:T(8,128)S(1)}, u32[]{:S(2)}, u32[]{:S(2)}) collective-permute-start(f32[128,512]{1,0:T(8,128)S(1)} %get-tuple-element.20), channel_id=1, source_target_pairs={{0,1},{1,0},{2,3},{3,2},{4,5},{5,4},{6,7},{7,6},{8,9},{9,8},{10,11... | collective-permute-start | bytes 786440 | tf_op jit(solution)/shard_map/ppermute | solution.py:26
  16.4 5.2 %collective-permute-start.6 = (f32[64,512]{1,0:T(8,128)S(1)}, f32[64,512]{1,0:T(8,128)S(1)}, u32[]{:S(2)}, u32[]{:S(2)}) collective-permute-start(f32[64,512]{1,0:T(8,128)S(1)} %get-tuple-element.32), channel_id=1, source_target_pairs={{0,12},{4,0},{8,4},{12,8},{1,13},{5,1},{9,5},{13,9},{2,14},{6,2},{... | collective-permute-start | bytes 393224 | tf_op jit(solution)/shard_map/ppermute | solution.py:26
  20.2 8.5 %collective-permute-start.4 = (f32[128,512]{1,0:T(8,128)S(1)}, f32[128,512]{1,0:T(8,128)S(1)}, u32[]{:S(2)}, u32[]{:S(2)}) collective-permute-start(f32[128,512]{1,0:T(8,128)S(1)} %pad_maximum_fusion), channel_id=1, source_target_pairs={{0,4},{4,8},{8,12},{12,0},{1,5},{5,9},{9,13},{13,1},{2,6},{6,10},{... | collective-permute-start | bytes 786440 | tf_op jit(solution)/shard_map/ppermute | solution.py:26
  21.7 7.1 %collective-permute-start.7 = (f32[128,512]{1,0:T(8,128)S(1)}, f32[128,512]{1,0:T(8,128)S(1)}, u32[]{:S(2)}, u32[]{:S(2)}) collective-permute-start(f32[128,512]{1,0:T(8,128)S(1)} %pad_maximum_fusion.1), channel_id=1, source_target_pairs={{0,12},{4,0},{8,4},{12,8},{1,13},{5,1},{9,5},{13,9},{2,14},{6,2},{... | collective-permute-start | bytes 786440 | tf_op jit(solution)/shard_map/ppermute | solution.py:26
  59.4 8.5 %collective-permute-start.15 = (f32[512,128]{1,0:T(8,128)S(1)}, f32[512,128]{1,0:T(8,128)S(1)}, u32[]{:S(2)}, u32[]{:S(2)}) collective-permute-start(f32[512,128]{1,0:T(8,128)S(1)} %bitcast.14), channel_id=1, source_target_pairs={{0,12},{1,97},{4,8},{5,101},{8,4},{9,105},{12,0},{13,109},{2,14},{... | collective-permute-start | bytes 786440 | tf_op jit(solution)/shard_map/ppermute | solution.py:37
  60.4 9.7 %collective-permute-start.8 = (f32[512,128]{1,0:T(8,128)S(1)}, f32[512,128]{1,0:T(8,128)S(1)}, u32[]{:S(2)}, u32[]{:S(2)}) collective-permute-start(f32[512,128]{1,0:T(8,128)S(1)} %bitcast.15), channel_id=1, source_target_pairs={{0,4},{1,33},{4,0},{5,37},{8,12},{9,41},{12,8},{13,45},{2,6},{3,35... | collective-permute-start | bytes 786440 | tf_op jit(solution)/shard_map/ppermute | solution.py:37
  60.4 11.8 %collective-permute-start.14 = (f32[512,128]{1,0:T(8,128)S(1)}, f32[512,128]{1,0:T(8,128)S(1)}, u32[]{:S(2)}, u32[]{:S(2)}) collective-permute-start(f32[512,128]{1,0:T(8,128)S(1)} %bitcast.12), channel_id=1, source_target_pairs={{0,4},{1,33},{4,0},{5,37},{8,12},{9,41},{12,8},{13,45},{2,6},{3,35... | collective-permute-start | bytes 786440 | tf_op jit(solution)/shard_map/ppermute | solution.py:37
  61.8 10.8 %collective-permute-start.10 = (f32[512,128]{1,0:T(8,128)S(1)}, f32[512,128]{1,0:T(8,128)S(1)}, u32[]{:S(2)}, u32[]{:S(2)}) collective-permute-start(f32[512,128]{1,0:T(8,128)S(1)} %bitcast.13), channel_id=1, source_target_pairs={{0,12},{1,97},{4,8},{5,101},{8,4},{9,105},{12,0},{13,109},{2,14},{... | collective-permute-start | bytes 786440 | tf_op jit(solution)/shard_map/ppermute | solution.py:37
  63.7 18.9 %collective-permute-start.16 = (f32[1024,128]{1,0:T(8,128)S(1)}, f32[1024,128]{1,0:T(8,128)S(1)}, u32[]{:S(2)}, u32[]{:S(2)}) collective-permute-start(f32[1024,128]{1,0:T(8,128)S(1)} %bitcast.8), channel_id=1, source_target_pairs={{0,1},{1,0},{2,3},{3,2},{4,5},{5,4},{6,7},{7,6},{8,9},{9,8},{10,11... | collective-permute-start | bytes 1572872 | tf_op jit(solution)/shard_map/ppermute | solution.py:26
  67.9 4.7 %collective-permute-start.19 = (f32[512,128]{1,0:T(8,128)S(1)}, f32[512,128]{1,0:T(8,128)S(1)}, u32[]{:S(2)}, u32[]{:S(2)}) collective-permute-start(f32[512,128]{1,0:T(8,128)S(1)} %collective-permute-done.15.refs_3_), channel_id=1, source_target_pairs={{0,1},{1,0},{2,3},{3,2},{4,5},{5,4},{6,7},{7,6},{8,9},{9,8},{10,11... | collective-permute-start | bytes 786440 | tf_op jit(solution)/shard_map/ppermute | solution.py:26
  70.1 5.3 %collective-permute-start.17 = (f32[512,128]{1,0:T(8,128)S(1)}, f32[512,128]{1,0:T(8,128)S(1)}, u32[]{:S(2)}, u32[]{:S(2)}) collective-permute-start(f32[512,128]{1,0:T(8,128)S(1)} %collective-permute-done.8.refs_1_), channel_id=1, source_target_pairs={{0,1},{1,0},{2,3},{3,2},{4,5},{5,4},{6,7},{7,6},{8,9},{9,8},{10,11... | collective-permute-start | bytes 786440 | tf_op jit(solution)/shard_map/ppermute | solution.py:26
  72.1 6.4 %collective-permute-start.9 = (f32[512,128]{1,0:T(8,128)S(1)}, f32[512,128]{1,0:T(8,128)S(1)}, u32[]{:S(2)}, u32[]{:S(2)}) collective-permute-start(f32[512,128]{1,0:T(8,128)S(1)} %collective-permute-done.8.refs_1_), channel_id=1, source_target_pairs={{0,12},{1,97},{4,8},{5,101},{8,4},{9,105},{12,0},{13,109},{2,14},{... | collective-permute-start | bytes 786440 | tf_op jit(solution)/shard_map/ppermute | solution.py:37
  72.6 9.9 %collective-permute-start.11 = (f32[512,128]{1,0:T(8,128)S(1)}, f32[512,128]{1,0:T(8,128)S(1)}, u32[]{:S(2)}, u32[]{:S(2)}) collective-permute-start(f32[512,128]{1,0:T(8,128)S(1)} %collective-permute-done.10.refs_4_), channel_id=1, source_target_pairs={{0,4},{1,33},{4,0},{5,37},{8,12},{9,41},{12,8},{13,45},{2,6},{3,35... | collective-permute-start | bytes 786440 | tf_op jit(solution)/shard_map/ppermute | solution.py:37
  72.6 9.9 %collective-permute-start.18 = (f32[512,128]{1,0:T(8,128)S(1)}, f32[512,128]{1,0:T(8,128)S(1)}, u32[]{:S(2)}, u32[]{:S(2)}) collective-permute-start(f32[512,128]{1,0:T(8,128)S(1)} %collective-permute-done.14.refs_2_), channel_id=1, source_target_pairs={{0,1},{1,0},{2,3},{3,2},{4,5},{5,4},{6,7},{7,6},{8,9},{9,8},{10,11... | collective-permute-start | bytes 786440 | tf_op jit(solution)/shard_map/ppermute | solution.py:26
  75.4 7.2 %collective-permute-start.20 = (f32[512,128]{1,0:T(8,128)S(1)}, f32[512,128]{1,0:T(8,128)S(1)}, u32[]{:S(2)}, u32[]{:S(2)}) collective-permute-start(f32[512,128]{1,0:T(8,128)S(1)} %collective-permute-done.10.refs_4_), channel_id=1, source_target_pairs={{0,1},{1,0},{2,3},{3,2},{4,5},{5,4},{6,7},{7,6},{8,9},{9,8},{10,11... | collective-permute-start | bytes 786440 | tf_op jit(solution)/shard_map/ppermute | solution.py:26
  78.6 5.8 %collective-permute-start.12 = (f32[512,128]{1,0:T(8,128)S(1)}, f32[512,128]{1,0:T(8,128)S(1)}, u32[]{:S(2)}, u32[]{:S(2)}) collective-permute-start(f32[512,128]{1,0:T(8,128)S(1)} %collective-permute-done.9.refs_0_), channel_id=1, source_target_pairs={{0,1},{1,0},{2,3},{3,2},{4,5},{5,4},{6,7},{7,6},{8,9},{9,8},{10,11... | collective-permute-start | bytes 786440 | tf_op jit(solution)/shard_map/ppermute | solution.py:26
  82.5 1.9 %collective-permute-start.13 = (f32[512,128]{1,0:T(8,128)S(1)}, f32[512,128]{1,0:T(8,128)S(1)}, u32[]{:S(2)}, u32[]{:S(2)}) collective-permute-start(f32[512,128]{1,0:T(8,128)S(1)} %collective-permute-done.11.refs_1_), channel_id=1, source_target_pairs={{0,1},{1,0},{2,3},{3,2},{4,5},{5,4},{6,7},{7,6},{8,9},{9,8},{10,11... | collective-permute-start | bytes 786440 | tf_op jit(solution)/shard_map/ppermute | solution.py:26
